TPU v7x, 32 devices: a whole 2x2x4 slice. The times are simulated.
32 devices in a mesh: ctx: 4 (over z), fsdp: 8 (over y, x, core).
Axes of the slice: x: 2, y: 2, z: 4, core: 2. Of those that a mesh axis runs over, the one named last changes fastest.
Arguments:
- tokens_in: bfloat16 [8, 4096, 768], P('fsdp', 'ctx'), may hold values from -6 to 6
- out_grad: bfloat16 [8, 4096, 768], P('fsdp', 'ctx'), may hold values from -6 to 6
- gain_attn: bfloat16 [768], P('fsdp'), may hold values from 0.5 to 1.5
- gain_mlp: bfloat16 [768], P('fsdp'), may hold values from 0.5 to 1.5
- w_qkv: bfloat16 [768, 2304], P('fsdp'), may hold values from -0.21875 to 0.21875
- w_out: bfloat16 [768, 768], P('fsdp'), may hold values from -6 to 6
- w_up: bfloat16 [768, 3072], P('fsdp'), may hold values from -0.21875 to 0.21875
- w_down: bfloat16 [3072, 768], P('fsdp'), may hold values from -0.109375 to 0.109375
- lengths: int32 [8], P('fsdp'), may hold values from 1024 to 4096, as said below
- block_order: int32 [8, 8], P('fsdp'), may hold values from 0 to 7, as said below
Outputs:
- result: bfloat16 [8, 4096, 768], P('fsdp', 'ctx')
- grad_tokens: bfloat16 [8, 4096, 768], P('fsdp', 'ctx')
- grad_gain_attn: float32 [768], P('fsdp')
- grad_gain_mlp: float32 [768], P('fsdp')
- grad_w_qkv: float32 [768, 2304], P('fsdp')
- grad_w_out: float32 [768, 768], P('fsdp')
- grad_w_up: float32 [768, 3072], P('fsdp')
- grad_w_down: float32 [3072, 768], P('fsdp')
Inputs may be any that keep to these rules, and one draw needn't show every extreme that they name: `lengths`: some sequence has exactly 4096 valid tokens and some exactly 1024. `block_order`: each row holds every block number once; stored blocks 2 c and 2 c + 1 of a row are block numbers p and 7 - p in some order, for some p.
All inputs are finite; a program needn't handle non-finite values.
Results may differ from a plain program's by a relative error of at most 0.015.
The roundings to bfloat16 on the way count: a program that leaves them out, or rounds other values in their place, can miss the bound.
Values may be sent and summed in bfloat16 or wider, within the bound.
A program may use at most 256 MiB of HBM per device.

v0:
```python
import functools

import jax
import jax.numpy as jnp
from jax import lax
from jax.experimental import pallas as pl
from jax.experimental.pallas import tpu as pltpu
from jax.sharding import PartitionSpec as P


HEAD_DIM = 64
BLK = 512
HALF = 256
LOG2E = 1.4426950408889634
BIG = 3e38
LOW = -1e30


def nn(left, right):
    return lax.dot_general(left, right, (((1,), (0,)), ((), ())), preferred_element_type=jnp.float32)


def nt(left, right):
    return lax.dot_general(left, right, (((1,), (1,)), ((), ())), preferred_element_type=jnp.float32)


def sign_of(scores):
    return jnp.tanh(scores.astype(jnp.bfloat16) * jnp.bfloat16(BIG))


def block_mask(key_start, query_start, length, shape):
    keys = key_start + lax.broadcasted_iota(jnp.int32, shape, 0)
    queries = query_start + lax.broadcasted_iota(jnp.int32, shape, 1)
    return keys <= jnp.minimum(queries, length - 1)


def gather_columns(refs, out):
    span = refs[0].shape[1]
    for part, ref in enumerate(refs):
        out[:, part * span : (part + 1) * span] = ref[...]


def turn_rows(source, out, twice):
    for part in range(source.shape[1] // BLK):
        span = slice(part * BLK, (part + 1) * BLK)
        piece = source[:, span]
        out[span, :] = jnp.concatenate([piece, piece if twice else jnp.zeros_like(piece)], axis=0).T


def query_weights(query_t):
    scaled = query_t.astype(jnp.float32) * (LOG2E * HEAD_DIM ** -0.5)
    high = scaled.astype(jnp.bfloat16)
    return jnp.concatenate([high, (scaled - high.astype(jnp.float32)).astype(jnp.bfloat16)], axis=0)


def forward_kernel(parts, table, *refs):
    query_refs, key_refs, value_refs = refs[:parts], refs[parts : 2 * parts], refs[2 * parts : 3 * parts]
    sends = refs[3 * parts : 4 * parts]
    exact_ref, log_ref, queries, keys_t, values, keys, weights = refs[4 * parts :]
    blocks = queries.shape[1] // BLK
    length = table[blocks]
    gather_columns(query_refs, queries)
    gather_columns(key_refs, keys_t)
    gather_columns(value_refs, values)
    turn_rows(keys_t, keys, True)
    full = (length + BLK - 1) // BLK

    @pl.loop(0, blocks)
    def _(place):
        span = pl.ds(pl.multiple_of(table[place] * BLK, BLK), BLK)
        weights[...] = query_weights(queries[:, span])
        count = jnp.minimum(place + 1, full)

        def step(number, carry, masked):
            key_span = pl.ds(pl.multiple_of(table[number] * BLK, BLK), BLK)
            key_rows = keys[key_span, :]
            value_rows = values[:, key_span]
            result = []
            scores_list = [nn(key_rows, weights[:, h * HALF : (h + 1) * HALF]) for h in range(2)]
            for half in range(2):
                top, total, mixed = carry[half]
                scores = scores_list[half]
                size = jnp.abs(scores)
                if masked:
                    mask = block_mask(number * BLK, place * BLK + half * HALF, length, size.shape)
                    size = jnp.where(mask, size, LOW)
                new_top = jnp.maximum(top, jnp.max(size, axis=0, keepdims=True))
                fade = jnp.exp2(top - new_top)
                powers = jnp.exp2(size - new_top)
                new_total = total * fade + jnp.sum(powers, axis=0, keepdims=True)
                signed = powers.astype(jnp.bfloat16) * sign_of(scores)
                result.append((new_top, new_total, mixed * fade + nn(value_rows, signed)))
            return tuple(result)

        begin = (
            jnp.full((1, HALF), LOW, jnp.float32),
            jnp.zeros((1, HALF), jnp.float32),
            jnp.zeros((HEAD_DIM, HALF), jnp.float32),
        )
        carry = lax.fori_loop(0, count - 1, functools.partial(step, masked=False), (begin, begin))
        carry = step(count - 1, carry, True)
        exact_ref[:, span] = jnp.concatenate([c[2] / c[1] for c in carry], axis=1)
        log_ref[:, span] = jnp.concatenate([c[0] + jnp.log2(c[1]) for c in carry], axis=1)

    width = sends[0].shape[1]
    for part in range(parts):
        sends[part][...] = exact_ref[:, part * width : (part + 1) * width].astype(jnp.bfloat16)


def backward_kernel(parts, table, *refs):
    query_refs, key_refs, value_refs = refs[:parts], refs[parts : 2 * parts], refs[2 * parts : 3 * parts]
    grad_refs, refs = refs[3 * parts : 4 * parts], refs[4 * parts :]
    exact_ref, log_ref, sends, refs = refs[0], refs[1], refs[2 : 2 + parts], refs[2 + parts :]
    whole_ref, queries, keys_t, values_t, grads, keys, values, sums, weights, grad_weights, dots = refs
    blocks = queries.shape[1] // BLK
    length = table[blocks]
    scale = HEAD_DIM ** -0.5
    gather_columns(query_refs, queries)
    gather_columns(key_refs, keys_t)
    gather_columns(value_refs, values_t)
    gather_columns(grad_refs, grads)
    turn_rows(keys_t, keys, True)
    turn_rows(values_t, values, False)
    sums[...] = jnp.zeros_like(sums)
    grad_weights[...] = jnp.zeros_like(grad_weights)
    full = (length + BLK - 1) // BLK

    @pl.loop(0, full)
    def _(place):
        span = pl.ds(pl.multiple_of(table[place] * BLK, BLK), BLK)
        weights[...] = query_weights(queries[:, span])
        grad_t = grads[:, span]
        grad_weights[:HEAD_DIM, :] = grad_t
        dots[...] = jnp.sum(grad_t.astype(jnp.float32) * exact_ref[:, span], axis=0, keepdims=True)

        def step(number, masked):
            key_span = pl.ds(pl.multiple_of(table[number] * BLK, BLK), BLK)
            key_rows, value_rows = keys[key_span, :], values[key_span, :]
            halves = [slice(h * HALF, (h + 1) * HALF) for h in range(2)]
            scores_list = [nn(key_rows, weights[:, h]) for h in halves]
            inner_list = [nn(value_rows, grad_weights[:, h]) for h in halves]
            signed_list, score_grads_list = [], []
            for half in range(2):
                scores = scores_list[half]
                log_row = log_ref[:, pl.ds(pl.multiple_of(table[place] * BLK + half * HALF, HALF), HALF)]
                size = jnp.abs(scores) - log_row
                if masked:
                    mask = block_mask(number * BLK, place * BLK + half * HALF, length, size.shape)
                    size = jnp.where(mask, size, LOW)
                positive = jnp.exp2(size).astype(jnp.bfloat16)
                sign = sign_of(scores)
                signed_list.append(positive * sign)
                inner = inner_list[half] - dots[:, halves[half]] * sign.astype(jnp.float32)
                score_grads_list.append((positive.astype(jnp.float32) * inner).astype(jnp.bfloat16))
            signed = jnp.concatenate(signed_list, axis=1)
            score_grads = jnp.concatenate(score_grads_list, axis=1)
            sums[0:64, span] += nn(keys_t[:, key_span], score_grads)
            sums[64:128, key_span] += nt(queries[:, span], score_grads)
            sums[128:192, key_span] += nt(grads[:, span], signed)

        @pl.loop(0, place)
        def _(number):
            step(number, False)

        step(place, True)

    width = sends[0].shape[1]
    for part in range(parts):
        span = slice(part * width, (part + 1) * width)
        for rows, factor in ((slice(0, 128), scale), (slice(128, 192), 1.0)):
            done = (sums[rows, span] * factor).astype(jnp.bfloat16)
            whole_ref[rows, span] = done
            sends[part][rows, :] = done


def make_table(block_order, length, ctx_index, ctx):
    here = block_order.shape[0] // ctx
    order = (ctx_index - jnp.arange(ctx)) % ctx
    places = block_order.reshape(ctx, here)[order].reshape(-1)
    return jnp.concatenate([jnp.argsort(places).astype(jnp.int32), length[None]])


def head_specs(parts, span, row):
    return [pl.BlockSpec((HEAD_DIM, span), lambda i, t, row=row: (row, 0)) for _ in range(parts)]


def attend_forward(table, head, heads, packed_list):
    parts, span = len(packed_list), packed_list[0].shape[1]
    slots = parts * span
    whole = lambda shape: pl.BlockSpec(shape, lambda i, t: (0, 0))
    return pl.pallas_call(
        functools.partial(forward_kernel, parts),
        grid_spec=pltpu.PrefetchScalarGridSpec(
            num_scalar_prefetch=1,
            grid=(1,),
            in_specs=head_specs(parts, span, head)
            + head_specs(parts, span, heads + head)
            + head_specs(parts, span, 2 * heads + head),
            out_specs=[whole((HEAD_DIM, span))] * parts + [whole((HEAD_DIM, slots)), whole((1, slots))],
            scratch_shapes=[pltpu.VMEM((HEAD_DIM, slots), jnp.bfloat16)] * 3
            + [pltpu.VMEM((slots, 128), jnp.bfloat16), pltpu.VMEM((128, BLK), jnp.bfloat16)],
        ),
        out_shape=[jax.ShapeDtypeStruct((HEAD_DIM, span), jnp.bfloat16)] * parts
        + [
            jax.ShapeDtypeStruct((HEAD_DIM, slots), jnp.float32),
            jax.ShapeDtypeStruct((1, slots), jnp.float32),
        ],
        compiler_params=pltpu.CompilerParams(vmem_limit_bytes=40 << 20),
        cost_estimate=pl.CostEstimate(flops=20_000_000_000, bytes_accessed=4_000_000, transcendentals=0),
        name="attend_forward",
    )(table, *packed_list, *packed_list, *packed_list)


def attend_backward(table, head, heads, packed_list, grad_list, exact, logs):
    parts, span = len(packed_list), packed_list[0].shape[1]
    slots = parts * span
    whole = lambda shape: pl.BlockSpec(shape, lambda i, t: (0, 0))
    three = 3 * HEAD_DIM
    return pl.pallas_call(
        functools.partial(backward_kernel, parts),
        grid_spec=pltpu.PrefetchScalarGridSpec(
            num_scalar_prefetch=1,
            grid=(1,),
            in_specs=head_specs(parts, span, head)
            + head_specs(parts, span, heads + head)
            + head_specs(parts, span, 2 * heads + head)
            + [whole((HEAD_DIM, span))] * parts
            + [whole((HEAD_DIM, slots)), whole((1, slots))],
            out_specs=[whole((three, span))] * parts + [whole((three, slots))],
            scratch_shapes=[pltpu.VMEM((HEAD_DIM, slots), jnp.bfloat16)] * 4
            + [pltpu.VMEM((slots, 128), jnp.bfloat16)] * 2
            + [
                pltpu.VMEM((three, slots), jnp.float32),
                pltpu.VMEM((128, BLK), jnp.bfloat16),
                pltpu.VMEM((128, BLK), jnp.bfloat16),
                pltpu.VMEM((1, BLK), jnp.float32),
            ],
        ),
        out_shape=[jax.ShapeDtypeStruct((three, span), jnp.bfloat16)] * parts
        + [jax.ShapeDtypeStruct((three, slots), jnp.bfloat16)],
        compiler_params=pltpu.CompilerParams(vmem_limit_bytes=40 << 20),
        cost_estimate=pl.CostEstimate(flops=40_000_000_000, bytes_accessed=6_000_000, transcendentals=0),
        name="attend_backward",
    )(table, *packed_list, *packed_list, *packed_list, *grad_list, exact, logs)


def layer_norm(values, gain):
    centre = jnp.mean(values, axis=-1, keepdims=True)
    centred = values - centre
    spread = jnp.mean(centred * centred, axis=-1, keepdims=True)
    return centred * lax.rsqrt(spread + 1e-05) * gain


def gelu_tanh(values):
    return jax.nn.gelu(values, approximate=True)


def product(equation, left, right):
    return jnp.einsum(equation, left, right, preferred_element_type=jnp.float32)


def shift(array, ctx, by):
    if by % ctx == 0:
        return array
    return lax.ppermute(array, "ctx", [(i, (i + by) % ctx) for i in range(ctx)])


def turned(array, axis, by):
    return lax.dynamic_slice_in_dim(
        jnp.concatenate([array, array], axis=axis), by, array.shape[axis], axis
    )


def gather_rows(array):
    return lax.all_gather(array, "fsdp", axis=0, tiled=True)


def scatter_rows(array):
    return lax.psum_scatter(
        array.astype(jnp.bfloat16), "fsdp", scatter_dimension=0, tiled=True
    )


def scatter_pairs(array, fsdp):
    me = lax.axis_index("fsdp")
    core, chip = me % 2, me // 2
    parts = array.reshape(fsdp // 2, 2, array.shape[0] // fsdp, array.shape[1])
    kept = lax.dynamic_index_in_dim(parts, core, 1, keepdims=False)
    sent = lax.dynamic_index_in_dim(parts, 1 - core, 1, keepdims=False).astype(jnp.bfloat16)
    got = lax.ppermute(sent, "fsdp", [(i, i ^ 1) for i in range(fsdp)])
    kept = kept.astype(jnp.float32) + got.astype(jnp.float32)
    total = lax.dynamic_index_in_dim(kept, chip, 0, keepdims=False)
    narrow = kept.astype(jnp.bfloat16)
    for other in range(1, fsdp // 2):
        sent = lax.dynamic_index_in_dim(narrow, chip ^ other, 0, keepdims=False)
        got = lax.ppermute(sent, "fsdp", [(i, i ^ (2 * other)) for i in range(fsdp)])
        total += got.astype(jnp.float32)
    return total


def per_device(
    ctx, fsdp, tokens_in, out_grad, gain_attn, gain_mlp, w_qkv, w_out, w_up, w_down, lengths, block_order
):
    local_rows, width = tokens_in.shape[1:]
    tokens_in, out_grad, length, block_order = tokens_in[0], out_grad[0], lengths[0], block_order[0]
    ctx_index = lax.axis_index("ctx")
    heads_here = width // HEAD_DIM // ctx
    own = heads_here * HEAD_DIM
    table = make_table(block_order, length, ctx_index, ctx)

    gains = jnp.stack([gain_attn, gain_mlp], axis=1)
    gains = jnp.pad(gains, ((0, 0), (0, 126)))
    first = gather_rows(jnp.concatenate([w_qkv, gains], axis=1))
    gain_one = first[:, 3 * width].astype(jnp.float32)
    gain_two = first[:, 3 * width + 1].astype(jnp.float32)
    w_out_all = gather_rows(w_out)
    w_up_all = gather_rows(w_up)
    w_down_all = gather_rows(w_down)
    w_own = jnp.concatenate(
        [
            lax.dynamic_slice_in_dim(first, kind * width + ctx_index * own, own, 1)
            for kind in range(3)
        ],
        axis=1,
    )
    w_out_turned = turned(w_out_all.reshape(ctx, heads_here, HEAD_DIM, width), 0, ctx_index)
    w_out_turned = w_out_turned.transpose(1, 0, 2, 3).reshape(width, width)
    w_turned = turned(first[:, : 3 * width].reshape(width, 3, ctx, heads_here, HEAD_DIM), 2, ctx_index)
    w_turned = w_turned.transpose(0, 3, 2, 1, 4).reshape(width, 3 * width)

    here = local_rows // BLK
    places = lax.dynamic_slice_in_dim(block_order, ctx_index * here, here)
    places = (places[:, None] * BLK + jnp.arange(BLK, dtype=jnp.int32)[None]).reshape(-1)
    grad_z = out_grad * (places < length).astype(jnp.bfloat16)[:, None]

    normed_list, packed_list = [], []
    tokens = tokens_in
    for part in range(ctx):
        normed = layer_norm(tokens.astype(jnp.float32), gain_one).astype(jnp.bfloat16)
        normed_list.append(normed)
        packed_list.append(product("jn,uj->nu", w_own, normed).astype(jnp.bfloat16))
        if part == ctx - 2:
            tokens, w_out_turned, w_turned, grad_z = lax.optimization_barrier(
                (tokens, w_out_turned, w_turned, grad_z)
            )
        if part < ctx - 1:
            tokens = shift(tokens, ctx, 1)
    kept, mixed_parts = [], []
    for head in range(heads_here):
        results = attend_forward(table, head, heads_here, packed_list)
        kept.append((results[ctx], results[ctx + 1]))
        mixed_parts += [shift(results[part], ctx, -part) for part in range(ctx)]
    mixed_t = jnp.concatenate(mixed_parts, axis=0)

    tokens_f = tokens_in.astype(jnp.float32)
    middle = tokens_f + product("nu,nj->uj", mixed_t, w_out_turned)
    normed_two, norm_two_back = jax.vjp(lambda v: layer_norm(v, gain_two), middle)
    normed_two = normed_two.astype(jnp.bfloat16)
    pre_act = product("uj,jn->un", normed_two, w_up_all)
    activation, gelu_back = jax.vjp(gelu_tanh, pre_act)
    activation = activation.astype(jnp.bfloat16)
    result = (middle + product("un,nj->uj", activation, w_down_all)).astype(jnp.bfloat16)

    grad_act = product("uj,nj->un", grad_z, w_down_all)
    grad_pre = gelu_back(grad_act)[0].astype(jnp.bfloat16)
    grad_normed_two = product("un,jn->uj", grad_pre, w_up_all)
    grad_middle = grad_z.astype(jnp.float32) + norm_two_back(grad_normed_two)[0]
    grad_branch = grad_middle.astype(jnp.bfloat16)
    grad_mixed_t = product("nj,uj->nu", w_out_turned, grad_branch).astype(jnp.bfloat16)
    grads_by_head = []
    for head in range(heads_here):
        pieces = []
        for part in range(ctx):
            row = (head * ctx + part) * HEAD_DIM
            piece = grad_mixed_t[row : row + HEAD_DIM]
            pieces.append(shift(piece, ctx, part))
        grads_by_head.append(pieces)

    grad_w_down = product("un,uj->nj", activation, grad_z).astype(jnp.bfloat16)
    grad_w_up = product("uj,un->jn", normed_two, grad_pre).astype(jnp.bfloat16)
    grad_w_out = product("nu,uj->nj", mixed_t, grad_branch).astype(jnp.bfloat16)
    grad_w_out = turned(
        grad_w_out.reshape(heads_here, ctx, HEAD_DIM, width).transpose(1, 0, 2, 3), 0, (ctx - ctx_index) % ctx
    )
    grad_w_down = scatter_rows(grad_w_down)
    grad_up_out = scatter_rows(
        jnp.concatenate([grad_w_up, grad_w_out.reshape(width, width)], axis=1)
    )

    grad_parts, grad_whole = [], []
    for head in range(heads_here):
        if head == heads_here - 1:
            grad_up_out, grad_w_down, table = lax.optimization_barrier(
                (grad_up_out, grad_w_down, table)
            )
            grad_up_out, grad_w_down = lax.psum((grad_up_out, grad_w_down), "ctx")
        results = attend_backward(
            table, head, heads_here, packed_list, grads_by_head[head], *kept[head]
        )
        grad_parts += [shift(results[part], ctx, -part) for part in range(ctx)]
        grad_whole.append(results[ctx])
    normed_all = jnp.concatenate(normed_list, axis=0)
    grad_qkv_own = product("uj,nu->jn", normed_all, jnp.concatenate(grad_whole, axis=0))
    grad_qkv_own = scatter_pairs(grad_qkv_own, fsdp).astype(jnp.bfloat16)
    grad_qkv = lax.all_gather(grad_qkv_own, "ctx", axis=0)
    rows_here = grad_qkv.shape[1]
    grad_qkv = grad_qkv.reshape(ctx, rows_here, heads_here, 3, HEAD_DIM)
    grad_w_qkv = grad_qkv.transpose(1, 3, 0, 2, 4).reshape(rows_here, 3 * width).astype(jnp.float32)

    grad_packed_t = jnp.concatenate(grad_parts, axis=0)
    grad_normed_one = product("nu,jn->uj", grad_packed_t, w_turned)
    norm_one_back = jax.vjp(lambda v: layer_norm(v, gain_one), tokens_f)[1]
    grad_tokens = (grad_middle + norm_one_back(grad_normed_one)[0]).astype(jnp.bfloat16)

    grad_w_down = grad_w_down.astype(jnp.float32)
    grad_w_up = grad_up_out[:, : w_up.shape[1]].astype(jnp.float32)
    grad_w_out = grad_up_out[:, w_up.shape[1] :].astype(jnp.float32)

    def gain_grad(grad_weight, weight, gain):
        total = jnp.sum(grad_weight * weight.astype(jnp.float32), axis=1)
        return total / gain.astype(jnp.float32)

    return (
        result[None],
        grad_tokens[None],
        gain_grad(grad_w_qkv, w_qkv, gain_attn),
        gain_grad(grad_w_up, w_up, gain_mlp),
        grad_w_qkv,
        grad_w_out,
        grad_w_up,
        grad_w_down,
    )


def solution(mesh):
    rows = P("fsdp", None)
    whole = P("fsdp", "ctx", None)
    ctx, fsdp = mesh.shape["ctx"], mesh.shape["fsdp"]

    def layer(*arrays):
        return per_device(ctx, fsdp, *arrays)

    return jax.shard_map(
        layer,
        mesh=mesh,
        in_specs=(whole, whole, P("fsdp"), P("fsdp"), rows, rows, rows, rows, P("fsdp"), rows),
        out_specs=(whole, whole, P("fsdp"), P("fsdp"), rows, rows, rows, rows),
        check_vma=False,
    )
```

profile of v0, /device:TPU:0, one launch (start us, length us, event | category | flops | bytes accessed | tf_op | source)
XLA Modules:
  0.0 606.8 jit_solution(13972256891861155565)
XLA Ops:
  20.3 32.5 %collective-permute-done = bf16[1024,768]{0,1:T(8,128)(2,1)} collective-permute-done((bf16[1024,768]{0,1:T(8,128)(2,1)S(1)}, bf16[1024,768]{0,1:T(8,128)(2,1)}, u32[]{:S(2)}, u32[]{:S(2)}) %collective-permute-start) | collective-permute-done | bytes 1572896 | tf_op jit(solution)/shard_map/ppermute | solution.py:265
  64.4 9.4 %all-gather.6.cloned.1.call-done = bf16[768,2432]{1,0:T(8,128)(2,1)} async-done(((bf16[96,2432]{1,0:T(8,128)(2,1)}), bf16[768,2432]{1,0:T(8,128)(2,1)}) %all-gather.6.cloned.1.call-update) | async-done | bytes 3735568 | tf_op jit(solution)/shard_map/all_gather | solution.py:275
  73.8 4.0 slice.71
  77.8 5.8 copy.102
  83.5 3.4 fusion.31
  100.0 28.1 %collective-permute-done.2 = bf16[1024,768]{0,1:T(8,128)(2,1)S(1)} collective-permute-done((bf16[1024,768]{0,1:T(8,128)(2,1)}, bf16[1024,768]{0,1:T(8,128)(2,1)S(1)}, u32[]{:S(2)}, u32[]{:S(2)}) %collective-permute-start.2) | collective-permute-done | bytes 1572896 | tf_op jit(solution)/shard_map/ppermute | solution.py:265
  128.9 3.8 fusion.34
  138.2 16.0 %attend_forward.5 = (bf16[64,1024]{1,0:T(8,128)(2,1)S(1)}, bf16[64,1024]{1,0:T(8,128)(2,1)S(1)}, bf16[64,1024]{1,0:T(8,128)(2,1)S(1)}, bf16[64,1024]{1,0:T(8,128...) custom-call(s32[9]{0:T(128)S(1)} %pad_add_fusion.table, ...), custom_call_target="tpu_custom_call" | custom-call | flops 20000000000 | bytes 4000000 | tf_op jit(solution)/shard_map/attend_forward/pallas_call | solution.py:191
  154.1 15.9 %attend_forward.3 = (bf16[64,1024]{1,0:T(8,128)(2,1)S(1)}, bf16[64,1024]{1,0:T(8,128)(2,1)S(1)}, bf16[64,1024]{1,0:T(8,128)(2,1)S(1)}, bf16[64,1024]{1,0:T(8,128...) custom-call(s32[9]{0:T(128)S(1)} %pad_add_fusion.table, ...), custom_call_target="tpu_custom_call" | custom-call | flops 20000000000 | bytes 4000000 | tf_op jit(solution)/shard_map/attend_forward/pallas_call | solution.py:191
  172.8 15.9 %attend_forward.4 = (bf16[64,1024]{1,0:T(8,128)(2,1)S(1)}, bf16[64,1024]{1,0:T(8,128)(2,1)S(1)}, bf16[64,1024]{1,0:T(8,128)(2,1)S(1)}, bf16[64,1024]{1,0:T(8,128...) custom-call(s32[9]{0:T(128)S(1)} %pad_add_fusion.table, ...), custom_call_target="tpu_custom_call" | custom-call | flops 20000000000 | bytes 4000000 | tf_op jit(solution)/shard_map/attend_forward/pallas_call | solution.py:191
  195.2 8.3 %collective-permute-done.4 = bf16[64,1024]{1,0:T(8,128)(2,1)S(1)} collective-permute-done((bf16[64,1024]{1,0:T(8,128)(2,1)S(1)}, bf16[64,1024]{1,0:T(8,128)(2,1)S(1)}, u32[]{:S(2)}, u32[]{:S(2)}) %collective-permute-start.4) | collective-permute-done | bytes 131104 | tf_op jit(solution)/shard_map/ppermute | solution.py:265
  208.5 3.4 collective-permute-done.7
  220.9 11.2 %fusion.66 = f32[1024,3072]{1,0:T(8,128)} fusion(bf16[768,3072]{1,0:T(8,128)(2,1)} %all-gather.10.cloned.1.call-done, f32[1024,768]{0,1:T(8,128)} %get-tuple-element.171, f32[768]{0:T(1024)S(1)} %get-tuple-element.138, f32[1024]{0:T(1024)S(1)} %fusion.59, f32[1024]{0:T(1024)S(1)} %broadcast_multiply_fusion), kind=kOutput, calls=%fused_computation.170 | convolution fusion | flops 4834983936 | bytes 20458496 | tf_op jit(solution)/shard_map/uj,jn->un/dot_general | solution.py:259
  232.1 12.8 %convolution_convert_fusion = bf16[3072,768]{1,0:T(8,128)(2,1)} fusion(bf16[1024,768]{0,1:T(8,128)(2,1)S(1)} %copy-done.24, f32[1024,3072]{1,0:T(8,128)} %fusion.66), kind=kOutput, calls=%fused_computation.22 | convolution fusion | flops 4862509056 | bytes 18874368 | tf_op jit(solution)/shard_map/un,uj->nj/dot_general | solution.py:259
  245.2 14.6 %fusion.6 = bf16[1024,3072]{1,0:T(8,128)(2,1)S(1)} fusion(f32[1024,3072]{1,0:T(8,128)} %fusion.66, bf16[1024,768]{0,1:T(8,128)(2,1)S(1)} %copy-done.24, bf16[3072,768]{1,0:T(8,128)(2,1)} %all-gather.12.cloned.1.call-done), kind=kOutput, calls=%fused_computation.9 | convolution fusion | flops 4894752768 | bytes 25165824 | tf_op jit(solution)/shard_map/uj,nj->un/dot_general | solution.py:259
  259.8 7.7 %multiply_reduce_fusion = (f32[1024]{0:T(1024)S(1)}, f32[1024,768]{0,1:T(8,128)S(1)}) fusion(f32[1024,768]{0,1:T(8,128)} %get-tuple-element.171, f32[768]{0:T(1024)S(1)} %get-tuple-element.138, f32[1024]{0:T(1024)S(1)} %broadcast_multiply_fusion, bf16[1024,3072]{1,0:T(8,128)(2,1)S(1)} %fusion.6, bf16[768,3072]{1,0:T(8,128)(2,1)} %all-gather.10.cloned.1.call-done), kind=kOutput, calls=%fused_computation.67 | convolution fusion | flops 4834982912 | bytes 17312768 | tf_op jit(solution)/shard_map/un,jn->uj/dot_general | solution.py:259
  279.2 7.3 %convolution_convert_fusion.1 = bf16[768,3072]{1,0:T(8,128)(2,1)S(1)} fusion(bf16[1024,3072]{1,0:T(8,128)(2,1)S(1)} %fusion.6, f32[1024,768]{0,1:T(8,128)} %get-tuple-element.171, f32[768]{0:T(1024)S(1)} %get-tuple-element.138, f32[1024]{0:T(1024)S(1)} %fusion.59, f32[1024]{0:T(1024)S(1)} %broadcast_multiply_fusion), kind=kOutput, calls=%fused_computation.23 | convolution fusion | flops 4837343232 | bytes 14167040 | tf_op jit(solution)/shard_map/uj,un->jn/dot_general | solution.py:259
  289.9 11.7 %fusion.47 = bf16[1,1024,768]{1,2,0:T(8,128)(2,1)} fusion(f32[1024,768]{0,1:T(8,128)} %get-tuple-element.171, bf16[3072,768]{1,0:T(8,128)(2,1)} %all-gather.12.cloned.1.call-done, f32[1024,3072]{1,0:T(8,128)} %fusion.66), kind=kOutput, calls=%fused_computation.84 | convolution fusion | flops 4861722624 | bytes 22020096 | tf_op jit(solution)/shard_map/un,nj->uj/dot_general | solution.py:259
  317.5 8.3 %attend_backward.3 = (bf16[192,1024]{1,0:T(8,128)(2,1)S(1)}, bf16[192,1024]{1,0:T(8,128)(2,1)S(1)}, bf16[192,1024]{1,0:T(8,128)(2,1)S(1)}, bf16[192,1024]{1,0:T(8,128)(2,1)S(1)}, bf16[192,4096]{1,0:T(8,128)(2,1)S(1)}) custom-call(s32[9]{0:T(128)S(1)} %pad_add_fusion.table, bf16[576,1024]{1,0:T(8,128)(2,1)S(1)} %copy-done.8, bf16[576,1024]{1,0:T(8,128)(2,1)S(1)} %copy-done.1, ...), custom_call_target="tpu_custom_call" | custom-call | flops 40000000000 | bytes 6000000 | tf_op jit(solution)/shard_map/attend_backward/pallas_call | solution.py:219
  330.3 8.3 %attend_backward.4 = (bf16[192,1024]{1,0:T(8,128)(2,1)S(1)}, bf16[192,1024]{1,0:T(8,128)(2,1)S(1)}, bf16[192,1024]{1,0:T(8,128)(2,1)S(1)}, bf16[192,1024]{1,0:T(8,128)(2,1)S(1)}, bf16[192,4096]{1,0:T(8,128)(2,1)S(1)}) custom-call(s32[9]{0:T(128)S(1)} %pad_add_fusion.table, bf16[576,1024]{1,0:T(8,128)(2,1)S(1)} %copy-done.8, bf16[576,1024]{1,0:T(8,128)(2,1)S(1)} %copy-done.1, ...), custom_call_target="tpu_custom_call" | custom-call | flops 40000000000 | bytes 6000000 | tf_op jit(solution)/shard_map/attend_backward/pallas_call | solution.py:219
  343.0 13.6 %collective-permute-done.16 = bf16[192,1024]{1,0:T(8,128)(2,1)S(1)} collective-permute-done((bf16[192,1024]{1,0:T(8,128)(2,1)S(1)}, bf16[192,1024]{1,0:T(8,128)(2,1)S(1)}, u32[]{:S(2)}, u32[]{:S(2)}) %collective-permute-start.16) | collective-permute-done | bytes 393248 | tf_op jit(solution)/shard_map/ppermute | solution.py:265
  357.4 9.1 %collective-permute-start.23 = (bf16[192,1024]{1,0:T(8,128)(2,1)S(1)}, bf16[192,1024]{1,0:T(8,128)(2,1)S(1)}, u32[]{:S(2)}, u32[]{:S(2)}) collective-permute-start(bf16[192,1024]{1,0:T(8,128)(2,1)S(1)} %get-tuple-element.76), channel_id=1, source_target_pairs={{0,8},{8,16},{16,24},{24,0},{1,9},{9,17},{17,25},{25,1},{2,10},{10... | collective-permute-start | bytes 1179656 | tf_op jit(solution)/shard_map/ppermute | solution.py:265
  371.3 4.5 collective-permute-done.22
  377.3 13.3 %reduce-scatter.3.cloned.1.call-done = bf16[96,3840]{1,0:T(8,128)(2,1)} async-done(((bf16[768,3840]{1,0:T(8,128)(2,1)}), bf16[96,3840]{1,0:T(8,128)(2,1)}) %reduce-scatter.3.cloned.1.call-update) | async-done | bytes 737296 | tf_op jit(solution)/shard_map/reduce_scatter | solution.py:279
  395.7 8.4 %attend_backward.5 = (bf16[192,1024]{1,0:T(8,128)(2,1)S(1)}, bf16[192,1024]{1,0:T(8,128)(2,1)S(1)}, bf16[192,1024]{1,0:T(8,128)(2,1)S(1)}, bf16[192,1024]{1,0:T(8,128)(2,1)S(1)}, bf16[192,4096]{1,0:T(8,128)(2,1)S(1)}) custom-call(s32[9]{0:T(128)S(1)} %pad_add_fusion.table, bf16[576,1024]{1,0:T(8,128)(2,1)S(1)} %copy-done.9, bf16[576,1024]{1,0:T(8,128)(2,1)S(1)} %copy-done.2, ...), custom_call_target="tpu_custom_call" | custom-call | flops 40000000000 | bytes 6000000 | tf_op jit(solution)/shard_map/attend_backward/pallas_call | solution.py:219
  404.1 3.4 collective-permute-start.27
  408.7 7.8 %fusion.7 = f32[768,576]{1,0:T(8,128)} fusion(bf16[1024,768]{0,1:T(8,128)(2,1)S(1)} %copy-done.30, bf16[1024,768]{0,1:T(8,128)(2,1)S(1)} %copy-done.34, bf16[1024,768]{0,1:T(8,128)(2,1)S(1)} %copy-done.32, bf16[1024,768]{0,1:T(8,128)(2,1)} %copy-done.35, bf16[192,4096]{1,0:T(8,128)(2,1)S(1)} %get-tuple-element.87, bf16[192,4096]{1,0:T(8,128)(2,1)S(1)} %copy-done.13, ...), kind=kOutput, calls=%fused_computation.13 | convolution fusion | flops 3663200256 | bytes 12779520 | tf_op jit(solution)/shard_map/uj,nu->jn/dot_general | solution.py:259
  418.6 90.4 %collective-permute-start.30 = (bf16[4,96,576]{2,1,0:T(8,128)(2,1)}, bf16[4,96,576]{2,1,0:T(8,128)(2,1)}, u32[]{:S(2)}, u32[]{:S(2)}) collective-permute-start(bf16[4,96,576]{2,1,0:T(8,128)(2,1)} %fusion.52), channel_id=1, source_target_pairs={{0,1},{1,0},{2,3},{3,2},{4,5},{5,4},{6,7},{7,6},{8,9},{9,8},{10,11... | collective-permute-start | bytes 1327112 | tf_op jit(solution)/shard_map/ppermute | solution.py:290
  515.2 7.0 %fusion.44 = (f32[1024]{0:T(1024)S(1)}, f32[1024,768]{0,1:T(8,128)S(1)}) fusion(f32[768]{0:T(1024)S(1)} %copy-done.48, f32[1024]{0:T(1024)S(1)} %copy-done.46, bf16[1,1024,768]{1,2,0:T(8,128)(2,1)S(1)} %copy-done.21, bf16[2304,1024]{1,0:T(8,128)(2,1)} %constant_dynamic-update-slice_fusion.12, bf16[768,2304]{0,1:T(8,128)(2,1)} %bitcast.89), kind=kOutput, calls=%fused_computation.64 | convolution fusion | flops 3627809792 | bytes 12987392 | tf_op jit(solution)/shard_map/nu,jn->uj/dot_general | solution.py:259
  527.0 23.9 %collective-permute-start.31 = (bf16[96,576]{1,0:T(8,128)(2,1)}, bf16[96,576]{1,0:T(8,128)(2,1)S(1)}, u32[]{:S(2)}, u32[]{:S(2)}) collective-permute-start(bf16[96,576]{1,0:T(8,128)(2,1)} %get-tuple-element.163), channel_id=1, source_target_pairs={{0,2},{1,3},{2,0},{3,1},{4,6},{5,7},{6,4},{7,5},{8,10},{9,11},{10,... | collective-permute-start | bytes 331784 | tf_op jit(solution)/shard_map/ppermute | solution.py:296
  558.3 17.8 %all-gather = bf16[384,576]{1,0:T(8,128)(2,1)S(1)} all-gather(bf16[96,576]{1,0:T(8,128)(2,1)S(1)} %fusion.57), channel_id=2, replica_groups=mesh['ctx'=4,'fsdp'=8] {'ctx'}, dimensions={0}, use_global_device_ids=true | all-gather | bytes 552960 | tf_op jit(solution)/shard_map/all_gather | solution.py:405
  579.5 14.6 %all-reduce.4.cloned.1.call-done = (bf16[96,3840]{1,0:T(8,128)(2,1)}, bf16[384,768]{1,0:T(8,128)(2,1)}) async-done(((bf16[96,3840]{1,0:T(8,128)(2,1)}, bf16[384,768]{1,0:T(8,128)(2,1)}), (bf16[96,3840]{1,0:T(8,128)(2,1)}, bf16[384,768]{1,0:T(8,128)(2,1)})) %all-reduce.4.cloned.1.call-update) | async-done | bytes 1327120 | tf_op jit(solution)/shard_map/psum | solution.py:396
  (299 shorter events, 148.9 us)
Async XLA Ops:
  7.2 54.4 %all-gather.8.cloned.1.call-start = ((), (), s32[]{:S(2)}) async-start(), calls=%async_computation.3 | async-start | bytes 1327104 | tf_op jit(solution)/shard_map/all_gather | solution.py:275
  7.9 65.9 %all-gather.6.cloned.1.call-start = ((), (), s32[]{:S(2)}) async-start(), calls=%async_computation.2 | async-start | bytes 4202496 | tf_op jit(solution)/shard_map/all_gather | solution.py:275
  10.6 210.3 %all-gather.10.cloned.1.call-start = ((), (), s32[]{:S(2)}) async-start(), calls=%async_computation.4 | async-start | bytes 5308416 | tf_op jit(solution)/shard_map/all_gather | solution.py:275
  11.4 233.9 %all-gather.12.cloned.1.call-start = ((), (), s32[]{:S(2)}) async-start(), calls=%async_computation.5 | async-start | bytes 5308416 | tf_op jit(solution)/shard_map/all_gather | solution.py:275
  13.1 39.6 %collective-permute-start = (bf16[1024,768]{0,1:T(8,128)(2,1)S(1)}, bf16[1024,768]{0,1:T(8,128)(2,1)}, u32[]{:S(2)}, u32[]{:S(2)}) collective-permute-start(bf16[1024,768]{0,1:T(8,128)(2,1)S(1)} %bitcast.83), channel_id=1, source_target_pairs={{0,8},{8,16},{16,24},{24,0},{1,9},{9,17},{17,25},{25,1},{2,10},{10... | collective-permute-start | bytes 4718600 | tf_op jit(solution)/shard_map/ppermute | solution.py:265
  16.3 361.1 %reduce-scatter.5.cloned.1.call-start = ((), (), s32[]{:S(2)}) async-start(), calls=%async_computation.7 | async-start | bytes 5308416 | tf_op jit(solution)/shard_map/reduce_scatter | solution.py:279
  52.8 37.7 %collective-permute-start.1 = (bf16[1024,768]{0,1:T(8,128)(2,1)}, bf16[1024,768]{0,1:T(8,128)(2,1)}, u32[]{:S(2)}, u32[]{:S(2)}) collective-permute-start(bf16[1024,768]{0,1:T(8,128)(2,1)} %collective-permute-done), channel_id=1, source_target_pairs={{0,8},{8,16},{16,24},{24,0},{1,9},{9,17},{17,25},{25,1},{2,10},{10... | collective-permute-start | bytes 4718600 | tf_op jit(solution)/shard_map/ppermute | solution.py:265
  90.4 37.7 %collective-permute-start.2 = (bf16[1024,768]{0,1:T(8,128)(2,1)}, bf16[1024,768]{0,1:T(8,128)(2,1)S(1)}, u32[]{:S(2)}, u32[]{:S(2)}) collective-permute-start(bf16[1024,768]{0,1:T(8,128)(2,1)} %collective-permute-done.1), channel_id=1, source_target_pairs={{0,8},{8,16},{16,24},{24,0},{1,9},{9,17},{17,25},{25,1},{2,10},{10... | collective-permute-start | bytes 4718600 | tf_op jit(solution)/shard_map/ppermute | solution.py:265
  171.1 22.7 %collective-permute-start.3 = (bf16[64,1024]{1,0:T(8,128)(2,1)S(1)}, bf16[64,1024]{1,0:T(8,128)(2,1)S(1)}, u32[]{:S(2)}, u32[]{:S(2)}) collective-permute-start(bf16[64,1024]{1,0:T(8,128)(2,1)S(1)} %get-tuple-element.52), channel_id=1, source_target_pairs={{0,24},{8,0},{16,8},{24,16},{1,25},{9,1},{17,9},{25,17},{2,26},{10... | collective-permute-start | bytes 393224 | tf_op jit(solution)/shard_map/ppermute | solution.py:265
  188.8 26.5 %collective-permute-start.9 = (bf16[64,1024]{1,0:T(8,128)(2,1)S(1)}, bf16[64,1024]{1,0:T(8,128)(2,1)S(1)}, u32[]{:S(2)}, u32[]{:S(2)}) collective-permute-start(bf16[64,1024]{1,0:T(8,128)(2,1)S(1)} %get-tuple-element.60), channel_id=1, source_target_pairs={{0,24},{8,0},{16,8},{24,16},{1,25},{9,1},{17,9},{25,17},{2,26},{10... | collective-permute-start | bytes 393224 | tf_op jit(solution)/shard_map/ppermute | solution.py:265
  189.4 26.0 %collective-permute-start.10 = (bf16[64,1024]{1,0:T(8,128)(2,1)S(1)}, bf16[64,1024]{1,0:T(8,128)(2,1)S(1)}, u32[]{:S(2)}, u32[]{:S(2)}) collective-permute-start(bf16[64,1024]{1,0:T(8,128)(2,1)S(1)} %get-tuple-element.61), channel_id=1, source_target_pairs={{0,16},{8,24},{16,0},{24,8},{1,17},{9,25},{17,1},{25,9},{2,18},{10... | collective-permute-start | bytes 393224 | tf_op jit(solution)/shard_map/ppermute | solution.py:265
  190.8 24.6 %collective-permute-start.11 = (bf16[64,1024]{1,0:T(8,128)(2,1)S(1)}, bf16[64,1024]{1,0:T(8,128)(2,1)S(1)}, u32[]{:S(2)}, u32[]{:S(2)}) collective-permute-start(bf16[64,1024]{1,0:T(8,128)(2,1)S(1)} %get-tuple-element.62), channel_id=1, source_target_pairs={{0,8},{8,16},{16,24},{24,0},{1,9},{9,17},{17,25},{25,1},{2,10},{10... | collective-permute-start | bytes 393224 | tf_op jit(solution)/shard_map/ppermute | solution.py:265
  244.9 145.7 %reduce-scatter.3.cloned.1.call-start = ((), (), s32[]{:S(2)}) async-start(), calls=%async_computation.6 | async-start | bytes 6635520 | tf_op jit(solution)/shard_map/reduce_scatter | solution.py:279
  276.7 32.1 %collective-permute-start.14 = (bf16[64,1024]{1,0:T(8,128)(2,1)}, bf16[64,1024]{1,0:T(8,128)(2,1)S(1)}, u32[]{:S(2)}, u32[]{:S(2)}) collective-permute-start(bf16[64,1024]{1,0:T(8,128)(2,1)} %get-tuple-element.159), channel_id=1, source_target_pairs={{0,24},{8,0},{16,8},{24,16},{1,25},{9,1},{17,9},{25,17},{2,26},{10... | collective-permute-start | bytes 393224 | tf_op jit(solution)/shard_map/ppermute | solution.py:265
  277.9 31.9 %collective-permute-start.13 = (bf16[64,1024]{1,0:T(8,128)(2,1)}, bf16[64,1024]{1,0:T(8,128)(2,1)S(1)}, u32[]{:S(2)}, u32[]{:S(2)}) collective-permute-start(bf16[64,1024]{1,0:T(8,128)(2,1)} %get-tuple-element.160), channel_id=1, source_target_pairs={{0,16},{8,24},{16,0},{24,8},{1,17},{9,25},{17,1},{25,9},{2,18},{10... | collective-permute-start | bytes 393224 | tf_op jit(solution)/shard_map/ppermute | solution.py:265
  277.9 33.0 %collective-permute-start.12 = (bf16[64,1024]{1,0:T(8,128)(2,1)}, bf16[64,1024]{1,0:T(8,128)(2,1)S(1)}, u32[]{:S(2)}, u32[]{:S(2)}) collective-permute-start(bf16[64,1024]{1,0:T(8,128)(2,1)} %get-tuple-element.161), channel_id=1, source_target_pairs={{0,8},{8,16},{16,24},{24,0},{1,9},{9,17},{17,25},{25,1},{2,10},{10... | collective-permute-start | bytes 393224 | tf_op jit(solution)/shard_map/ppermute | solution.py:265
  289.4 304.7 %all-reduce.4.cloned.1.call-start = ((), (), s32[]{:S(2)}) async-start(), calls=%async_computation.8 | async-start | bytes 2654208 | tf_op jit(solution)/shard_map/psum | solution.py:396
  304.3 86.3 %collective-permute-start.26 = (bf16[64,1024]{1,0:T(8,128)(2,1)S(1)}, bf16[64,1024]{1,0:T(8,128)(2,1)S(1)}, u32[]{:S(2)}, u32[]{:S(2)}) collective-permute-start(bf16[64,1024]{1,0:T(8,128)(2,1)S(1)} %copy-done.41), channel_id=1, source_target_pairs={{0,24},{8,0},{16,8},{24,16},{1,25},{9,1},{17,9},{25,17},{2,26},{10... | collective-permute-start | bytes 393224 | tf_op jit(solution)/shard_map/ppermute | solution.py:265
  307.5 83.1 %collective-permute-start.25 = (bf16[64,1024]{1,0:T(8,128)(2,1)S(1)}, bf16[64,1024]{1,0:T(8,128)(2,1)S(1)}, u32[]{:S(2)}, u32[]{:S(2)}) collective-permute-start(bf16[64,1024]{1,0:T(8,128)(2,1)S(1)} %copy-done.40), channel_id=1, source_target_pairs={{0,16},{8,24},{16,0},{24,8},{1,17},{9,25},{17,1},{25,9},{2,18},{10... | collective-permute-start | bytes 393224 | tf_op jit(solution)/shard_map/ppermute | solution.py:265
  309.8 19.4 %collective-permute-start.19 = (bf16[64,1024]{1,0:T(8,128)(2,1)S(1)}, bf16[64,1024]{1,0:T(8,128)(2,1)S(1)}, u32[]{:S(2)}, u32[]{:S(2)}) collective-permute-start(bf16[64,1024]{1,0:T(8,128)(2,1)S(1)} %copy-done.43), channel_id=1, source_target_pairs={{0,16},{8,24},{16,0},{24,8},{1,17},{9,25},{17,1},{25,9},{2,18},{10... | collective-permute-start | bytes 393224 | tf_op jit(solution)/shard_map/ppermute | solution.py:265
  310.8 18.4 %collective-permute-start.18 = (bf16[64,1024]{1,0:T(8,128)(2,1)S(1)}, bf16[64,1024]{1,0:T(8,128)(2,1)S(1)}, u32[]{:S(2)}, u32[]{:S(2)}) collective-permute-start(bf16[64,1024]{1,0:T(8,128)(2,1)S(1)} %copy-done.42), channel_id=1, source_target_pairs={{0,8},{8,16},{16,24},{24,0},{1,9},{9,17},{17,25},{25,1},{2,10},{10... | collective-permute-start | bytes 393224 | tf_op jit(solution)/shard_map/ppermute | solution.py:265
  329.1 27.4 %collective-permute-start.16 = (bf16[192,1024]{1,0:T(8,128)(2,1)S(1)}, bf16[192,1024]{1,0:T(8,128)(2,1)S(1)}, u32[]{:S(2)}, u32[]{:S(2)}) collective-permute-start(bf16[192,1024]{1,0:T(8,128)(2,1)S(1)} %get-tuple-element.69), channel_id=1, source_target_pairs={{0,16},{8,24},{16,0},{24,8},{1,17},{9,25},{17,1},{25,9},{2,18},{10... | collective-permute-start | bytes 1179656 | tf_op jit(solution)/shard_map/ppermute | solution.py:265
  329.2 28.1 %collective-permute-start.17 = (bf16[192,1024]{1,0:T(8,128)(2,1)S(1)}, bf16[192,1024]{1,0:T(8,128)(2,1)S(1)}, u32[]{:S(2)}, u32[]{:S(2)}) collective-permute-start(bf16[192,1024]{1,0:T(8,128)(2,1)S(1)} %get-tuple-element.70), channel_id=1, source_target_pairs={{0,8},{8,16},{16,24},{24,0},{1,9},{9,17},{17,25},{25,1},{2,10},{10... | collective-permute-start | bytes 1179656 | tf_op jit(solution)/shard_map/ppermute | solution.py:265
  339.4 28.6 %collective-permute-start.21 = (bf16[192,1024]{1,0:T(8,128)(2,1)S(1)}, bf16[192,1024]{1,0:T(8,128)(2,1)S(1)}, u32[]{:S(2)}, u32[]{:S(2)}) collective-permute-start(bf16[192,1024]{1,0:T(8,128)(2,1)S(1)} %get-tuple-element.74), channel_id=1, source_target_pairs={{0,24},{8,0},{16,8},{24,16},{1,25},{9,1},{17,9},{25,17},{2,26},{10... | collective-permute-start | bytes 1179656 | tf_op jit(solution)/shard_map/ppermute | solution.py:265
  356.6 19.2 %collective-permute-start.22 = (bf16[192,1024]{1,0:T(8,128)(2,1)S(1)}, bf16[192,1024]{1,0:T(8,128)(2,1)S(1)}, u32[]{:S(2)}, u32[]{:S(2)}) collective-permute-start(bf16[192,1024]{1,0:T(8,128)(2,1)S(1)} %get-tuple-element.75), channel_id=1, source_target_pairs={{0,16},{8,24},{16,0},{24,8},{1,17},{9,25},{17,1},{25,9},{2,18},{10... | collective-permute-start | bytes 1179656 | tf_op jit(solution)/shard_map/ppermute | solution.py:265
  357.4 19.2 %collective-permute-start.23 = (bf16[192,1024]{1,0:T(8,128)(2,1)S(1)}, bf16[192,1024]{1,0:T(8,128)(2,1)S(1)}, u32[]{:S(2)}, u32[]{:S(2)}) collective-permute-start(bf16[192,1024]{1,0:T(8,128)(2,1)S(1)} %get-tuple-element.76), channel_id=1, source_target_pairs={{0,8},{8,16},{16,24},{24,0},{1,9},{9,17},{17,25},{25,1},{2,10},{10... | collective-permute-start | bytes 1179656 | tf_op jit(solution)/shard_map/ppermute | solution.py:265
  368.0 22.6 %collective-permute-start.24 = (bf16[64,1024]{1,0:T(8,128)(2,1)S(1)}, bf16[64,1024]{1,0:T(8,128)(2,1)S(1)}, u32[]{:S(2)}, u32[]{:S(2)}) collective-permute-start(bf16[64,1024]{1,0:T(8,128)(2,1)S(1)} %get-tuple-element.153), channel_id=1, source_target_pairs={{0,8},{8,16},{16,24},{24,0},{1,9},{9,17},{17,25},{25,1},{2,10},{10... | collective-permute-start | bytes 393224 | tf_op jit(solution)/shard_map/ppermute | solution.py:265
  404.1 105.7 %collective-permute-start.27 = (bf16[192,1024]{1,0:T(8,128)(2,1)S(1)}, bf16[192,1024]{1,0:T(8,128)(2,1)}, u32[]{:S(2)}, u32[]{:S(2)}) collective-permute-start(bf16[192,1024]{1,0:T(8,128)(2,1)S(1)} %get-tuple-element.81), channel_id=1, source_target_pairs={{0,24},{8,0},{16,8},{24,16},{1,25},{9,1},{17,9},{25,17},{2,26},{10... | collective-permute-start | bytes 1179656 | tf_op jit(solution)/shard_map/ppermute | solution.py:265
  407.5 104.1 %collective-permute-start.28 = (bf16[192,1024]{1,0:T(8,128)(2,1)S(1)}, bf16[192,1024]{1,0:T(8,128)(2,1)}, u32[]{:S(2)}, u32[]{:S(2)}) collective-permute-start(bf16[192,1024]{1,0:T(8,128)(2,1)S(1)} %get-tuple-element.82), channel_id=1, source_target_pairs={{0,16},{8,24},{16,0},{24,8},{1,17},{9,25},{17,1},{25,9},{2,18},{10... | collective-permute-start | bytes 1179656 | tf_op jit(solution)/shard_map/ppermute | solution.py:265
  407.5 105.9 %collective-permute-start.29 = (bf16[192,1024]{1,0:T(8,128)(2,1)S(1)}, bf16[192,1024]{1,0:T(8,128)(2,1)}, u32[]{:S(2)}, u32[]{:S(2)}) collective-permute-start(bf16[192,1024]{1,0:T(8,128)(2,1)S(1)} %get-tuple-element.83), channel_id=1, source_target_pairs={{0,8},{8,16},{16,24},{24,0},{1,9},{9,17},{17,25},{25,1},{2,10},{10... | collective-permute-start | bytes 1179656 | tf_op jit(solution)/shard_map/ppermute | solution.py:265
  418.6 104.6 %collective-permute-start.30 = (bf16[4,96,576]{2,1,0:T(8,128)(2,1)}, bf16[4,96,576]{2,1,0:T(8,128)(2,1)}, u32[]{:S(2)}, u32[]{:S(2)}) collective-permute-start(bf16[4,96,576]{2,1,0:T(8,128)(2,1)} %fusion.52), channel_id=1, source_target_pairs={{0,1},{1,0},{2,3},{3,2},{4,5},{5,4},{6,7},{7,6},{8,9},{9,8},{10,11... | collective-permute-start | bytes 1327112 | tf_op jit(solution)/shard_map/ppermute | solution.py:290
  527.0 28.6 %collective-permute-start.31 = (bf16[96,576]{1,0:T(8,128)(2,1)}, bf16[96,576]{1,0:T(8,128)(2,1)S(1)}, u32[]{:S(2)}, u32[]{:S(2)}) collective-permute-start(bf16[96,576]{1,0:T(8,128)(2,1)} %get-tuple-element.163), channel_id=1, source_target_pairs={{0,2},{1,3},{2,0},{3,1},{4,6},{5,7},{6,4},{7,5},{8,10},{9,11},{10,... | collective-permute-start | bytes 331784 | tf_op jit(solution)/shard_map/ppermute | solution.py:296
  (69 other events, 1397.9 us)
Sparse Core Ops, SparseCore 0:
  9.9 26.7 all-gather.7
  39.1 34.6 all-gather.5
  75.7 38.7 all-gather.9
  116.2 38.7 all-gather.11
  245.0 82.4 reduce-scatter.4
  330.9 59.6 reduce-scatter.2
  509.2 84.8 all-reduce.3
where the time goes:
time: 613 us; the launch traced here: 607 us
  starting transfers between devices  163 us (27%)
  waiting for transfers between devices  139 us (23%)
  matrix products  91.1 us (15%)
  Pallas kernels  72.8 us (12%)
  local copies, waits for them, and re-layouts  60.3 us (10%)
  other arithmetic  47.7 us (8%)
  blocking collectives  17.8 us (3%)
  between operations  15.9 us (3%)
    ppermute x30, waiting for transfers between devices, shift(): return lax.ppermute(array, 'ctx', [(i, (i + by) % ctx) for i in range(ctx)])  98.4 us
    dot_general x15, matrix products, product(): return jnp.einsum(equation, left, right, preferred_element_type=jnp.float32)  91.1 us
    ppermute x1, starting transfers between devices, scatter_pairs(): got = lax.ppermute(sent, 'fsdp', [(i, i ^ 1) for i in range(fsdp)])  90.4 us
    pallas_call x3, Pallas kernels, attend_forward(): pl.pallas_call(functools.partial(forward_kernel, parts), grid_spec=pltpu....  47.8 us
    ppermute x30, starting transfers between devices, shift(): return lax.ppermute(array, 'ctx', [(i, (i + by) % ctx) for i in range(ctx)])  45.8 us
    unnamed x152, local copies, waits for them, and re-layouts  43.2 us
    ppermute x3, starting transfers between devices, scatter_pairs(): got = lax.ppermute(sent, 'fsdp', [(i, i ^ 2 * other) for i in range(fsdp)])  25.4 us
    pallas_call x3, Pallas kernels, attend_backward(): pl.pallas_call(functools.partial(backward_kernel, parts), grid_spec=pltpu...  25 us
  transfers between devices with their start and end apart: 41, of which 14 were waited for; matrix products, arithmetic and copies ran while one was open for 29% of the time, Pallas kernels for 11%

commit v1 on v0

--- a/solution.py
+++ b/solution.py
@@ -53,58 +53,97 @@
     return jnp.concatenate([high, (scaled - high.astype(jnp.float32)).astype(jnp.bfloat16)], axis=0)
 
 
-def forward_kernel(parts, table, *refs):
+def pair_step(table, index, masked, weights, keys, values, top_ref, total_ref, mixed_ref):
+    blocks = keys.shape[0] // BLK
+    code = table[3 + blocks + index]
+    query_block, key_block = code // blocks, code % blocks
+    key_span = pl.ds(pl.multiple_of(key_block * BLK, BLK), BLK)
+    key_rows, value_rows = keys[key_span, :], values[:, key_span]
+    spans = [
+        pl.ds(pl.multiple_of(query_block * BLK + half * HALF, HALF), HALF) for half in range(2)
+    ]
+    scores_list = [nn(key_rows, weights[:, span]) for span in spans]
+    for half in range(2):
+        span, scores = spans[half], scores_list[half]
+        top = top_ref[:, span]
+        size = jnp.abs(scores)
+        if masked:
+            key_start = table[3 + key_block] * BLK
+            query_start = table[3 + query_block] * BLK + half * HALF
+            size = jnp.where(block_mask(key_start, query_start, table[2], size.shape), size, LOW)
+        new_top = jnp.maximum(top, jnp.max(size, axis=0, keepdims=True))
+        fade = jnp.exp2(top - new_top)
+        powers = jnp.exp2(size - new_top)
+        signed = powers.astype(jnp.bfloat16) * sign_of(scores)
+        top_ref[:, span] = new_top
+        total_ref[:, span] = total_ref[:, span] * fade + jnp.sum(powers, axis=0, keepdims=True)
+        mixed_ref[:, span] = mixed_ref[:, span] * fade + nn(value_rows, signed)
+
+
+def run_pairs(table, *refs):
+    @pl.loop(0, table[0])
+    def _(index):
+        pair_step(table, index, False, *refs)
+
+    @pl.loop(table[0], table[1])
+    def _(index):
+        pair_step(table, index, True, *refs)
+
+
+def load_head_part(part, query_ref, key_ref, value_ref, weights, keys, values):
+    width = query_ref.shape[1]
+    span = slice(part * width, (part + 1) * width)
+    weights[:, span] = query_weights(query_ref[...])
+    key_rows = key_ref[...]
+    for start in range(0, width, BLK):
+        piece = key_rows[:, start : start + BLK]
+        rows = slice(part * width + start, part * width + start + BLK)
+        keys[rows, :] = jnp.concatenate([piece, piece], axis=0).T
+    values[:, span] = value_ref[...]
+
+
+def early_kernel(parts, heads, first, table, *refs):
+    packed_refs, refs = refs[:parts], refs[parts:]
+    if not first:
+        before, refs = refs[:3], refs[3:]
+    top_ref, total_ref, mixed_ref, weights, keys, values = refs
+
+    @pl.loop(0, heads)
+    def _(head):
+        def rows_of(kind):
+            return pl.ds(pl.multiple_of((kind * heads + head) * HEAD_DIM, HEAD_DIM), HEAD_DIM)
+
+        for part, ref in enumerate(packed_refs):
+            three = [ref.at[rows_of(kind), :] for kind in range(3)]
+            load_head_part(part, *three, weights, keys, values)
+        state = (top_ref.at[head], total_ref.at[head], mixed_ref.at[head])
+        if first:
+            for ref, value in zip(state, (LOW, 0.0, 0.0)):
+                ref[...] = jnp.full(ref.shape, value, jnp.float32)
+        else:
+            for ref, old in zip(state, before):
+                ref[...] = old[head]
+        run_pairs(table, weights, keys, values, *state)
+
+
+def last_kernel(parts, table, *refs):
     query_refs, key_refs, value_refs = refs[:parts], refs[parts : 2 * parts], refs[2 * parts : 3 * parts]
-    sends = refs[3 * parts : 4 * parts]
-    exact_ref, log_ref, queries, keys_t, values, keys, weights = refs[4 * parts :]
-    blocks = queries.shape[1] // BLK
-    length = table[blocks]
-    gather_columns(query_refs, queries)
-    gather_columns(key_refs, keys_t)
-    gather_columns(value_refs, values)
-    turn_rows(keys_t, keys, True)
-    full = (length + BLK - 1) // BLK
-
-    @pl.loop(0, blocks)
-    def _(place):
-        span = pl.ds(pl.multiple_of(table[place] * BLK, BLK), BLK)
-        weights[...] = query_weights(queries[:, span])
-        count = jnp.minimum(place + 1, full)
-
-        def step(number, carry, masked):
-            key_span = pl.ds(pl.multiple_of(table[number] * BLK, BLK), BLK)
-            key_rows = keys[key_span, :]
-            value_rows = values[:, key_span]
-            result = []
-            scores_list = [nn(key_rows, weights[:, h * HALF : (h + 1) * HALF]) for h in range(2)]
-            for half in range(2):
-                top, total, mixed = carry[half]
-                scores = scores_list[half]
-                size = jnp.abs(scores)
-                if masked:
-                    mask = block_mask(number * BLK, place * BLK + half * HALF, length, size.shape)
-                    size = jnp.where(mask, size, LOW)
-                new_top = jnp.maximum(top, jnp.max(size, axis=0, keepdims=True))
-                fade = jnp.exp2(top - new_top)
-                powers = jnp.exp2(size - new_top)
-                new_total = total * fade + jnp.sum(powers, axis=0, keepdims=True)
-                signed = powers.astype(jnp.bfloat16) * sign_of(scores)
-                result.append((new_top, new_total, mixed * fade + nn(value_rows, signed)))
-            return tuple(result)
-
-        begin = (
-            jnp.full((1, HALF), LOW, jnp.float32),
-            jnp.zeros((1, HALF), jnp.float32),
-            jnp.zeros((HEAD_DIM, HALF), jnp.float32),
-        )
-        carry = lax.fori_loop(0, count - 1, functools.partial(step, masked=False), (begin, begin))
-        carry = step(count - 1, carry, True)
-        exact_ref[:, span] = jnp.concatenate([c[2] / c[1] for c in carry], axis=1)
-        log_ref[:, span] = jnp.concatenate([c[0] + jnp.log2(c[1]) for c in carry], axis=1)
-
+    before, refs = refs[3 * parts : 3 * parts + 3], refs[3 * parts + 3 :]
+    sends, refs = refs[:parts], refs[parts:]
+    exact_ref, log_ref, weights, keys, values, top_ref, total_ref = refs
+    for part in range(parts):
+        load_head_part(part, query_refs[part], key_refs[part], value_refs[part], weights, keys, values)
+    top_ref[...] = before[0][0]
+    total_ref[...] = before[1][0]
+    exact_ref[...] = before[2][0]
+    run_pairs(table, weights, keys, values, top_ref, total_ref, exact_ref)
+    log_ref[...] = top_ref[...] + jnp.log2(total_ref[...])
     width = sends[0].shape[1]
     for part in range(parts):
-        sends[part][...] = exact_ref[:, part * width : (part + 1) * width].astype(jnp.bfloat16)
+        span = slice(part * width, (part + 1) * width)
+        done = exact_ref[:, span] / total_ref[:, span]
+        exact_ref[:, span] = done
+        sends[part][...] = done.astype(jnp.bfloat16)
 
 
 def backward_kernel(parts, table, *refs):
@@ -184,21 +223,78 @@
     return [pl.BlockSpec((HEAD_DIM, span), lambda i, t, row=row: (row, 0)) for _ in range(parts)]
 
 
-def attend_forward(table, head, heads, packed_list):
+def pair_tables(block_order, length, ctx_index, ctx):
+    here = block_order.shape[0] // ctx
+    order = (ctx_index - jnp.arange(ctx)) % ctx
+    places = block_order.reshape(ctx, here)[order].reshape(-1)
+    blocks = places.shape[0]
+    part = jnp.arange(blocks) // here
+    query, key = places[:, None], places[None, :]
+    seen = ((key <= query) & (key * BLK < length)).reshape(-1)
+    masked = ((key == query) | ((key + 1) * BLK > length)).reshape(-1)
+    newest = jnp.maximum(part[:, None], part[None, :]).reshape(-1)
+    phase = jnp.maximum(newest, 1)
+    pairs = jnp.arange(blocks * blocks, dtype=jnp.int32)
+    tables = []
+    for number in range(1, ctx):
+        mine = seen & (phase == number)
+        plain = mine & ~masked
+        rank = jnp.where(plain, 0, jnp.where(mine, 1, 2)) * pairs.shape[0] + pairs
+        slot = jnp.sum((rank[None, :] < rank[:, None]).astype(jnp.int32), axis=1)
+        codes = jnp.sum(jnp.where(slot[:, None] == pairs[None, :], pairs[:, None], 0), axis=0)
+        counts = jnp.stack([jnp.sum(plain.astype(jnp.int32)), jnp.sum(mine.astype(jnp.int32)), length])
+        tables.append(jnp.concatenate([counts, places, codes]).astype(jnp.int32))
+    return tables
+
+
+def attend_early(table, heads, ctx, packed_list, state):
+    parts, span = len(packed_list), packed_list[0].shape[1]
+    slots = ctx * span
+    shapes = [(heads, 1, slots), (heads, 1, slots), (heads, HEAD_DIM, slots)]
+    whole = lambda shape: pl.BlockSpec(shape, lambda i, t: (0,) * len(shape))
+    return pl.pallas_call(
+        functools.partial(early_kernel, parts, heads, state is None),
+        grid_spec=pltpu.PrefetchScalarGridSpec(
+            num_scalar_prefetch=1,
+            grid=(1,),
+            in_specs=[whole(packed_list[0].shape)] * parts
+            + ([] if state is None else [whole(shape) for shape in shapes]),
+            out_specs=[whole(shape) for shape in shapes],
+            scratch_shapes=[
+                pltpu.VMEM((128, slots), jnp.bfloat16),
+                pltpu.VMEM((slots, 128), jnp.bfloat16),
+                pltpu.VMEM((HEAD_DIM, slots), jnp.bfloat16),
+            ],
+        ),
+        out_shape=[jax.ShapeDtypeStruct(shape, jnp.float32) for shape in shapes],
+        compiler_params=pltpu.CompilerParams(vmem_limit_bytes=48 << 20),
+        cost_estimate=pl.CostEstimate(flops=20_000_000_000, bytes_accessed=4_000_000, transcendentals=0),
+        name="attend_early",
+    )(table, *packed_list, *([] if state is None else state))
+
+
+def attend_last(table, head, heads, packed_list, state):
     parts, span = len(packed_list), packed_list[0].shape[1]
     slots = parts * span
-    whole = lambda shape: pl.BlockSpec(shape, lambda i, t: (0, 0))
+    whole = lambda shape: pl.BlockSpec(shape, lambda i, t: (0,) * len(shape))
+    piece = lambda rows: pl.BlockSpec((1, rows, slots), lambda i, t: (head, 0, 0))
     return pl.pallas_call(
-        functools.partial(forward_kernel, parts),
+        functools.partial(last_kernel, parts),
         grid_spec=pltpu.PrefetchScalarGridSpec(
             num_scalar_prefetch=1,
             grid=(1,),
             in_specs=head_specs(parts, span, head)
             + head_specs(parts, span, heads + head)
-            + head_specs(parts, span, 2 * heads + head),
+            + head_specs(parts, span, 2 * heads + head)
+            + [piece(1), piece(1), piece(HEAD_DIM)],
             out_specs=[whole((HEAD_DIM, span))] * parts + [whole((HEAD_DIM, slots)), whole((1, slots))],
-            scratch_shapes=[pltpu.VMEM((HEAD_DIM, slots), jnp.bfloat16)] * 3
-            + [pltpu.VMEM((slots, 128), jnp.bfloat16), pltpu.VMEM((128, BLK), jnp.bfloat16)],
+            scratch_shapes=[
+                pltpu.VMEM((128, slots), jnp.bfloat16),
+                pltpu.VMEM((slots, 128), jnp.bfloat16),
+                pltpu.VMEM((HEAD_DIM, slots), jnp.bfloat16),
+                pltpu.VMEM((1, slots), jnp.float32),
+                pltpu.VMEM((1, slots), jnp.float32),
+            ],
         ),
         out_shape=[jax.ShapeDtypeStruct((HEAD_DIM, span), jnp.bfloat16)] * parts
         + [
@@ -206,9 +302,9 @@
             jax.ShapeDtypeStruct((1, slots), jnp.float32),
         ],
         compiler_params=pltpu.CompilerParams(vmem_limit_bytes=40 << 20),
-        cost_estimate=pl.CostEstimate(flops=20_000_000_000, bytes_accessed=4_000_000, transcendentals=0),
-        name="attend_forward",
-    )(table, *packed_list, *packed_list, *packed_list)
+        cost_estimate=pl.CostEstimate(flops=10_000_000_000, bytes_accessed=4_000_000, transcendentals=0),
+        name="attend_last",
+    )(table, *packed_list, *packed_list, *packed_list, *state)
 
 
 def attend_backward(table, head, heads, packed_list, grad_list, exact, logs):
@@ -316,38 +412,41 @@
     w_out_all = gather_rows(w_out)
     w_up_all = gather_rows(w_up)
     w_down_all = gather_rows(w_down)
-    w_own = jnp.concatenate(
-        [
-            lax.dynamic_slice_in_dim(first, kind * width + ctx_index * own, own, 1)
+
+    def columns(by):
+        device = (ctx_index + by) % ctx
+        return [
+            lax.dynamic_slice_in_dim(first, kind * width + device * own, own, 1)
             for kind in range(3)
-        ],
-        axis=1,
-    )
+        ]
+
+    w_own = jnp.concatenate(columns(0), axis=1)
     w_out_turned = turned(w_out_all.reshape(ctx, heads_here, HEAD_DIM, width), 0, ctx_index)
     w_out_turned = w_out_turned.transpose(1, 0, 2, 3).reshape(width, width)
-    w_turned = turned(first[:, : 3 * width].reshape(width, 3, ctx, heads_here, HEAD_DIM), 2, ctx_index)
-    w_turned = w_turned.transpose(0, 3, 2, 1, 4).reshape(width, 3 * width)
+    w_turned = jnp.concatenate(sum([columns(by) for by in range(ctx)], []), axis=1)
 
     here = local_rows // BLK
     places = lax.dynamic_slice_in_dim(block_order, ctx_index * here, here)
     places = (places[:, None] * BLK + jnp.arange(BLK, dtype=jnp.int32)[None]).reshape(-1)
     grad_z = out_grad * (places < length).astype(jnp.bfloat16)[:, None]
 
+    tables = pair_tables(block_order, length, ctx_index, ctx)
     normed_list, packed_list = [], []
-    tokens = tokens_in
+    tokens, state = tokens_in, None
     for part in range(ctx):
-        normed = layer_norm(tokens.astype(jnp.float32), gain_one).astype(jnp.bfloat16)
+        here_tokens, gain_here, state = lax.optimization_barrier((tokens, gain_one, state))
+        normed = layer_norm(here_tokens.astype(jnp.float32), gain_here).astype(jnp.bfloat16)
         normed_list.append(normed)
         packed_list.append(product("jn,uj->nu", w_own, normed).astype(jnp.bfloat16))
-        if part == ctx - 2:
-            tokens, w_out_turned, w_turned, grad_z = lax.optimization_barrier(
-                (tokens, w_out_turned, w_turned, grad_z)
-            )
+        if 0 < part < ctx - 1:
+            state = attend_early(tables[part - 1], heads_here, ctx, packed_list, state)
+        if part == 1:
+            tokens, grad_z, tables = lax.optimization_barrier((tokens, grad_z, tables))
         if part < ctx - 1:
             tokens = shift(tokens, ctx, 1)
     kept, mixed_parts = [], []
     for head in range(heads_here):
-        results = attend_forward(table, head, heads_here, packed_list)
+        results = attend_last(tables[-1], head, heads_here, packed_list, state)
         kept.append((results[ctx], results[ctx + 1]))
         mixed_parts += [shift(results[part], ctx, -part) for part in range(ctx)]
     mixed_t = jnp.concatenate(mixed_parts, axis=0)
@@ -397,7 +496,7 @@
         results = attend_backward(
             table, head, heads_here, packed_list, grads_by_head[head], *kept[head]
         )
-        grad_parts += [shift(results[part], ctx, -part) for part in range(ctx)]
+        grad_parts.append([shift(results[part], ctx, -part) for part in range(ctx)])
         grad_whole.append(results[ctx])
     normed_all = jnp.concatenate(normed_list, axis=0)
     grad_qkv_own = product("uj,nu->jn", normed_all, jnp.concatenate(grad_whole, axis=0))
@@ -407,7 +506,15 @@
     grad_qkv = grad_qkv.reshape(ctx, rows_here, heads_here, 3, HEAD_DIM)
     grad_w_qkv = grad_qkv.transpose(1, 3, 0, 2, 4).reshape(rows_here, 3 * width).astype(jnp.float32)
 
-    grad_packed_t = jnp.concatenate(grad_parts, axis=0)
+    grad_packed_t = jnp.concatenate(
+        [
+            grad_parts[head][part][kind * HEAD_DIM : (kind + 1) * HEAD_DIM]
+            for part in range(ctx)
+            for kind in range(3)
+            for head in range(heads_here)
+        ],
+        axis=0,
+    )
     grad_normed_one = product("nu,jn->uj", grad_packed_t, w_turned)
     norm_one_back = jax.vjp(lambda v: layer_norm(v, gain_one), tokens_f)[1]
     grad_tokens = (grad_middle + norm_one_back(grad_normed_one)[0]).astype(jnp.bfloat16)

time: 613 us -> 613 us (level)
  the two profiles are of different devices: /device:TPU:0 before, /device:TPU:1 now
where the time goes in v1:
time: 613 us; the launch traced here: 603 us
  Pallas kernels  208 us (34%)
  local copies, waits for them, and re-layouts  111 us (18%)
  waiting for transfers between devices  94.4 us (15%)
  matrix products  85.6 us (14%)
  other arithmetic  41.5 us (7%)
  starting transfers between devices  34.3 us (6%)
  between operations  16.2 us (3%)
  blocking collectives  11.8 us (2%)
    pallas_call x3, Pallas kernels, attend_backward(): pl.pallas_call(functools.partial(backward_kernel, parts), grid_spec=pltpu...  123 us
    ppermute x30, waiting for transfers between devices, shift(): return lax.ppermute(array, 'ctx', [(i, (i + by) % ctx) for i in range(ctx)])  92.4 us
    unnamed x181, local copies, waits for them, and re-layouts  90.2 us
    dot_general x15, matrix products, product(): return jnp.einsum(equation, left, right, preferred_element_type=jnp.float32)  85.6 us
    pallas_call x2, Pallas kernels, attend_early(): pl.pallas_call(functools.partial(early_kernel, parts, heads, state is Non...  50.7 us
    pallas_call x3, Pallas kernels, attend_last(): pl.pallas_call(functools.partial(last_kernel, parts), grid_spec=pltpu.Pre...  34.8 us
    ppermute x30, starting transfers between devices, shift(): return lax.ppermute(array, 'ctx', [(i, (i + by) % ctx) for i in range(ctx)])  30.9 us
  transfers between devices with their start and end apart: 41, of which 8 were waited for; matrix products, arithmetic and copies ran while one was open for 33% of the time, Pallas kernels for 35%

profile of v1, /device:TPU:1, one launch (start us, length us, event | category | flops | bytes accessed | tf_op | source)
XLA Modules:
  0.0 602.8 jit_solution(12883762801742848739)
XLA Ops:
  28.4 22.1 %collective-permute-done = bf16[1024,768]{0,1:T(8,128)(2,1)S(1)} collective-permute-done((bf16[1024,768]{0,1:T(8,128)(2,1)S(1)}, bf16[1024,768]{0,1:T(8,128)(2,1)S(1)}, u32[]{:S(2)}, u32[]{:S(2)}) %collective-permute-start) | collective-permute-done | bytes 1572896 | tf_op jit(solution)/shard_map/ppermute | solution.py:361
  57.5 29.6 %collective-permute-done.1 = bf16[1024,768]{0,1:T(8,128)(2,1)} collective-permute-done((bf16[1024,768]{0,1:T(8,128)(2,1)S(1)}, bf16[1024,768]{0,1:T(8,128)(2,1)}, u32[]{:S(2)}, u32[]{:S(2)}) %collective-permute-start.1) | collective-permute-done | bytes 1572896 | tf_op jit(solution)/shard_map/ppermute | solution.py:361
  92.6 3.9 constant_dynamic-slice_fusion
  99.0 22.5 %attend_early.2 = (f32[3,1,4096]{2,1,0:T(1,128)S(1)}, f32[3,1,4096]{2,1,0:T(1,128)S(1)}, f32[3,64,4096]{2,1,0:T(8,128)S(1)}) custom-call(s32[75]{0:T(128)S(1)} %concatenate.42.table, bf16[576,1024]{1,0:T(8,128)(2,1)S(1)} %convolution_convert_fusion.7.refs_0_.refs_4_.refs_8_, bf16[576,1024]{1,0:T(8,128)(2,1)S(1)} %convolution_convert_fusion.6.refs_1_.refs_5_.refs_9_), custom_call_target="tpu_custom_call" | custom-call | flops 20000000000 | bytes 4000000 | tf_op jit(solution)/shard_map/attend_early/pallas_call | solution.py:255
  121.6 2.9 convert_reduce_fusion.2
  129.6 28.1 %attend_early.3 = (f32[3,1,4096]{2,1,0:T(1,128)S(1)}, f32[3,1,4096]{2,1,0:T(1,128)S(1)}, f32[3,64,4096]{2,1,0:T(8,128)}) custom-call(s32[75]{0:T(128)S(1)} %concatenate.43.table, bf16[576,1024]{1,0:T(8,128)(2,1)S(1)} %convolution_convert_fusion.7.refs_0_.refs_4_.refs_8_, bf16[576,1024]{1,0:T(8,128)(2,1)S(1)} %convolution_convert_fusion.6.refs_1_.refs_5_.refs_9_, ...), custom_call_target="tpu_custom_call" | custom-call | flops 20000000000 | bytes 4000000 | tf_op jit(solution)/shard_map/attend_early/pallas_call | solution.py:255
  165.7 11.5 %attend_last.3 = (bf16[64,1024]{1,0:T(8,128)(2,1)S(1)}, bf16[64,1024]{1,0:T(8,128)(2,1)S(1)}, bf16[64,1024]{1,0:T(8,128)(2,1)S(1)}, bf16[64,1024]{1,0:T(8,128)(2...) custom-call(s32[75]{0:T(128)S(1)} %concatenate.44.table, ...), custom_call_target="tpu_custom_call" | custom-call | flops 10000000000 | bytes 4000000 | tf_op jit(solution)/shard_map/attend_last/pallas_call | solution.py:281
  178.2 3.3 collective-permute-start.3
  181.5 11.9 %attend_last.5 = (bf16[64,1024]{1,0:T(8,128)(2,1)S(1)}, bf16[64,1024]{1,0:T(8,128)(2,1)S(1)}, bf16[64,1024]{1,0:T(8,128)(2,1)S(1)}, bf16[64,1024]{1,0:T(8,128)(2...) custom-call(s32[75]{0:T(128)S(1)} %concatenate.44.table, ...), custom_call_target="tpu_custom_call" | custom-call | flops 10000000000 | bytes 4000000 | tf_op jit(solution)/shard_map/attend_last/pallas_call | solution.py:281
  194.4 11.5 %attend_last.4 = (bf16[64,1024]{1,0:T(8,128)(2,1)S(1)}, bf16[64,1024]{1,0:T(8,128)(2,1)S(1)}, bf16[64,1024]{1,0:T(8,128)(2,1)S(1)}, bf16[64,1024]{1,0:T(8,128)(2...) custom-call(s32[75]{0:T(128)S(1)} %concatenate.44.table, ...), custom_call_target="tpu_custom_call" | custom-call | flops 10000000000 | bytes 4000000 | tf_op jit(solution)/shard_map/attend_last/pallas_call | solution.py:281
  211.3 6.8 %concatenate.53 = bf16[768,2304]{1,0:T(8,128)(2,1)} concatenate(bf16[768,192]{1,0:T(8,128)(2,1)} %copy-done.46, bf16[768,192]{1,0:T(8,128)(2,1)} %copy-done.45, bf16[768,192]{1,0:T(8,128)(2,1)} %copy-done.44, bf16[768,192]{1,0:T(8,128)(2,1)} %get-tuple-element.207, bf16[768,192]{1,0:T(8,128)(2,1)} %get-tuple-element.206, bf16[768,192]{1,0:T(8,128)(2,1)} %get-tuple-element.205, ...), dimensions={1} | concatenate | bytes 7077888 | tf_op jit(solution)/shard_map/concatenate | solution.py:426
  218.9 3.2 collective-permute-start.6
  225.9 2.7 collective-permute-done.7
  234.2 3.8 fusion.79
  240.1 8.3 %fusion.75 = f32[1024,3072]{1,0:T(8,128)S(1)} fusion(bf16[768,3072]{1,0:T(8,128)(2,1)} %all-gather.10.cloned.1.call-done, f32[1024,768]{0,1:T(8,128)} %copy-done.33, f32[768]{0:T(1024)S(1)} %get-tuple-element.178, f32[1024]{0:T(1024)S(1)} %fusion.64, f32[1024]{0:T(1024)S(1)} %broadcast_multiply_fusion.1), kind=kOutput, calls=%fused_computation.244 | convolution fusion | flops 4834983936 | bytes 20458496 | tf_op jit(solution)/shard_map/uj,jn->un/dot_general | solution.py:355
  248.4 4.5 copy-done.39
  252.9 10.0 %convolution_convert_fusion = bf16[3072,768]{1,0:T(8,128)(2,1)} fusion(bf16[1024,768]{0,1:T(8,128)(2,1)S(1)} %copy-done.37, f32[1024,3072]{1,0:T(8,128)S(1)} %fusion.75), kind=kOutput, calls=%fused_computation.20 | convolution fusion | flops 4862509056 | bytes 18874368 | tf_op jit(solution)/shard_map/un,uj->nj/dot_general | solution.py:355
  263.3 14.6 %fusion.6 = bf16[1024,3072]{1,0:T(8,128)(2,1)S(1)} fusion(f32[1024,3072]{1,0:T(8,128)} %copy-done.39, bf16[1024,768]{0,1:T(8,128)(2,1)S(1)} %copy-done.37, bf16[3072,768]{1,0:T(8,128)(2,1)} %all-gather.12.cloned.1.call-done), kind=kOutput, calls=%fused_computation.9 | convolution fusion | flops 4894752768 | bytes 25165824 | tf_op jit(solution)/shard_map/uj,nj->un/dot_general | solution.py:355
  277.9 8.4 %multiply_reduce_fusion = (f32[1024]{0:T(1024)S(1)}, f32[1024,768]{0,1:T(8,128)S(1)}) fusion(f32[1024,768]{0,1:T(8,128)} %copy-done.33, f32[768]{0:T(1024)S(1)} %get-tuple-element.178, f32[1024]{0:T(1024)S(1)} %broadcast_multiply_fusion.1, bf16[1024,3072]{1,0:T(8,128)(2,1)S(1)} %fusion.6, bf16[768,3072]{1,0:T(8,128)(2,1)} %all-gather.10.cloned.1.call-done), kind=kOutput, calls=%fused_computation.67 | convolution fusion | flops 4834982912 | bytes 17312768 | tf_op jit(solution)/shard_map/un,jn->uj/dot_general | solution.py:355
  296.0 5.4 convolution_convert_fusion.1
  301.4 2.9 pad_maximum_fusion
  304.6 12.1 %fusion.47 = bf16[1,1024,768]{1,2,0:T(8,128)(2,1)} fusion(f32[1024,768]{0,1:T(8,128)} %copy-done.33, bf16[3072,768]{1,0:T(8,128)(2,1)} %all-gather.12.cloned.1.call-done, f32[1024,3072]{1,0:T(8,128)} %copy-done.39), kind=kOutput, calls=%fused_computation.84 | convolution fusion | flops 4861722624 | bytes 22020096 | tf_op jit(solution)/shard_map/un,nj->uj/dot_general | solution.py:355
  332.5 41.1 %attend_backward.3 = (bf16[192,1024]{1,0:T(8,128)(2,1)S(1)}, bf16[192,1024]{1,0:T(8,128)(2,1)}, bf16[192,1024]{1,0:T(8,128)(2,1)S(1)}, bf16[192,1024]{1,0:T(8,128)(2,1)S(1)}, bf16[192,4096]{1,0:T(8,128)(2,1)S(1)}) custom-call(s32[9]{0:T(128)S(1)} %pad_add_fusion.table, bf16[576,1024]{1,0:T(8,128)(2,1)S(1)} %copy-done.7, bf16[576,1024]{1,0:T(8,128)(2,1)S(1)} %copy-done.10, ...), custom_call_target="tpu_custom_call" | custom-call | flops 40000000000 | bytes 6000000 | tf_op jit(solution)/shard_map/attend_backward/pallas_call | solution.py:315
  375.5 3.1 collective-permute-start.21
  378.6 41.1 %attend_backward.4 = (bf16[192,1024]{1,0:T(8,128)(2,1)S(1)}, bf16[192,1024]{1,0:T(8,128)(2,1)}, bf16[192,1024]{1,0:T(8,128)(2,1)S(1)}, bf16[192,1024]{1,0:T(8,128)(2,1)S(1)}, bf16[192,4096]{1,0:T(8,128)(2,1)S(1)}) custom-call(s32[9]{0:T(128)S(1)} %pad_add_fusion.table, bf16[576,1024]{1,0:T(8,128)(2,1)S(1)} %copy-done.7, bf16[576,1024]{1,0:T(8,128)(2,1)S(1)} %copy-done.10, ...), custom_call_target="tpu_custom_call" | custom-call | flops 40000000000 | bytes 6000000 | tf_op jit(solution)/shard_map/attend_backward/pallas_call | solution.py:315
  421.9 2.9 collective-permute-start.22
  434.0 40.7 %attend_backward.5 = (bf16[192,1024]{1,0:T(8,128)(2,1)S(1)}, bf16[192,1024]{1,0:T(8,128)(2,1)S(1)}, bf16[192,1024]{1,0:T(8,128)(2,1)S(1)}, bf16[192,1024]{1,0:T(8,128)(2,1)S(1)}, bf16[192,4096]{1,0:T(8,128)(2,1)S(1)}) custom-call(s32[9]{0:T(128)S(1)} %pad_add_fusion.table, bf16[576,1024]{1,0:T(8,128)(2,1)S(1)} %copy-done.8, ...), custom_call_target="tpu_custom_call" | custom-call | flops 40000000000 | bytes 6000000 | tf_op jit(solution)/shard_map/attend_backward/pallas_call | solution.py:315
  480.7 9.3 %fusion.7 = f32[768,576]{1,0:T(8,128)S(1)} fusion(bf16[1024,768]{0,1:T(8,128)(2,1)} %copy-done.51, bf16[1024,768]{0,1:T(8,128)(2,1)} %copy-done.50, bf16[1024,768]{0,1:T(8,128)(2,1)} %copy-done.49, bf16[1024,768]{0,1:T(8,128)(2,1)} %copy-done.48, bf16[192,4096]{1,0:T(8,128)(2,1)} %copy-done.27, bf16[192,4096]{1,0:T(8,128)(2,1)} %copy-done.26, ...), kind=kOutput, calls=%fused_computation.11 | convolution fusion | flops 3663200256 | bytes 12779520 | tf_op jit(solution)/shard_map/uj,nu->jn/dot_general | solution.py:355
  496.1 22.1 %collective-permute-done.23 = bf16[192,1024]{1,0:T(8,128)(2,1)S(1)} collective-permute-done((bf16[192,1024]{1,0:T(8,128)(2,1)S(1)}, bf16[192,1024]{1,0:T(8,128)(2,1)S(1)}, u32[]{:S(2)}, u32[]{:S(2)}) %collective-permute-start.23) | collective-permute-done | bytes 393248 | tf_op jit(solution)/shard_map/ppermute | solution.py:361
  531.1 13.2 %collective-permute-done.26 = bf16[192,1024]{1,0:T(8,128)(2,1)S(1)} collective-permute-done((bf16[192,1024]{1,0:T(8,128)(2,1)S(1)}, bf16[192,1024]{1,0:T(8,128)(2,1)S(1)}, u32[]{:S(2)}, u32[]{:S(2)}) %collective-permute-start.26) | collective-permute-done | bytes 393248 | tf_op jit(solution)/shard_map/ppermute | solution.py:361
  561.2 5.9 fusion.43
  574.8 11.8 %all-gather = bf16[384,576]{1,0:T(8,128)(2,1)S(1)} all-gather(bf16[96,576]{1,0:T(8,128)(2,1)S(1)} %fusion.57), channel_id=2, replica_groups=mesh['ctx'=4,'fsdp'=8] {'ctx'}, dimensions={0}, use_global_device_ids=true | all-gather | bytes 552960 | tf_op jit(solution)/shard_map/all_gather | solution.py:504
  (351 shorter events, 165.3 us)
Async XLA Ops:
  7.2 47.5 %all-gather.8.cloned.1.call-start = ((), (), s32[]{:S(2)}) async-start(), calls=%async_computation.3 | async-start | bytes 1327104 | tf_op jit(solution)/shard_map/all_gather | solution.py:371
  7.9 79.2 %all-gather.6.cloned.1.call-start = ((), (), s32[]{:S(2)}) async-start(), calls=%async_computation.2 | async-start | bytes 4202496 | tf_op jit(solution)/shard_map/all_gather | solution.py:371
  10.6 229.5 %all-gather.10.cloned.1.call-start = ((), (), s32[]{:S(2)}) async-start(), calls=%async_computation.4 | async-start | bytes 5308416 | tf_op jit(solution)/shard_map/all_gather | solution.py:371
  11.4 251.9 %all-gather.12.cloned.1.call-start = ((), (), s32[]{:S(2)}) async-start(), calls=%async_computation.5 | async-start | bytes 5308416 | tf_op jit(solution)/shard_map/all_gather | solution.py:371
  12.2 38.3 %collective-permute-start = (bf16[1024,768]{0,1:T(8,128)(2,1)S(1)}, bf16[1024,768]{0,1:T(8,128)(2,1)S(1)}, u32[]{:S(2)}, u32[]{:S(2)}) collective-permute-start(bf16[1024,768]{0,1:T(8,128)(2,1)S(1)} %bitcast.85), channel_id=1, source_target_pairs={{0,8},{8,16},{16,24},{24,0},{1,9},{9,17},{17,25},{25,1},{2,10},{10... | collective-permute-start | bytes 4718600 | tf_op jit(solution)/shard_map/ppermute | solution.py:361
  50.5 36.6 %collective-permute-start.1 = (bf16[1024,768]{0,1:T(8,128)(2,1)S(1)}, bf16[1024,768]{0,1:T(8,128)(2,1)}, u32[]{:S(2)}, u32[]{:S(2)}) collective-permute-start(bf16[1024,768]{0,1:T(8,128)(2,1)S(1)} %collective-permute-done), channel_id=1, source_target_pairs={{0,8},{8,16},{16,24},{24,0},{1,9},{9,17},{17,25},{25,1},{2,10},{10... | collective-permute-start | bytes 4718600 | tf_op jit(solution)/shard_map/ppermute | solution.py:361
  50.5 371.1 %reduce-scatter.5.cloned.1.call-start = ((), (), s32[]{:S(2)}) async-start(), calls=%async_computation.7 | async-start | bytes 5308416 | tf_op jit(solution)/shard_map/reduce_scatter | solution.py:375
  87.1 70.7 %collective-permute-start.2 = (bf16[1024,768]{0,1:T(8,128)(2,1)}, bf16[1024,768]{0,1:T(8,128)(2,1)}, u32[]{:S(2)}, u32[]{:S(2)}) collective-permute-start(bf16[1024,768]{0,1:T(8,128)(2,1)} %collective-permute-done.1), channel_id=1, source_target_pairs={{0,8},{8,16},{16,24},{24,0},{1,9},{9,17},{17,25},{25,1},{2,10},{10... | collective-permute-start | bytes 4718600 | tf_op jit(solution)/shard_map/ppermute | solution.py:361
  178.2 39.9 %collective-permute-start.3 = (bf16[64,1024]{1,0:T(8,128)(2,1)S(1)}, bf16[64,1024]{1,0:T(8,128)(2,1)S(1)}, u32[]{:S(2)}, u32[]{:S(2)}) collective-permute-start(bf16[64,1024]{1,0:T(8,128)(2,1)S(1)} %get-tuple-element.93), channel_id=1, source_target_pairs={{0,24},{8,0},{16,8},{24,16},{1,25},{9,1},{17,9},{25,17},{2,26},{10... | collective-permute-start | bytes 393224 | tf_op jit(solution)/shard_map/ppermute | solution.py:361
  206.8 26.0 %collective-permute-start.10 = (bf16[64,1024]{1,0:T(8,128)(2,1)S(1)}, bf16[64,1024]{1,0:T(8,128)(2,1)S(1)}, u32[]{:S(2)}, u32[]{:S(2)}) collective-permute-start(bf16[64,1024]{1,0:T(8,128)(2,1)S(1)} %get-tuple-element.102), channel_id=1, source_target_pairs={{0,16},{8,24},{16,0},{24,8},{1,17},{9,25},{17,1},{25,9},{2,18},{10... | collective-permute-start | bytes 393224 | tf_op jit(solution)/shard_map/ppermute | solution.py:361
  206.8 26.7 %collective-permute-start.11 = (bf16[64,1024]{1,0:T(8,128)(2,1)S(1)}, bf16[64,1024]{1,0:T(8,128)(2,1)S(1)}, u32[]{:S(2)}, u32[]{:S(2)}) collective-permute-start(bf16[64,1024]{1,0:T(8,128)(2,1)S(1)} %get-tuple-element.103), channel_id=1, source_target_pairs={{0,8},{8,16},{16,24},{24,0},{1,9},{9,17},{17,25},{25,1},{2,10},{10... | collective-permute-start | bytes 393224 | tf_op jit(solution)/shard_map/ppermute | solution.py:361
  263.0 158.6 %reduce-scatter.3.cloned.1.call-start = ((), (), s32[]{:S(2)}) async-start(), calls=%async_computation.6 | async-start | bytes 6635520 | tf_op jit(solution)/shard_map/reduce_scatter | solution.py:375
  293.5 28.7 %collective-permute-start.14 = (bf16[64,1024]{1,0:T(8,128)(2,1)S(1)}, bf16[64,1024]{1,0:T(8,128)(2,1)S(1)}, u32[]{:S(2)}, u32[]{:S(2)}) collective-permute-start(bf16[64,1024]{1,0:T(8,128)(2,1)S(1)} %get-tuple-element.219), channel_id=1, source_target_pairs={{0,24},{8,0},{16,8},{24,16},{1,25},{9,1},{17,9},{25,17},{2,26},{10... | collective-permute-start | bytes 393224 | tf_op jit(solution)/shard_map/ppermute | solution.py:361
  294.7 28.4 %collective-permute-start.13 = (bf16[64,1024]{1,0:T(8,128)(2,1)S(1)}, bf16[64,1024]{1,0:T(8,128)(2,1)S(1)}, u32[]{:S(2)}, u32[]{:S(2)}) collective-permute-start(bf16[64,1024]{1,0:T(8,128)(2,1)S(1)} %get-tuple-element.220), channel_id=1, source_target_pairs={{0,16},{8,24},{16,0},{24,8},{1,17},{9,25},{17,1},{25,9},{2,18},{10... | collective-permute-start | bytes 393224 | tf_op jit(solution)/shard_map/ppermute | solution.py:361
  294.7 29.4 %collective-permute-start.12 = (bf16[64,1024]{1,0:T(8,128)(2,1)S(1)}, bf16[64,1024]{1,0:T(8,128)(2,1)S(1)}, u32[]{:S(2)}, u32[]{:S(2)}) collective-permute-start(bf16[64,1024]{1,0:T(8,128)(2,1)S(1)} %get-tuple-element.221), channel_id=1, source_target_pairs={{0,8},{8,16},{16,24},{24,0},{1,9},{9,17},{17,25},{25,1},{2,10},{10... | collective-permute-start | bytes 393224 | tf_op jit(solution)/shard_map/ppermute | solution.py:361
  304.3 285.5 %all-reduce.4.cloned.1.call-start = ((), (), s32[]{:S(2)}) async-start(), calls=%async_computation.8 | async-start | bytes 2654208 | tf_op jit(solution)/shard_map/psum | solution.py:495
  319.2 102.4 %collective-permute-start.20 = (bf16[64,1024]{1,0:T(8,128)(2,1)}, bf16[64,1024]{1,0:T(8,128)(2,1)S(1)}, u32[]{:S(2)}, u32[]{:S(2)}) collective-permute-start(bf16[64,1024]{1,0:T(8,128)(2,1)} %get-tuple-element.211), channel_id=1, source_target_pairs={{0,24},{8,0},{16,8},{24,16},{1,25},{9,1},{17,9},{25,17},{2,26},{10... | collective-permute-start | bytes 393224 | tf_op jit(solution)/shard_map/ppermute | solution.py:361
  321.6 100.3 %collective-permute-start.19 = (bf16[64,1024]{1,0:T(8,128)(2,1)S(1)}, bf16[64,1024]{1,0:T(8,128)(2,1)S(1)}, u32[]{:S(2)}, u32[]{:S(2)}) collective-permute-start(bf16[64,1024]{1,0:T(8,128)(2,1)S(1)} %get-tuple-element.212), channel_id=1, source_target_pairs={{0,16},{8,24},{16,0},{24,8},{1,17},{9,25},{17,1},{25,9},{2,18},{10... | collective-permute-start | bytes 393224 | tf_op jit(solution)/shard_map/ppermute | solution.py:361
  322.2 53.2 %collective-permute-start.17 = (bf16[64,1024]{1,0:T(8,128)(2,1)S(1)}, bf16[64,1024]{1,0:T(8,128)(2,1)S(1)}, u32[]{:S(2)}, u32[]{:S(2)}) collective-permute-start(bf16[64,1024]{1,0:T(8,128)(2,1)S(1)} %get-tuple-element.215), channel_id=1, source_target_pairs={{0,24},{8,0},{16,8},{24,16},{1,25},{9,1},{17,9},{25,17},{2,26},{10... | collective-permute-start | bytes 393224 | tf_op jit(solution)/shard_map/ppermute | solution.py:361
  323.1 52.4 %collective-permute-start.16 = (bf16[64,1024]{1,0:T(8,128)(2,1)S(1)}, bf16[64,1024]{1,0:T(8,128)(2,1)S(1)}, u32[]{:S(2)}, u32[]{:S(2)}) collective-permute-start(bf16[64,1024]{1,0:T(8,128)(2,1)S(1)} %get-tuple-element.216), channel_id=1, source_target_pairs={{0,16},{8,24},{16,0},{24,8},{1,17},{9,25},{17,1},{25,9},{2,18},{10... | collective-permute-start | bytes 393224 | tf_op jit(solution)/shard_map/ppermute | solution.py:361
  324.1 54.6 %collective-permute-start.15 = (bf16[64,1024]{1,0:T(8,128)(2,1)S(1)}, bf16[64,1024]{1,0:T(8,128)(2,1)S(1)}, u32[]{:S(2)}, u32[]{:S(2)}) collective-permute-start(bf16[64,1024]{1,0:T(8,128)(2,1)S(1)} %get-tuple-element.217), channel_id=1, source_target_pairs={{0,8},{8,16},{16,24},{24,0},{1,9},{9,17},{17,25},{25,1},{2,10},{10... | collective-permute-start | bytes 393224 | tf_op jit(solution)/shard_map/ppermute | solution.py:361
  375.3 49.5 %collective-permute-start.18 = (bf16[64,1024]{1,0:T(8,128)(2,1)S(1)}, bf16[64,1024]{1,0:T(8,128)(2,1)S(1)}, u32[]{:S(2)}, u32[]{:S(2)}) collective-permute-start(bf16[64,1024]{1,0:T(8,128)(2,1)S(1)} %get-tuple-element.213), channel_id=1, source_target_pairs={{0,8},{8,16},{16,24},{24,0},{1,9},{9,17},{17,25},{25,1},{2,10},{10... | collective-permute-start | bytes 393224 | tf_op jit(solution)/shard_map/ppermute | solution.py:361
  375.5 115.9 %collective-permute-start.21 = (bf16[192,1024]{1,0:T(8,128)(2,1)}, bf16[192,1024]{1,0:T(8,128)(2,1)}, u32[]{:S(2)}, u32[]{:S(2)}) collective-permute-start(bf16[192,1024]{1,0:T(8,128)(2,1)} %get-tuple-element.116), channel_id=1, source_target_pairs={{0,24},{8,0},{16,8},{24,16},{1,25},{9,1},{17,9},{25,17},{2,26},{10... | collective-permute-start | bytes 1179656 | tf_op jit(solution)/shard_map/ppermute | solution.py:361
  378.6 147.9 %collective-permute-start.24 = (bf16[192,1024]{1,0:T(8,128)(2,1)S(1)}, bf16[192,1024]{1,0:T(8,128)(2,1)}, u32[]{:S(2)}, u32[]{:S(2)}) collective-permute-start(bf16[192,1024]{1,0:T(8,128)(2,1)S(1)} %get-tuple-element.119), channel_id=1, source_target_pairs={{0,16},{8,24},{16,0},{24,8},{1,17},{9,25},{17,1},{25,9},{2,18},{10... | collective-permute-start | bytes 1179656 | tf_op jit(solution)/shard_map/ppermute | solution.py:361
  421.6 130.9 %collective-permute-start.27 = (bf16[192,1024]{1,0:T(8,128)(2,1)S(1)}, bf16[192,1024]{1,0:T(8,128)(2,1)}, u32[]{:S(2)}, u32[]{:S(2)}) collective-permute-start(bf16[192,1024]{1,0:T(8,128)(2,1)S(1)} %get-tuple-element.122), channel_id=1, source_target_pairs={{0,8},{8,16},{16,24},{24,0},{1,9},{9,17},{17,25},{25,1},{2,10},{10... | collective-permute-start | bytes 1179656 | tf_op jit(solution)/shard_map/ppermute | solution.py:361
  421.9 71.9 %collective-permute-start.22 = (bf16[192,1024]{1,0:T(8,128)(2,1)}, bf16[192,1024]{1,0:T(8,128)(2,1)}, u32[]{:S(2)}, u32[]{:S(2)}) collective-permute-start(bf16[192,1024]{1,0:T(8,128)(2,1)} %get-tuple-element.117), channel_id=1, source_target_pairs={{0,24},{8,0},{16,8},{24,16},{1,25},{9,1},{17,9},{25,17},{2,26},{10... | collective-permute-start | bytes 1179656 | tf_op jit(solution)/shard_map/ppermute | solution.py:361
  425.5 104.0 %collective-permute-start.25 = (bf16[192,1024]{1,0:T(8,128)(2,1)S(1)}, bf16[192,1024]{1,0:T(8,128)(2,1)}, u32[]{:S(2)}, u32[]{:S(2)}) collective-permute-start(bf16[192,1024]{1,0:T(8,128)(2,1)S(1)} %get-tuple-element.120), channel_id=1, source_target_pairs={{0,16},{8,24},{16,0},{24,8},{1,17},{9,25},{17,1},{25,9},{2,18},{10... | collective-permute-start | bytes 1179656 | tf_op jit(solution)/shard_map/ppermute | solution.py:361
  491.4 26.8 %collective-permute-start.23 = (bf16[192,1024]{1,0:T(8,128)(2,1)S(1)}, bf16[192,1024]{1,0:T(8,128)(2,1)S(1)}, u32[]{:S(2)}, u32[]{:S(2)}) collective-permute-start(bf16[192,1024]{1,0:T(8,128)(2,1)S(1)} %copy-done.3), channel_id=1, source_target_pairs={{0,24},{8,0},{16,8},{24,16},{1,25},{9,1},{17,9},{25,17},{2,26},{10... | collective-permute-start | bytes 1179656 | tf_op jit(solution)/shard_map/ppermute | solution.py:361
  493.9 60.2 %collective-permute-start.28 = (bf16[192,1024]{1,0:T(8,128)(2,1)S(1)}, bf16[192,1024]{1,0:T(8,128)(2,1)S(1)}, u32[]{:S(2)}, u32[]{:S(2)}) collective-permute-start(bf16[192,1024]{1,0:T(8,128)(2,1)S(1)} %get-tuple-element.123), channel_id=1, source_target_pairs={{0,8},{8,16},{16,24},{24,0},{1,9},{9,17},{17,25},{25,1},{2,10},{10... | collective-permute-start | bytes 1179656 | tf_op jit(solution)/shard_map/ppermute | solution.py:361
  518.2 26.2 %collective-permute-start.26 = (bf16[192,1024]{1,0:T(8,128)(2,1)S(1)}, bf16[192,1024]{1,0:T(8,128)(2,1)S(1)}, u32[]{:S(2)}, u32[]{:S(2)}) collective-permute-start(bf16[192,1024]{1,0:T(8,128)(2,1)S(1)} %copy-done.1), channel_id=1, source_target_pairs={{0,16},{8,24},{16,0},{24,8},{1,17},{9,25},{17,1},{25,9},{2,18},{10... | collective-permute-start | bytes 1179656 | tf_op jit(solution)/shard_map/ppermute | solution.py:361
  526.5 28.3 %collective-permute-start.29 = (bf16[192,1024]{1,0:T(8,128)(2,1)S(1)}, bf16[192,1024]{1,0:T(8,128)(2,1)S(1)}, u32[]{:S(2)}, u32[]{:S(2)}) collective-permute-start(bf16[192,1024]{1,0:T(8,128)(2,1)S(1)} %get-tuple-element.124), channel_id=1, source_target_pairs={{0,8},{8,16},{16,24},{24,0},{1,9},{9,17},{17,25},{25,1},{2,10},{10... | collective-permute-start | bytes 1179656 | tf_op jit(solution)/shard_map/ppermute | solution.py:361
  529.6 38.5 %collective-permute-start.30 = (bf16[4,96,576]{2,1,0:T(8,128)(2,1)S(1)}, bf16[4,96,576]{2,1,0:T(8,128)(2,1)S(1)}, u32[]{:S(2)}, u32[]{:S(2)}) collective-permute-start(bf16[4,96,576]{2,1,0:T(8,128)(2,1)S(1)} %fusion.52), channel_id=1, source_target_pairs={{0,1},{1,0},{2,3},{3,2},{4,5},{5,4},{6,7},{7,6},{8,9},{9,8},{10,11... | collective-permute-start | bytes 1327112 | tf_op jit(solution)/shard_map/ppermute | solution.py:386
  (72 other events, 1108.8 us)
Sparse Core Ops, SparseCore 0:
  9.9 26.3 all-gather.7
  38.8 35.0 all-gather.5
  75.7 38.7 all-gather.9
  116.3 38.8 all-gather.11
  263.1 53.0 reduce-scatter.4
  319.6 59.6 reduce-scatter.2
  480.8 75.1 all-reduce.3

commit v2 on v1

--- a/solution.py
+++ b/solution.py
@@ -111,7 +111,7 @@
     @pl.loop(0, heads)
     def _(head):
         def rows_of(kind):
-            return pl.ds(pl.multiple_of((kind * heads + head) * HEAD_DIM, HEAD_DIM), HEAD_DIM)
+            return pl.ds(pl.multiple_of((3 * head + kind) * HEAD_DIM, HEAD_DIM), HEAD_DIM)
 
         for part, ref in enumerate(packed_refs):
             three = [ref.at[rows_of(kind), :] for kind in range(3)]
@@ -273,7 +273,7 @@
     )(table, *packed_list, *([] if state is None else state))
 
 
-def attend_last(table, head, heads, packed_list, state):
+def attend_last(table, head, packed_list, state):
     parts, span = len(packed_list), packed_list[0].shape[1]
     slots = parts * span
     whole = lambda shape: pl.BlockSpec(shape, lambda i, t: (0,) * len(shape))
@@ -283,9 +283,9 @@
         grid_spec=pltpu.PrefetchScalarGridSpec(
             num_scalar_prefetch=1,
             grid=(1,),
-            in_specs=head_specs(parts, span, head)
-            + head_specs(parts, span, heads + head)
-            + head_specs(parts, span, 2 * heads + head)
+            in_specs=head_specs(parts, span, 3 * head)
+            + head_specs(parts, span, 3 * head + 1)
+            + head_specs(parts, span, 3 * head + 2)
             + [piece(1), piece(1), piece(HEAD_DIM)],
             out_specs=[whole((HEAD_DIM, span))] * parts + [whole((HEAD_DIM, slots)), whole((1, slots))],
             scratch_shapes=[
@@ -307,7 +307,7 @@
     )(table, *packed_list, *packed_list, *packed_list, *state)
 
 
-def attend_backward(table, head, heads, packed_list, grad_list, exact, logs):
+def attend_backward(table, head, packed_list, grad_list, exact, logs):
     parts, span = len(packed_list), packed_list[0].shape[1]
     slots = parts * span
     whole = lambda shape: pl.BlockSpec(shape, lambda i, t: (0, 0))
@@ -317,9 +317,9 @@
         grid_spec=pltpu.PrefetchScalarGridSpec(
             num_scalar_prefetch=1,
             grid=(1,),
-            in_specs=head_specs(parts, span, head)
-            + head_specs(parts, span, heads + head)
-            + head_specs(parts, span, 2 * heads + head)
+            in_specs=head_specs(parts, span, 3 * head)
+            + head_specs(parts, span, 3 * head + 1)
+            + head_specs(parts, span, 3 * head + 2)
             + [whole((HEAD_DIM, span))] * parts
             + [whole((HEAD_DIM, slots)), whole((1, slots))],
             out_specs=[whole((three, span))] * parts + [whole((three, slots))],
@@ -406,24 +406,17 @@
 
     gains = jnp.stack([gain_attn, gain_mlp], axis=1)
     gains = jnp.pad(gains, ((0, 0), (0, 126)))
-    first = gather_rows(jnp.concatenate([w_qkv, gains], axis=1))
+    ordered = w_qkv.reshape(-1, 3, ctx, heads_here, HEAD_DIM).transpose(0, 2, 3, 1, 4)
+    ordered = turned(ordered.reshape(-1, ctx, 3 * own), 1, ctx_index).reshape(w_qkv.shape)
+    first = gather_rows(jnp.concatenate([ordered, gains], axis=1))
     gain_one = first[:, 3 * width].astype(jnp.float32)
     gain_two = first[:, 3 * width + 1].astype(jnp.float32)
     w_out_all = gather_rows(w_out)
     w_up_all = gather_rows(w_up)
     w_down_all = gather_rows(w_down)
-
-    def columns(by):
-        device = (ctx_index + by) % ctx
-        return [
-            lax.dynamic_slice_in_dim(first, kind * width + device * own, own, 1)
-            for kind in range(3)
-        ]
-
-    w_own = jnp.concatenate(columns(0), axis=1)
+    w_own = first[:, : 3 * own]
     w_out_turned = turned(w_out_all.reshape(ctx, heads_here, HEAD_DIM, width), 0, ctx_index)
     w_out_turned = w_out_turned.transpose(1, 0, 2, 3).reshape(width, width)
-    w_turned = jnp.concatenate(sum([columns(by) for by in range(ctx)], []), axis=1)
 
     here = local_rows // BLK
     places = lax.dynamic_slice_in_dim(block_order, ctx_index * here, here)
@@ -446,7 +439,7 @@
             tokens = shift(tokens, ctx, 1)
     kept, mixed_parts = [], []
     for head in range(heads_here):
-        results = attend_last(tables[-1], head, heads_here, packed_list, state)
+        results = attend_last(tables[-1], head, packed_list, state)
         kept.append((results[ctx], results[ctx + 1]))
         mixed_parts += [shift(results[part], ctx, -part) for part in range(ctx)]
     mixed_t = jnp.concatenate(mixed_parts, axis=0)
@@ -488,14 +481,12 @@
 
     grad_parts, grad_whole = [], []
     for head in range(heads_here):
-        if head == heads_here - 1:
+        if head == max(heads_here - 2, 0):
             grad_up_out, grad_w_down, table = lax.optimization_barrier(
                 (grad_up_out, grad_w_down, table)
             )
             grad_up_out, grad_w_down = lax.psum((grad_up_out, grad_w_down), "ctx")
-        results = attend_backward(
-            table, head, heads_here, packed_list, grads_by_head[head], *kept[head]
-        )
+        results = attend_backward(table, head, packed_list, grads_by_head[head], *kept[head])
         grad_parts.append([shift(results[part], ctx, -part) for part in range(ctx)])
         grad_whole.append(results[ctx])
     normed_all = jnp.concatenate(normed_list, axis=0)
@@ -507,15 +498,9 @@
     grad_w_qkv = grad_qkv.transpose(1, 3, 0, 2, 4).reshape(rows_here, 3 * width).astype(jnp.float32)
 
     grad_packed_t = jnp.concatenate(
-        [
-            grad_parts[head][part][kind * HEAD_DIM : (kind + 1) * HEAD_DIM]
-            for part in range(ctx)
-            for kind in range(3)
-            for head in range(heads_here)
-        ],
-        axis=0,
-    )
-    grad_normed_one = product("nu,jn->uj", grad_packed_t, w_turned)
+        [grad_parts[head][part] for part in range(ctx) for head in range(heads_here)], axis=0
+    )
+    grad_normed_one = product("nu,jn->uj", grad_packed_t, first[:, : 3 * width])
     norm_one_back = jax.vjp(lambda v: layer_norm(v, gain_one), tokens_f)[1]
     grad_tokens = (grad_middle + norm_one_back(grad_normed_one)[0]).astype(jnp.bfloat16)
 

time: 613 us -> 579 us (0.945)
  the two profiles are of different devices: /device:TPU:1 before, /device:TPU:0 now
where the time goes in v2:
time: 579 us; the launch traced here: 570 us
  waiting for transfers between devices  156 us (27%)
  starting transfers between devices  116 us (20%)
  Pallas kernels  81.6 us (14%)
  matrix products  80.5 us (14%)
  local copies, waits for them, and re-layouts  55.4 us (10%)
  other arithmetic  42.8 us (7%)
  blocking collectives  20.6 us (4%)
  between operations  16.2 us (3%)
    ppermute x30, waiting for transfers between devices, shift(): return lax.ppermute(array, 'ctx', [(i, (i + by) % ctx) for i in range(ctx)])  97 us
    dot_general x15, matrix products, product(): return jnp.einsum(equation, left, right, preferred_element_type=jnp.float32)  80.5 us
    ppermute x1, starting transfers between devices, scatter_pairs(): got = lax.ppermute(sent, 'fsdp', [(i, i ^ 1) for i in range(fsdp)])  69.9 us
    reduce_scatter x2, waiting for transfers between devices, scatter_rows(): lax.psum_scatter(array.astype(jnp.bfloat16), 'fsdp', scatter_dimension=0,...  56.5 us
    unnamed x162, local copies, waits for them, and re-layouts  46.6 us
    ppermute x30, starting transfers between devices, shift(): return lax.ppermute(array, 'ctx', [(i, (i + by) % ctx) for i in range(ctx)])  42.4 us
    pallas_call x2, Pallas kernels, attend_early(): pl.pallas_call(functools.partial(early_kernel, parts, heads, state is Non...  30.8 us
    pallas_call x3, Pallas kernels, attend_backward(): pl.pallas_call(functools.partial(backward_kernel, parts), grid_spec=pltpu...  26.3 us
  transfers between devices with their start and end apart: 41, of which 10 were waited for; matrix products, arithmetic and copies ran while one was open for 25% of the time, Pallas kernels for 14%

profile of v2, /device:TPU:0, one launch (start us, length us, event | category | flops | bytes accessed | tf_op | source)
XLA Modules:
  0.0 569.6 jit_solution(6491599321564923382)
XLA Ops:
  13.2 3.1 collective-permute-start
  30.3 22.4 %collective-permute-done = bf16[1024,768]{0,1:T(8,128)(2,1)S(1)} collective-permute-done((bf16[1024,768]{0,1:T(8,128)(2,1)S(1)}, bf16[1024,768]{0,1:T(8,128)(2,1)S(1)}, u32[]{:S(2)}, u32[]{:S(2)}) %collective-permute-start) | collective-permute-done | bytes 1572896 | tf_op jit(solution)/shard_map/ppermute | solution.py:361
  55.7 34.5 %collective-permute-done.1 = bf16[1024,768]{0,1:T(8,128)(2,1)} collective-permute-done((bf16[1024,768]{0,1:T(8,128)(2,1)S(1)}, bf16[1024,768]{0,1:T(8,128)(2,1)}, u32[]{:S(2)}, u32[]{:S(2)}) %collective-permute-start.1) | collective-permute-done | bytes 1572896 | tf_op jit(solution)/shard_map/ppermute | solution.py:361
  98.0 10.3 %attend_early.2 = (f32[3,1,4096]{2,1,0:T(1,128)S(1)}, f32[3,1,4096]{2,1,0:T(1,128)S(1)}, f32[3,64,4096]{2,1,0:T(8,128)S(1)}) custom-call(s32[75]{0:T(128)S(1)} %concatenate.39.table, bf16[576,1024]{1,0:T(8,128)(2,1)S(1)} %convolution_convert_fusion.7.refs_0_.refs_4_.refs_8_, bf16[576,1024]{1,0:T(8,128)(2,1)S(1)} %convolution_convert_fusion.6.refs_1_.refs_5_.refs_9_), custom_call_target="tpu_custom_call" | custom-call | flops 20000000000 | bytes 4000000 | tf_op jit(solution)/shard_map/attend_early/pallas_call | solution.py:255
  116.2 20.5 %attend_early.3 = (f32[3,1,4096]{2,1,0:T(1,128)S(1)}, f32[3,1,4096]{2,1,0:T(1,128)S(1)}, f32[3,64,4096]{2,1,0:T(8,128)}) custom-call(s32[75]{0:T(128)S(1)} %concatenate.40.table, bf16[576,1024]{1,0:T(8,128)(2,1)S(1)} %convolution_convert_fusion.7.refs_0_.refs_4_.refs_8_, bf16[576,1024]{1,0:T(8,128)(2,1)S(1)} %convolution_convert_fusion.6.refs_1_.refs_5_.refs_9_, ...), custom_call_target="tpu_custom_call" | custom-call | flops 20000000000 | bytes 4000000 | tf_op jit(solution)/shard_map/attend_early/pallas_call | solution.py:255
  145.0 8.1 %attend_last.3 = (bf16[64,1024]{1,0:T(8,128)(2,1)S(1)}, bf16[64,1024]{1,0:T(8,128)(2,1)S(1)}, bf16[64,1024]{1,0:T(8,128)(2,1)S(1)}, bf16[64,1024]{1,0:T(8,128)(2...) custom-call(s32[75]{0:T(128)S(1)} %concatenate.41.table, ...), custom_call_target="tpu_custom_call" | custom-call | flops 10000000000 | bytes 4000000 | tf_op jit(solution)/shard_map/attend_last/pallas_call | solution.py:281
  154.1 3.7 collective-permute-start.3
  157.8 8.1 %attend_last.5 = (bf16[64,1024]{1,0:T(8,128)(2,1)S(1)}, bf16[64,1024]{1,0:T(8,128)(2,1)S(1)}, bf16[64,1024]{1,0:T(8,128)(2,1)S(1)}, bf16[64,1024]{1,0:T(8,128)(2...) custom-call(s32[75]{0:T(128)S(1)} %concatenate.41.table, ...), custom_call_target="tpu_custom_call" | custom-call | flops 10000000000 | bytes 4000000 | tf_op jit(solution)/shard_map/attend_last/pallas_call | solution.py:281
  166.0 8.3 %attend_last.4 = (bf16[64,1024]{1,0:T(8,128)(2,1)S(1)}, bf16[64,1024]{1,0:T(8,128)(2,1)S(1)}, bf16[64,1024]{1,0:T(8,128)(2,1)S(1)}, bf16[64,1024]{1,0:T(8,128)(2...) custom-call(s32[75]{0:T(128)S(1)} %concatenate.41.table, ...), custom_call_target="tpu_custom_call" | custom-call | flops 10000000000 | bytes 4000000 | tf_op jit(solution)/shard_map/attend_last/pallas_call | solution.py:281
  174.3 3.3 collective-permute-start.9
  182.1 7.8 %collective-permute-done.4 = bf16[64,1024]{1,0:T(8,128)(2,1)S(1)} collective-permute-done((bf16[64,1024]{1,0:T(8,128)(2,1)S(1)}, bf16[64,1024]{1,0:T(8,128)(2,1)S(1)}, u32[]{:S(2)}, u32[]{:S(2)}) %collective-permute-start.4) | collective-permute-done | bytes 131104 | tf_op jit(solution)/shard_map/ppermute | solution.py:361
  194.9 3.8 collective-permute-done.7
  198.7 3.1 collective-permute-done.8
  205.6 8.3 %fusion.82 = f32[1024,3072]{1,0:T(8,128)S(1)} fusion(bf16[768,3072]{1,0:T(8,128)(2,1)} %all-gather.10.cloned.1.call-done, f32[1024,768]{0,1:T(8,128)} %copy-done.29, f32[768]{0:T(1024)S(1)} %get-tuple-element.202, f32[1024]{0:T(1024)S(1)} %fusion.71, f32[1024]{0:T(1024)S(1)} %broadcast_multiply_fusion.1), kind=kOutput, calls=%fused_computation.216 | convolution fusion | flops 4834983936 | bytes 20458496 | tf_op jit(solution)/shard_map/uj,jn->un/dot_general | solution.py:355
  214.0 4.5 copy-done.36
  218.5 9.9 %convolution_convert_fusion = bf16[3072,768]{1,0:T(8,128)(2,1)} fusion(bf16[1024,768]{0,1:T(8,128)(2,1)S(1)} %copy-done.34, f32[1024,3072]{1,0:T(8,128)S(1)} %fusion.82), kind=kOutput, calls=%fused_computation.20 | convolution fusion | flops 4862509056 | bytes 18874368 | tf_op jit(solution)/shard_map/un,uj->nj/dot_general | solution.py:355
  228.7 14.6 %fusion.6 = bf16[1024,3072]{1,0:T(8,128)(2,1)S(1)} fusion(f32[1024,3072]{1,0:T(8,128)} %copy-done.36, bf16[1024,768]{0,1:T(8,128)(2,1)S(1)} %copy-done.34, bf16[3072,768]{1,0:T(8,128)(2,1)} %all-gather.12.cloned.1.call-done), kind=kOutput, calls=%fused_computation.9 | convolution fusion | flops 4894752768 | bytes 25165824 | tf_op jit(solution)/shard_map/uj,nj->un/dot_general | solution.py:355
  243.3 8.5 %multiply_reduce_fusion = (f32[1024]{0:T(1024)S(1)}, f32[1024,768]{0,1:T(8,128)S(1)}) fusion(f32[1024,768]{0,1:T(8,128)} %copy-done.29, f32[768]{0:T(1024)S(1)} %get-tuple-element.202, f32[1024]{0:T(1024)S(1)} %broadcast_multiply_fusion.1, bf16[1024,3072]{1,0:T(8,128)(2,1)S(1)} %fusion.6, bf16[768,3072]{1,0:T(8,128)(2,1)} %all-gather.10.cloned.1.call-done), kind=kOutput, calls=%fused_computation.69 | convolution fusion | flops 4834982912 | bytes 17312768 | tf_op jit(solution)/shard_map/un,jn->uj/dot_general | solution.py:355
  257.2 5.4 convolution_convert_fusion.1
  262.6 3.1 pad_maximum_fusion
  269.7 3.0 convolution_convert_fusion.2
  276.8 9.9 %fusion.49 = bf16[1,1024,768]{1,2,0:T(8,128)(2,1)} fusion(f32[1024,768]{0,1:T(8,128)S(1)} %copy-done.31, bf16[3072,768]{1,0:T(8,128)(2,1)S(1)} %bitcast.108, f32[1024,3072]{1,0:T(8,128)} %copy-done.36), kind=kOutput, calls=%fused_computation.86 | convolution fusion | flops 4861722624 | bytes 22020096 | tf_op jit(solution)/shard_map/un,nj->uj/dot_general | solution.py:355
  289.3 3.4 collective-permute-start.20
  304.1 8.3 %attend_backward.3 = (bf16[192,1024]{1,0:T(8,128)(2,1)S(1)}, bf16[192,1024]{1,0:T(8,128)(2,1)S(1)}, bf16[192,1024]{1,0:T(8,128)(2,1)S(1)}, bf16[192,1024]{1,0:T(8,128)(2,1)S(1)}, bf16[192,4096]{1,0:T(8,128)(2,1)S(1)}) custom-call(s32[9]{0:T(128)S(1)} %pad_add_fusion.table, bf16[576,1024]{1,0:T(8,128)(2,1)S(1)} %copy-done.3, bf16[576,1024]{1,0:T(8,128)(2,1)S(1)} %copy-done.6, ...), custom_call_target="tpu_custom_call" | custom-call | flops 40000000000 | bytes 6000000 | tf_op jit(solution)/shard_map/attend_backward/pallas_call | solution.py:315
  314.3 56.5 %reduce-scatter.3.cloned.1.call-done = bf16[96,3840]{1,0:T(8,128)(2,1)} async-done(((bf16[768,3840]{1,0:T(8,128)(2,1)}), bf16[96,3840]{1,0:T(8,128)(2,1)}) %reduce-scatter.3.cloned.1.call-update) | async-done | bytes 737296 | tf_op jit(solution)/shard_map/reduce_scatter | solution.py:375
  381.5 8.9 %attend_backward.4 = (bf16[192,1024]{1,0:T(8,128)(2,1)S(1)}, bf16[192,1024]{1,0:T(8,128)(2,1)}, bf16[192,1024]{1,0:T(8,128)(2,1)S(1)}, bf16[192,1024]{1,0:T(8,128)(2,1)S(1)}, bf16[192,4096]{1,0:T(8,128)(2,1)S(1)}) custom-call(s32[9]{0:T(128)S(1)} %pad_add_fusion.table, bf16[576,1024]{1,0:T(8,128)(2,1)S(1)} %copy-done.4, bf16[576,1024]{1,0:T(8,128)(2,1)S(1)} %copy-done.7, ...), custom_call_target="tpu_custom_call" | custom-call | flops 40000000000 | bytes 6000000 | tf_op jit(solution)/shard_map/attend_backward/pallas_call | solution.py:315
  395.5 9.1 %attend_backward.5 = (bf16[192,1024]{1,0:T(8,128)(2,1)S(1)}, bf16[192,1024]{1,0:T(8,128)(2,1)}, bf16[192,1024]{1,0:T(8,128)(2,1)S(1)}, bf16[192,1024]{1,0:T(8,128)(2,1)S(1)}, bf16[192,4096]{1,0:T(8,128)(2,1)S(1)}) custom-call(s32[9]{0:T(128)S(1)} %pad_add_fusion.table, bf16[576,1024]{1,0:T(8,128)(2,1)S(1)} %copy-done.4, bf16[576,1024]{1,0:T(8,128)(2,1)S(1)} %copy-done.7, ...), custom_call_target="tpu_custom_call" | custom-call | flops 40000000000 | bytes 6000000 | tf_op jit(solution)/shard_map/attend_backward/pallas_call | solution.py:315
  406.6 9.4 %fusion.7 = f32[768,576]{1,0:T(8,128)S(1)} fusion(bf16[1024,768]{0,1:T(8,128)(2,1)} %copy-done.44, bf16[1024,768]{0,1:T(8,128)(2,1)} %copy-done.43, bf16[1024,768]{0,1:T(8,128)(2,1)} %copy-done.42, bf16[1024,768]{0,1:T(8,128)(2,1)} %copy-done.41, bf16[192,4096]{1,0:T(8,128)(2,1)} %copy-done.23, bf16[192,4096]{1,0:T(8,128)(2,1)} %copy-done.22, ...), kind=kOutput, calls=%fused_computation.11 | convolution fusion | flops 3663200256 | bytes 12779520 | tf_op jit(solution)/shard_map/uj,nu->jn/dot_general | solution.py:355
  425.8 23.0 %collective-permute-done.25 = bf16[192,1024]{1,0:T(8,128)(2,1)S(1)} collective-permute-done((bf16[192,1024]{1,0:T(8,128)(2,1)S(1)}, bf16[192,1024]{1,0:T(8,128)(2,1)S(1)}, u32[]{:S(2)}, u32[]{:S(2)}) %collective-permute-start.25) | collective-permute-done | bytes 393248 | tf_op jit(solution)/shard_map/ppermute | solution.py:361
  448.7 69.9 %collective-permute-start.30 = (bf16[4,96,576]{2,1,0:T(8,128)(2,1)S(1)}, bf16[4,96,576]{2,1,0:T(8,128)(2,1)S(1)}, u32[]{:S(2)}, u32[]{:S(2)}) collective-permute-start(bf16[4,96,576]{2,1,0:T(8,128)(2,1)S(1)} %fusion.59), channel_id=1, source_target_pairs={{0,1},{1,0},{2,3},{3,2},{4,5},{5,4},{6,7},{7,6},{8,9},{9,8},{10,11... | collective-permute-start | bytes 1327112 | tf_op jit(solution)/shard_map/ppermute | solution.py:386
  519.9 4.1 fusion.45
  532.9 20.6 %all-gather = bf16[384,576]{1,0:T(8,128)(2,1)S(1)} all-gather(bf16[96,576]{1,0:T(8,128)(2,1)S(1)} %fusion.64), channel_id=2, replica_groups=mesh['ctx'=4,'fsdp'=8] {'ctx'}, dimensions={0}, use_global_device_ids=true | all-gather | bytes 552960 | tf_op jit(solution)/shard_map/all_gather | solution.py:495
  (335 shorter events, 135.9 us)
Async XLA Ops:
  7.2 45.7 %all-gather.8.cloned.1.call-start = ((), (), s32[]{:S(2)}) async-start(), calls=%async_computation.3 | async-start | bytes 1327104 | tf_op jit(solution)/shard_map/all_gather | solution.py:371
  7.9 82.3 %all-gather.6.cloned.1.call-start = ((), (), s32[]{:S(2)}) async-start(), calls=%async_computation.2 | async-start | bytes 4202496 | tf_op jit(solution)/shard_map/all_gather | solution.py:371
  11.7 193.9 %all-gather.10.cloned.1.call-start = ((), (), s32[]{:S(2)}) async-start(), calls=%async_computation.4 | async-start | bytes 5308416 | tf_op jit(solution)/shard_map/all_gather | solution.py:371
  12.4 216.3 %all-gather.12.cloned.1.call-start = ((), (), s32[]{:S(2)}) async-start(), calls=%async_computation.5 | async-start | bytes 5308416 | tf_op jit(solution)/shard_map/all_gather | solution.py:371
  13.2 39.5 %collective-permute-start = (bf16[1024,768]{0,1:T(8,128)(2,1)S(1)}, bf16[1024,768]{0,1:T(8,128)(2,1)S(1)}, u32[]{:S(2)}, u32[]{:S(2)}) collective-permute-start(bf16[1024,768]{0,1:T(8,128)(2,1)S(1)} %bitcast.89), channel_id=1, source_target_pairs={{0,8},{8,16},{16,24},{24,0},{1,9},{9,17},{17,25},{25,1},{2,10},{10... | collective-permute-start | bytes 4718600 | tf_op jit(solution)/shard_map/ppermute | solution.py:361
  52.8 37.5 %collective-permute-start.1 = (bf16[1024,768]{0,1:T(8,128)(2,1)S(1)}, bf16[1024,768]{0,1:T(8,128)(2,1)}, u32[]{:S(2)}, u32[]{:S(2)}) collective-permute-start(bf16[1024,768]{0,1:T(8,128)(2,1)S(1)} %collective-permute-done), channel_id=1, source_target_pairs={{0,8},{8,16},{16,24},{24,0},{1,9},{9,17},{17,25},{25,1},{2,10},{10... | collective-permute-start | bytes 4718600 | tf_op jit(solution)/shard_map/ppermute | solution.py:361
  52.8 261.5 %reduce-scatter.5.cloned.1.call-start = ((), (), s32[]{:S(2)}) async-start(), calls=%async_computation.7 | async-start | bytes 5308416 | tf_op jit(solution)/shard_map/reduce_scatter | solution.py:375
  90.2 46.5 %collective-permute-start.2 = (bf16[1024,768]{0,1:T(8,128)(2,1)}, bf16[1024,768]{0,1:T(8,128)(2,1)}, u32[]{:S(2)}, u32[]{:S(2)}) collective-permute-start(bf16[1024,768]{0,1:T(8,128)(2,1)} %collective-permute-done.1), channel_id=1, source_target_pairs={{0,8},{8,16},{16,24},{24,0},{1,9},{9,17},{17,25},{25,1},{2,10},{10... | collective-permute-start | bytes 4718600 | tf_op jit(solution)/shard_map/ppermute | solution.py:361
  154.1 26.4 %collective-permute-start.3 = (bf16[64,1024]{1,0:T(8,128)(2,1)S(1)}, bf16[64,1024]{1,0:T(8,128)(2,1)S(1)}, u32[]{:S(2)}, u32[]{:S(2)}) collective-permute-start(bf16[64,1024]{1,0:T(8,128)(2,1)S(1)} %get-tuple-element.93), channel_id=1, source_target_pairs={{0,24},{8,0},{16,8},{24,16},{1,25},{9,1},{17,9},{25,17},{2,26},{10... | collective-permute-start | bytes 393224 | tf_op jit(solution)/shard_map/ppermute | solution.py:361
  174.3 27.5 %collective-permute-start.9 = (bf16[64,1024]{1,0:T(8,128)(2,1)S(1)}, bf16[64,1024]{1,0:T(8,128)(2,1)S(1)}, u32[]{:S(2)}, u32[]{:S(2)}) collective-permute-start(bf16[64,1024]{1,0:T(8,128)(2,1)S(1)} %get-tuple-element.101), channel_id=1, source_target_pairs={{0,24},{8,0},{16,8},{24,16},{1,25},{9,1},{17,9},{25,17},{2,26},{10... | collective-permute-start | bytes 393224 | tf_op jit(solution)/shard_map/ppermute | solution.py:361
  177.6 24.3 %collective-permute-start.10 = (bf16[64,1024]{1,0:T(8,128)(2,1)S(1)}, bf16[64,1024]{1,0:T(8,128)(2,1)S(1)}, u32[]{:S(2)}, u32[]{:S(2)}) collective-permute-start(bf16[64,1024]{1,0:T(8,128)(2,1)S(1)} %get-tuple-element.102), channel_id=1, source_target_pairs={{0,16},{8,24},{16,0},{24,8},{1,17},{9,25},{17,1},{25,9},{2,18},{10... | collective-permute-start | bytes 393224 | tf_op jit(solution)/shard_map/ppermute | solution.py:361
  177.6 24.3 %collective-permute-start.11 = (bf16[64,1024]{1,0:T(8,128)(2,1)S(1)}, bf16[64,1024]{1,0:T(8,128)(2,1)S(1)}, u32[]{:S(2)}, u32[]{:S(2)}) collective-permute-start(bf16[64,1024]{1,0:T(8,128)(2,1)S(1)} %get-tuple-element.103), channel_id=1, source_target_pairs={{0,8},{8,16},{16,24},{24,0},{1,9},{9,17},{17,25},{25,1},{2,10},{10... | collective-permute-start | bytes 393224 | tf_op jit(solution)/shard_map/ppermute | solution.py:361
  228.4 142.4 %reduce-scatter.3.cloned.1.call-start = ((), (), s32[]{:S(2)}) async-start(), calls=%async_computation.6 | async-start | bytes 6635520 | tf_op jit(solution)/shard_map/reduce_scatter | solution.py:375
  265.8 291.0 %all-reduce.4.cloned.1.call-start = ((), (), s32[]{:S(2)}) async-start(), calls=%async_computation.8 | async-start | bytes 2654208 | tf_op jit(solution)/shard_map/psum | solution.py:488
  273.6 19.9 %collective-permute-start.14 = (bf16[64,1024]{1,0:T(8,128)(2,1)S(1)}, bf16[64,1024]{1,0:T(8,128)(2,1)S(1)}, u32[]{:S(2)}, u32[]{:S(2)}) collective-permute-start(bf16[64,1024]{1,0:T(8,128)(2,1)S(1)} %get-tuple-element.231), channel_id=1, source_target_pairs={{0,24},{8,0},{16,8},{24,16},{1,25},{9,1},{17,9},{25,17},{2,26},{10... | collective-permute-start | bytes 393224 | tf_op jit(solution)/shard_map/ppermute | solution.py:361
  276.1 18.3 %collective-permute-start.13 = (bf16[64,1024]{1,0:T(8,128)(2,1)S(1)}, bf16[64,1024]{1,0:T(8,128)(2,1)S(1)}, u32[]{:S(2)}, u32[]{:S(2)}) collective-permute-start(bf16[64,1024]{1,0:T(8,128)(2,1)S(1)} %get-tuple-element.232), channel_id=1, source_target_pairs={{0,16},{8,24},{16,0},{24,8},{1,17},{9,25},{17,1},{25,9},{2,18},{10... | collective-permute-start | bytes 393224 | tf_op jit(solution)/shard_map/ppermute | solution.py:361
  276.1 19.5 %collective-permute-start.12 = (bf16[64,1024]{1,0:T(8,128)(2,1)S(1)}, bf16[64,1024]{1,0:T(8,128)(2,1)S(1)}, u32[]{:S(2)}, u32[]{:S(2)}) collective-permute-start(bf16[64,1024]{1,0:T(8,128)(2,1)S(1)} %get-tuple-element.233), channel_id=1, source_target_pairs={{0,8},{8,16},{16,24},{24,0},{1,9},{9,17},{17,25},{25,1},{2,10},{10... | collective-permute-start | bytes 393224 | tf_op jit(solution)/shard_map/ppermute | solution.py:361
  289.3 102.4 %collective-permute-start.20 = (bf16[64,1024]{1,0:T(8,128)(2,1)}, bf16[64,1024]{1,0:T(8,128)(2,1)S(1)}, u32[]{:S(2)}, u32[]{:S(2)}) collective-permute-start(bf16[64,1024]{1,0:T(8,128)(2,1)} %get-tuple-element.223), channel_id=1, source_target_pairs={{0,24},{8,0},{16,8},{24,16},{1,25},{9,1},{17,9},{25,17},{2,26},{10... | collective-permute-start | bytes 393224 | tf_op jit(solution)/shard_map/ppermute | solution.py:361
  292.7 100.5 %collective-permute-start.19 = (bf16[64,1024]{1,0:T(8,128)(2,1)}, bf16[64,1024]{1,0:T(8,128)(2,1)S(1)}, u32[]{:S(2)}, u32[]{:S(2)}) collective-permute-start(bf16[64,1024]{1,0:T(8,128)(2,1)} %get-tuple-element.224), channel_id=1, source_target_pairs={{0,16},{8,24},{16,0},{24,8},{1,17},{9,25},{17,1},{25,9},{2,18},{10... | collective-permute-start | bytes 393224 | tf_op jit(solution)/shard_map/ppermute | solution.py:361
  293.5 77.3 %collective-permute-start.17 = (bf16[64,1024]{1,0:T(8,128)(2,1)}, bf16[64,1024]{1,0:T(8,128)(2,1)S(1)}, u32[]{:S(2)}, u32[]{:S(2)}) collective-permute-start(bf16[64,1024]{1,0:T(8,128)(2,1)} %get-tuple-element.227), channel_id=1, source_target_pairs={{0,24},{8,0},{16,8},{24,16},{1,25},{9,1},{17,9},{25,17},{2,26},{10... | collective-permute-start | bytes 393224 | tf_op jit(solution)/shard_map/ppermute | solution.py:361
  294.4 77.8 %collective-permute-start.16 = (bf16[64,1024]{1,0:T(8,128)(2,1)}, bf16[64,1024]{1,0:T(8,128)(2,1)S(1)}, u32[]{:S(2)}, u32[]{:S(2)}) collective-permute-start(bf16[64,1024]{1,0:T(8,128)(2,1)} %get-tuple-element.228), channel_id=1, source_target_pairs={{0,16},{8,24},{16,0},{24,8},{1,17},{9,25},{17,1},{25,9},{2,18},{10... | collective-permute-start | bytes 393224 | tf_op jit(solution)/shard_map/ppermute | solution.py:361
  295.7 78.9 %collective-permute-start.15 = (bf16[64,1024]{1,0:T(8,128)(2,1)S(1)}, bf16[64,1024]{1,0:T(8,128)(2,1)S(1)}, u32[]{:S(2)}, u32[]{:S(2)}) collective-permute-start(bf16[64,1024]{1,0:T(8,128)(2,1)S(1)} %get-tuple-element.229), channel_id=1, source_target_pairs={{0,8},{8,16},{16,24},{24,0},{1,9},{9,17},{17,25},{25,1},{2,10},{10... | collective-permute-start | bytes 393224 | tf_op jit(solution)/shard_map/ppermute | solution.py:361
  370.8 24.7 %collective-permute-start.18 = (bf16[64,1024]{1,0:T(8,128)(2,1)S(1)}, bf16[64,1024]{1,0:T(8,128)(2,1)S(1)}, u32[]{:S(2)}, u32[]{:S(2)}) collective-permute-start(bf16[64,1024]{1,0:T(8,128)(2,1)S(1)} %get-tuple-element.225), channel_id=1, source_target_pairs={{0,8},{8,16},{16,24},{24,0},{1,9},{9,17},{17,25},{25,1},{2,10},{10... | collective-permute-start | bytes 393224 | tf_op jit(solution)/shard_map/ppermute | solution.py:361
  372.3 43.9 %collective-permute-start.21 = (bf16[192,1024]{1,0:T(8,128)(2,1)S(1)}, bf16[192,1024]{1,0:T(8,128)(2,1)}, u32[]{:S(2)}, u32[]{:S(2)}) collective-permute-start(bf16[192,1024]{1,0:T(8,128)(2,1)S(1)} %get-tuple-element.116), channel_id=1, source_target_pairs={{0,24},{8,0},{16,8},{24,16},{1,25},{9,1},{17,9},{25,17},{2,26},{10... | collective-permute-start | bytes 1179656 | tf_op jit(solution)/shard_map/ppermute | solution.py:361
  374.6 49.8 %collective-permute-start.24 = (bf16[192,1024]{1,0:T(8,128)(2,1)S(1)}, bf16[192,1024]{1,0:T(8,128)(2,1)}, u32[]{:S(2)}, u32[]{:S(2)}) collective-permute-start(bf16[192,1024]{1,0:T(8,128)(2,1)S(1)} %get-tuple-element.119), channel_id=1, source_target_pairs={{0,16},{8,24},{16,0},{24,8},{1,17},{9,25},{17,1},{25,9},{2,18},{10... | collective-permute-start | bytes 1179656 | tf_op jit(solution)/shard_map/ppermute | solution.py:361
  391.6 127.1 %collective-permute-start.27 = (bf16[192,1024]{1,0:T(8,128)(2,1)S(1)}, bf16[192,1024]{1,0:T(8,128)(2,1)}, u32[]{:S(2)}, u32[]{:S(2)}) collective-permute-start(bf16[192,1024]{1,0:T(8,128)(2,1)S(1)} %get-tuple-element.122), channel_id=1, source_target_pairs={{0,8},{8,16},{16,24},{24,0},{1,9},{9,17},{17,25},{25,1},{2,10},{10... | collective-permute-start | bytes 1179656 | tf_op jit(solution)/shard_map/ppermute | solution.py:361
  393.2 25.2 %collective-permute-start.22 = (bf16[192,1024]{1,0:T(8,128)(2,1)}, bf16[192,1024]{1,0:T(8,128)(2,1)}, u32[]{:S(2)}, u32[]{:S(2)}) collective-permute-start(bf16[192,1024]{1,0:T(8,128)(2,1)} %get-tuple-element.117), channel_id=1, source_target_pairs={{0,24},{8,0},{16,8},{24,16},{1,25},{9,1},{17,9},{25,17},{2,26},{10... | collective-permute-start | bytes 1179656 | tf_op jit(solution)/shard_map/ppermute | solution.py:361
  416.2 32.6 %collective-permute-start.25 = (bf16[192,1024]{1,0:T(8,128)(2,1)S(1)}, bf16[192,1024]{1,0:T(8,128)(2,1)S(1)}, u32[]{:S(2)}, u32[]{:S(2)}) collective-permute-start(bf16[192,1024]{1,0:T(8,128)(2,1)S(1)} %get-tuple-element.120), channel_id=1, source_target_pairs={{0,16},{8,24},{16,0},{24,8},{1,17},{9,25},{17,1},{25,9},{2,18},{10... | collective-permute-start | bytes 1179656 | tf_op jit(solution)/shard_map/ppermute | solution.py:361
  418.5 100.2 %collective-permute-start.26 = (bf16[192,1024]{1,0:T(8,128)(2,1)S(1)}, bf16[192,1024]{1,0:T(8,128)(2,1)S(1)}, u32[]{:S(2)}, u32[]{:S(2)}) collective-permute-start(bf16[192,1024]{1,0:T(8,128)(2,1)S(1)} %copy-done.1), channel_id=1, source_target_pairs={{0,16},{8,24},{16,0},{24,8},{1,17},{9,25},{17,1},{25,9},{2,18},{10... | collective-permute-start | bytes 1179656 | tf_op jit(solution)/shard_map/ppermute | solution.py:361
  421.3 98.4 %collective-permute-start.28 = (bf16[192,1024]{1,0:T(8,128)(2,1)S(1)}, bf16[192,1024]{1,0:T(8,128)(2,1)S(1)}, u32[]{:S(2)}, u32[]{:S(2)}) collective-permute-start(bf16[192,1024]{1,0:T(8,128)(2,1)S(1)} %get-tuple-element.123), channel_id=1, source_target_pairs={{0,8},{8,16},{16,24},{24,0},{1,9},{9,17},{17,25},{25,1},{2,10},{10... | collective-permute-start | bytes 1179656 | tf_op jit(solution)/shard_map/ppermute | solution.py:361
  424.4 95.4 %collective-permute-start.29 = (bf16[192,1024]{1,0:T(8,128)(2,1)S(1)}, bf16[192,1024]{1,0:T(8,128)(2,1)S(1)}, u32[]{:S(2)}, u32[]{:S(2)}) collective-permute-start(bf16[192,1024]{1,0:T(8,128)(2,1)S(1)} %get-tuple-element.124), channel_id=1, source_target_pairs={{0,8},{8,16},{16,24},{24,0},{1,9},{9,17},{17,25},{25,1},{2,10},{10... | collective-permute-start | bytes 1179656 | tf_op jit(solution)/shard_map/ppermute | solution.py:361
  448.7 76.2 %collective-permute-start.30 = (bf16[4,96,576]{2,1,0:T(8,128)(2,1)S(1)}, bf16[4,96,576]{2,1,0:T(8,128)(2,1)S(1)}, u32[]{:S(2)}, u32[]{:S(2)}) collective-permute-start(bf16[4,96,576]{2,1,0:T(8,128)(2,1)S(1)} %fusion.59), channel_id=1, source_target_pairs={{0,1},{1,0},{2,3},{3,2},{4,5},{5,4},{6,7},{7,6},{8,9},{9,8},{10,11... | collective-permute-start | bytes 1327112 | tf_op jit(solution)/shard_map/ppermute | solution.py:386
  (75 other events, 1192.2 us)
Sparse Core Ops, SparseCore 0:
  9.9 26.7 all-gather.7
  39.1 34.6 all-gather.5
  75.7 38.8 all-gather.9
  116.3 38.8 all-gather.11
  228.5 79.2 reduce-scatter.4
  311.1 59.6 reduce-scatter.2
  406.7 148.9 all-reduce.3

commit v3 on v2

--- a/solution.py
+++ b/solution.py
@@ -25,7 +25,7 @@
 
 
 def sign_of(scores):
-    return jnp.tanh(scores.astype(jnp.bfloat16) * jnp.bfloat16(BIG))
+    return jnp.clip(scores.astype(jnp.bfloat16) * jnp.bfloat16(BIG), -1.0, 1.0).astype(jnp.bfloat16)
 
 
 def block_mask(key_start, query_start, length, shape):
@@ -189,8 +189,9 @@
                 positive = jnp.exp2(size).astype(jnp.bfloat16)
                 sign = sign_of(scores)
                 signed_list.append(positive * sign)
-                inner = inner_list[half] - dots[:, halves[half]] * sign.astype(jnp.float32)
-                score_grads_list.append((positive.astype(jnp.float32) * inner).astype(jnp.bfloat16))
+                dot_row = dots[:, halves[half]].astype(jnp.bfloat16)
+                inner = inner_list[half].astype(jnp.bfloat16) - dot_row * sign
+                score_grads_list.append(positive * inner)
             signed = jnp.concatenate(signed_list, axis=1)
             score_grads = jnp.concatenate(score_grads_list, axis=1)
             sums[0:64, span] += nn(keys_t[:, key_span], score_grads)

time: 579 us -> 568 us (0.981)
  starting transfers between devices: 116 us -> 108 us
    ppermute x1, starting transfers between devices: 69.9 us -> 61.6 us  [scatter_pairs(): got = lax.ppermute(sent, 'fsdp', [(i, i ^ 1) for i in range(fsdp)])]
  transfers between devices with their start and end apart: 41 -> 41, of which waited for: 10 -> 10; matrix products, arithmetic and copies ran while one was open for 25% -> 26% of each run, Pallas kernels for 14% -> 14%
where the time goes in v3:
time: 568 us; the launch traced here: 559 us
  waiting for transfers between devices  157 us (28%)
  starting transfers between devices  108 us (19%)
  matrix products  80.5 us (14%)
  Pallas kernels  78.8 us (14%)
  local copies, waits for them, and re-layouts  55.3 us (10%)
  other arithmetic  42.9 us (8%)
  blocking collectives  20.6 us (4%)
  between operations  16.2 us (3%)
    ppermute x30, waiting for transfers between devices, shift(): return lax.ppermute(array, 'ctx', [(i, (i + by) % ctx) for i in range(ctx)])  97.1 us
    dot_general x15, matrix products, product(): return jnp.einsum(equation, left, right, preferred_element_type=jnp.float32)  80.5 us
    ppermute x1, starting transfers between devices, scatter_pairs(): got = lax.ppermute(sent, 'fsdp', [(i, i ^ 1) for i in range(fsdp)])  61.6 us
    reduce_scatter x2, waiting for transfers between devices, scatter_rows(): lax.psum_scatter(array.astype(jnp.bfloat16), 'fsdp', scatter_dimension=0,...  57.2 us
    unnamed x162, local copies, waits for them, and re-layouts  46.5 us
    ppermute x30, starting transfers between devices, shift(): return lax.ppermute(array, 'ctx', [(i, (i + by) % ctx) for i in range(ctx)])  42.3 us
    pallas_call x2, Pallas kernels, attend_early(): pl.pallas_call(functools.partial(early_kernel, parts, heads, state is Non...  30.6 us
    pallas_call x3, Pallas kernels, attend_last(): pl.pallas_call(functools.partial(last_kernel, parts), grid_spec=pltpu.Pre...  24.4 us
  transfers between devices with their start and end apart: 41, of which 10 were waited for; matrix products, arithmetic and copies ran while one was open for 26% of the time, Pallas kernels for 14%

profile of v3, /device:TPU:0, one launch (start us, length us, event | category | flops | bytes accessed | tf_op | source)
XLA Modules:
  0.0 559.2 jit_solution(15954121105973123374)
XLA Ops:
  13.2 3.1 collective-permute-start
  30.3 22.4 %collective-permute-done = bf16[1024,768]{0,1:T(8,128)(2,1)S(1)} collective-permute-done((bf16[1024,768]{0,1:T(8,128)(2,1)S(1)}, bf16[1024,768]{0,1:T(8,128)(2,1)S(1)}, u32[]{:S(2)}, u32[]{:S(2)}) %collective-permute-start) | collective-permute-done | bytes 1572896 | tf_op jit(solution)/shard_map/ppermute | solution.py:362
  55.7 34.5 %collective-permute-done.1 = bf16[1024,768]{0,1:T(8,128)(2,1)} collective-permute-done((bf16[1024,768]{0,1:T(8,128)(2,1)S(1)}, bf16[1024,768]{0,1:T(8,128)(2,1)}, u32[]{:S(2)}, u32[]{:S(2)}) %collective-permute-start.1) | collective-permute-done | bytes 1572896 | tf_op jit(solution)/shard_map/ppermute | solution.py:362
  98.0 10.2 %attend_early.2 = (f32[3,1,4096]{2,1,0:T(1,128)S(1)}, f32[3,1,4096]{2,1,0:T(1,128)S(1)}, f32[3,64,4096]{2,1,0:T(8,128)S(1)}) custom-call(s32[75]{0:T(128)S(1)} %concatenate.39.table, bf16[576,1024]{1,0:T(8,128)(2,1)S(1)} %convolution_convert_fusion.7.refs_0_.refs_4_.refs_8_, bf16[576,1024]{1,0:T(8,128)(2,1)S(1)} %convolution_convert_fusion.6.refs_1_.refs_5_.refs_9_), custom_call_target="tpu_custom_call" | custom-call | flops 20000000000 | bytes 4000000 | tf_op jit(solution)/shard_map/attend_early/pallas_call | solution.py:256
  116.1 20.4 %attend_early.3 = (f32[3,1,4096]{2,1,0:T(1,128)S(1)}, f32[3,1,4096]{2,1,0:T(1,128)S(1)}, f32[3,64,4096]{2,1,0:T(8,128)}) custom-call(s32[75]{0:T(128)S(1)} %concatenate.40.table, bf16[576,1024]{1,0:T(8,128)(2,1)S(1)} %convolution_convert_fusion.7.refs_0_.refs_4_.refs_8_, bf16[576,1024]{1,0:T(8,128)(2,1)S(1)} %convolution_convert_fusion.6.refs_1_.refs_5_.refs_9_, ...), custom_call_target="tpu_custom_call" | custom-call | flops 20000000000 | bytes 4000000 | tf_op jit(solution)/shard_map/attend_early/pallas_call | solution.py:256
  144.9 8.1 %attend_last.3 = (bf16[64,1024]{1,0:T(8,128)(2,1)S(1)}, bf16[64,1024]{1,0:T(8,128)(2,1)S(1)}, bf16[64,1024]{1,0:T(8,128)(2,1)S(1)}, bf16[64,1024]{1,0:T(8,128)(2...) custom-call(s32[75]{0:T(128)S(1)} %concatenate.41.table, ...), custom_call_target="tpu_custom_call" | custom-call | flops 10000000000 | bytes 4000000 | tf_op jit(solution)/shard_map/attend_last/pallas_call | solution.py:282
  154.0 3.7 collective-permute-start.3
  157.7 8.1 %attend_last.5 = (bf16[64,1024]{1,0:T(8,128)(2,1)S(1)}, bf16[64,1024]{1,0:T(8,128)(2,1)S(1)}, bf16[64,1024]{1,0:T(8,128)(2,1)S(1)}, bf16[64,1024]{1,0:T(8,128)(2...) custom-call(s32[75]{0:T(128)S(1)} %concatenate.41.table, ...), custom_call_target="tpu_custom_call" | custom-call | flops 10000000000 | bytes 4000000 | tf_op jit(solution)/shard_map/attend_last/pallas_call | solution.py:282
  165.9 8.3 %attend_last.4 = (bf16[64,1024]{1,0:T(8,128)(2,1)S(1)}, bf16[64,1024]{1,0:T(8,128)(2,1)S(1)}, bf16[64,1024]{1,0:T(8,128)(2,1)S(1)}, bf16[64,1024]{1,0:T(8,128)(2...) custom-call(s32[75]{0:T(128)S(1)} %concatenate.41.table, ...), custom_call_target="tpu_custom_call" | custom-call | flops 10000000000 | bytes 4000000 | tf_op jit(solution)/shard_map/attend_last/pallas_call | solution.py:282
  174.2 3.0 collective-permute-start.9
  181.6 7.8 %collective-permute-done.4 = bf16[64,1024]{1,0:T(8,128)(2,1)S(1)} collective-permute-done((bf16[64,1024]{1,0:T(8,128)(2,1)S(1)}, bf16[64,1024]{1,0:T(8,128)(2,1)S(1)}, u32[]{:S(2)}, u32[]{:S(2)}) %collective-permute-start.4) | collective-permute-done | bytes 131104 | tf_op jit(solution)/shard_map/ppermute | solution.py:362
  194.4 3.8 collective-permute-done.7
  198.3 3.1 collective-permute-done.8
  205.2 8.3 %fusion.82 = f32[1024,3072]{1,0:T(8,128)S(1)} fusion(bf16[768,3072]{1,0:T(8,128)(2,1)} %all-gather.10.cloned.1.call-done, f32[1024,768]{0,1:T(8,128)} %copy-done.29, f32[768]{0:T(1024)S(1)} %get-tuple-element.202, f32[1024]{0:T(1024)S(1)} %fusion.71, f32[1024]{0:T(1024)S(1)} %broadcast_multiply_fusion.1), kind=kOutput, calls=%fused_computation.216 | convolution fusion | flops 4834983936 | bytes 20458496 | tf_op jit(solution)/shard_map/uj,jn->un/dot_general | solution.py:356
  213.5 4.5 copy-done.36
  218.0 9.9 %convolution_convert_fusion = bf16[3072,768]{1,0:T(8,128)(2,1)} fusion(bf16[1024,768]{0,1:T(8,128)(2,1)S(1)} %copy-done.34, f32[1024,3072]{1,0:T(8,128)S(1)} %fusion.82), kind=kOutput, calls=%fused_computation.20 | convolution fusion | flops 4862509056 | bytes 18874368 | tf_op jit(solution)/shard_map/un,uj->nj/dot_general | solution.py:356
  228.3 14.6 %fusion.6 = bf16[1024,3072]{1,0:T(8,128)(2,1)S(1)} fusion(f32[1024,3072]{1,0:T(8,128)} %copy-done.36, bf16[1024,768]{0,1:T(8,128)(2,1)S(1)} %copy-done.34, bf16[3072,768]{1,0:T(8,128)(2,1)} %all-gather.12.cloned.1.call-done), kind=kOutput, calls=%fused_computation.9 | convolution fusion | flops 4894752768 | bytes 25165824 | tf_op jit(solution)/shard_map/uj,nj->un/dot_general | solution.py:356
  242.9 8.5 %multiply_reduce_fusion = (f32[1024]{0:T(1024)S(1)}, f32[1024,768]{0,1:T(8,128)S(1)}) fusion(f32[1024,768]{0,1:T(8,128)} %copy-done.29, f32[768]{0:T(1024)S(1)} %get-tuple-element.202, f32[1024]{0:T(1024)S(1)} %broadcast_multiply_fusion.1, bf16[1024,3072]{1,0:T(8,128)(2,1)S(1)} %fusion.6, bf16[768,3072]{1,0:T(8,128)(2,1)} %all-gather.10.cloned.1.call-done), kind=kOutput, calls=%fused_computation.69 | convolution fusion | flops 4834982912 | bytes 17312768 | tf_op jit(solution)/shard_map/un,jn->uj/dot_general | solution.py:356
  256.8 5.4 convolution_convert_fusion.1
  262.2 3.0 pad_maximum_fusion
  269.2 3.0 convolution_convert_fusion.2
  276.4 9.9 %fusion.49 = bf16[1,1024,768]{1,2,0:T(8,128)(2,1)} fusion(f32[1024,768]{0,1:T(8,128)S(1)} %copy-done.31, bf16[3072,768]{1,0:T(8,128)(2,1)S(1)} %bitcast.108, f32[1024,3072]{1,0:T(8,128)} %copy-done.36), kind=kOutput, calls=%fused_computation.86 | convolution fusion | flops 4861722624 | bytes 22020096 | tf_op jit(solution)/shard_map/un,nj->uj/dot_general | solution.py:356
  288.9 3.4 collective-permute-start.20
  303.7 7.5 %attend_backward.3 = (bf16[192,1024]{1,0:T(8,128)(2,1)S(1)}, bf16[192,1024]{1,0:T(8,128)(2,1)S(1)}, bf16[192,1024]{1,0:T(8,128)(2,1)S(1)}, bf16[192,1024]{1,0:T(8,128)(2,1)S(1)}, bf16[192,4096]{1,0:T(8,128)(2,1)S(1)}) custom-call(s32[9]{0:T(128)S(1)} %pad_add_fusion.table, bf16[576,1024]{1,0:T(8,128)(2,1)S(1)} %copy-done.3, bf16[576,1024]{1,0:T(8,128)(2,1)S(1)} %copy-done.6, ...), custom_call_target="tpu_custom_call" | custom-call | flops 40000000000 | bytes 6000000 | tf_op jit(solution)/shard_map/attend_backward/pallas_call | solution.py:316
  313.1 57.2 %reduce-scatter.3.cloned.1.call-done = bf16[96,3840]{1,0:T(8,128)(2,1)} async-done(((bf16[768,3840]{1,0:T(8,128)(2,1)}), bf16[96,3840]{1,0:T(8,128)(2,1)}) %reduce-scatter.3.cloned.1.call-update) | async-done | bytes 737296 | tf_op jit(solution)/shard_map/reduce_scatter | solution.py:376
  381.2 8.1 %attend_backward.4 = (bf16[192,1024]{1,0:T(8,128)(2,1)S(1)}, bf16[192,1024]{1,0:T(8,128)(2,1)}, bf16[192,1024]{1,0:T(8,128)(2,1)S(1)}, bf16[192,1024]{1,0:T(8,128)(2,1)S(1)}, bf16[192,4096]{1,0:T(8,128)(2,1)S(1)}) custom-call(s32[9]{0:T(128)S(1)} %pad_add_fusion.table, bf16[576,1024]{1,0:T(8,128)(2,1)S(1)} %copy-done.4, bf16[576,1024]{1,0:T(8,128)(2,1)S(1)} %copy-done.7, ...), custom_call_target="tpu_custom_call" | custom-call | flops 40000000000 | bytes 6000000 | tf_op jit(solution)/shard_map/attend_backward/pallas_call | solution.py:316
  394.3 8.2 %attend_backward.5 = (bf16[192,1024]{1,0:T(8,128)(2,1)S(1)}, bf16[192,1024]{1,0:T(8,128)(2,1)}, bf16[192,1024]{1,0:T(8,128)(2,1)S(1)}, bf16[192,1024]{1,0:T(8,128)(2,1)S(1)}, bf16[192,4096]{1,0:T(8,128)(2,1)S(1)}) custom-call(s32[9]{0:T(128)S(1)} %pad_add_fusion.table, bf16[576,1024]{1,0:T(8,128)(2,1)S(1)} %copy-done.4, bf16[576,1024]{1,0:T(8,128)(2,1)S(1)} %copy-done.7, ...), custom_call_target="tpu_custom_call" | custom-call | flops 40000000000 | bytes 6000000 | tf_op jit(solution)/shard_map/attend_backward/pallas_call | solution.py:316
  404.6 9.4 %fusion.7 = f32[768,576]{1,0:T(8,128)S(1)} fusion(bf16[1024,768]{0,1:T(8,128)(2,1)} %copy-done.44, bf16[1024,768]{0,1:T(8,128)(2,1)} %copy-done.43, bf16[1024,768]{0,1:T(8,128)(2,1)} %copy-done.42, bf16[1024,768]{0,1:T(8,128)(2,1)} %copy-done.41, bf16[192,4096]{1,0:T(8,128)(2,1)} %copy-done.23, bf16[192,4096]{1,0:T(8,128)(2,1)} %copy-done.22, ...), kind=kOutput, calls=%fused_computation.11 | convolution fusion | flops 3663200256 | bytes 12779520 | tf_op jit(solution)/shard_map/uj,nu->jn/dot_general | solution.py:356
  423.6 23.1 %collective-permute-done.25 = bf16[192,1024]{1,0:T(8,128)(2,1)S(1)} collective-permute-done((bf16[192,1024]{1,0:T(8,128)(2,1)S(1)}, bf16[192,1024]{1,0:T(8,128)(2,1)S(1)}, u32[]{:S(2)}, u32[]{:S(2)}) %collective-permute-start.25) | collective-permute-done | bytes 393248 | tf_op jit(solution)/shard_map/ppermute | solution.py:362
  446.7 61.6 %collective-permute-start.30 = (bf16[4,96,576]{2,1,0:T(8,128)(2,1)S(1)}, bf16[4,96,576]{2,1,0:T(8,128)(2,1)S(1)}, u32[]{:S(2)}, u32[]{:S(2)}) collective-permute-start(bf16[4,96,576]{2,1,0:T(8,128)(2,1)S(1)} %fusion.59), channel_id=1, source_target_pairs={{0,1},{1,0},{2,3},{3,2},{4,5},{5,4},{6,7},{7,6},{8,9},{9,8},{10,11... | collective-permute-start | bytes 1327112 | tf_op jit(solution)/shard_map/ppermute | solution.py:387
  509.5 4.1 fusion.45
  522.6 20.6 %all-gather = bf16[384,576]{1,0:T(8,128)(2,1)S(1)} all-gather(bf16[96,576]{1,0:T(8,128)(2,1)S(1)} %fusion.64), channel_id=2, replica_groups=mesh['ctx'=4,'fsdp'=8] {'ctx'}, dimensions={0}, use_global_device_ids=true | all-gather | bytes 552960 | tf_op jit(solution)/shard_map/all_gather | solution.py:496
  (335 shorter events, 136.2 us)
Async XLA Ops:
  7.2 45.7 %all-gather.8.cloned.1.call-start = ((), (), s32[]{:S(2)}) async-start(), calls=%async_computation.3 | async-start | bytes 1327104 | tf_op jit(solution)/shard_map/all_gather | solution.py:372
  7.9 82.3 %all-gather.6.cloned.1.call-start = ((), (), s32[]{:S(2)}) async-start(), calls=%async_computation.2 | async-start | bytes 4202496 | tf_op jit(solution)/shard_map/all_gather | solution.py:372
  11.7 193.5 %all-gather.10.cloned.1.call-start = ((), (), s32[]{:S(2)}) async-start(), calls=%async_computation.4 | async-start | bytes 5308416 | tf_op jit(solution)/shard_map/all_gather | solution.py:372
  12.4 215.9 %all-gather.12.cloned.1.call-start = ((), (), s32[]{:S(2)}) async-start(), calls=%async_computation.5 | async-start | bytes 5308416 | tf_op jit(solution)/shard_map/all_gather | solution.py:372
  13.2 39.5 %collective-permute-start = (bf16[1024,768]{0,1:T(8,128)(2,1)S(1)}, bf16[1024,768]{0,1:T(8,128)(2,1)S(1)}, u32[]{:S(2)}, u32[]{:S(2)}) collective-permute-start(bf16[1024,768]{0,1:T(8,128)(2,1)S(1)} %bitcast.89), channel_id=1, source_target_pairs={{0,8},{8,16},{16,24},{24,0},{1,9},{9,17},{17,25},{25,1},{2,10},{10... | collective-permute-start | bytes 4718600 | tf_op jit(solution)/shard_map/ppermute | solution.py:362
  52.8 37.5 %collective-permute-start.1 = (bf16[1024,768]{0,1:T(8,128)(2,1)S(1)}, bf16[1024,768]{0,1:T(8,128)(2,1)}, u32[]{:S(2)}, u32[]{:S(2)}) collective-permute-start(bf16[1024,768]{0,1:T(8,128)(2,1)S(1)} %collective-permute-done), channel_id=1, source_target_pairs={{0,8},{8,16},{16,24},{24,0},{1,9},{9,17},{17,25},{25,1},{2,10},{10... | collective-permute-start | bytes 4718600 | tf_op jit(solution)/shard_map/ppermute | solution.py:362
  52.8 260.3 %reduce-scatter.5.cloned.1.call-start = ((), (), s32[]{:S(2)}) async-start(), calls=%async_computation.7 | async-start | bytes 5308416 | tf_op jit(solution)/shard_map/reduce_scatter | solution.py:376
  90.2 46.2 %collective-permute-start.2 = (bf16[1024,768]{0,1:T(8,128)(2,1)}, bf16[1024,768]{0,1:T(8,128)(2,1)}, u32[]{:S(2)}, u32[]{:S(2)}) collective-permute-start(bf16[1024,768]{0,1:T(8,128)(2,1)} %collective-permute-done.1), channel_id=1, source_target_pairs={{0,8},{8,16},{16,24},{24,0},{1,9},{9,17},{17,25},{25,1},{2,10},{10... | collective-permute-start | bytes 4718600 | tf_op jit(solution)/shard_map/ppermute | solution.py:362
  154.0 26.1 %collective-permute-start.3 = (bf16[64,1024]{1,0:T(8,128)(2,1)S(1)}, bf16[64,1024]{1,0:T(8,128)(2,1)S(1)}, u32[]{:S(2)}, u32[]{:S(2)}) collective-permute-start(bf16[64,1024]{1,0:T(8,128)(2,1)S(1)} %get-tuple-element.93), channel_id=1, source_target_pairs={{0,24},{8,0},{16,8},{24,16},{1,25},{9,1},{17,9},{25,17},{2,26},{10... | collective-permute-start | bytes 393224 | tf_op jit(solution)/shard_map/ppermute | solution.py:362
  174.2 27.2 %collective-permute-start.9 = (bf16[64,1024]{1,0:T(8,128)(2,1)S(1)}, bf16[64,1024]{1,0:T(8,128)(2,1)S(1)}, u32[]{:S(2)}, u32[]{:S(2)}) collective-permute-start(bf16[64,1024]{1,0:T(8,128)(2,1)S(1)} %get-tuple-element.101), channel_id=1, source_target_pairs={{0,24},{8,0},{16,8},{24,16},{1,25},{9,1},{17,9},{25,17},{2,26},{10... | collective-permute-start | bytes 393224 | tf_op jit(solution)/shard_map/ppermute | solution.py:362
  177.2 24.2 %collective-permute-start.10 = (bf16[64,1024]{1,0:T(8,128)(2,1)S(1)}, bf16[64,1024]{1,0:T(8,128)(2,1)S(1)}, u32[]{:S(2)}, u32[]{:S(2)}) collective-permute-start(bf16[64,1024]{1,0:T(8,128)(2,1)S(1)} %get-tuple-element.102), channel_id=1, source_target_pairs={{0,16},{8,24},{16,0},{24,8},{1,17},{9,25},{17,1},{25,9},{2,18},{10... | collective-permute-start | bytes 393224 | tf_op jit(solution)/shard_map/ppermute | solution.py:362
  177.2 24.3 %collective-permute-start.11 = (bf16[64,1024]{1,0:T(8,128)(2,1)S(1)}, bf16[64,1024]{1,0:T(8,128)(2,1)S(1)}, u32[]{:S(2)}, u32[]{:S(2)}) collective-permute-start(bf16[64,1024]{1,0:T(8,128)(2,1)S(1)} %get-tuple-element.103), channel_id=1, source_target_pairs={{0,8},{8,16},{16,24},{24,0},{1,9},{9,17},{17,25},{25,1},{2,10},{10... | collective-permute-start | bytes 393224 | tf_op jit(solution)/shard_map/ppermute | solution.py:362
  228.0 142.3 %reduce-scatter.3.cloned.1.call-start = ((), (), s32[]{:S(2)}) async-start(), calls=%async_computation.6 | async-start | bytes 6635520 | tf_op jit(solution)/shard_map/reduce_scatter | solution.py:376
  265.3 281.2 %all-reduce.4.cloned.1.call-start = ((), (), s32[]{:S(2)}) async-start(), calls=%async_computation.8 | async-start | bytes 2654208 | tf_op jit(solution)/shard_map/psum | solution.py:489
  273.1 20.1 %collective-permute-start.14 = (bf16[64,1024]{1,0:T(8,128)(2,1)S(1)}, bf16[64,1024]{1,0:T(8,128)(2,1)S(1)}, u32[]{:S(2)}, u32[]{:S(2)}) collective-permute-start(bf16[64,1024]{1,0:T(8,128)(2,1)S(1)} %get-tuple-element.231), channel_id=1, source_target_pairs={{0,24},{8,0},{16,8},{24,16},{1,25},{9,1},{17,9},{25,17},{2,26},{10... | collective-permute-start | bytes 393224 | tf_op jit(solution)/shard_map/ppermute | solution.py:362
  275.8 18.3 %collective-permute-start.13 = (bf16[64,1024]{1,0:T(8,128)(2,1)S(1)}, bf16[64,1024]{1,0:T(8,128)(2,1)S(1)}, u32[]{:S(2)}, u32[]{:S(2)}) collective-permute-start(bf16[64,1024]{1,0:T(8,128)(2,1)S(1)} %get-tuple-element.232), channel_id=1, source_target_pairs={{0,16},{8,24},{16,0},{24,8},{1,17},{9,25},{17,1},{25,9},{2,18},{10... | collective-permute-start | bytes 393224 | tf_op jit(solution)/shard_map/ppermute | solution.py:362
  275.8 19.5 %collective-permute-start.12 = (bf16[64,1024]{1,0:T(8,128)(2,1)S(1)}, bf16[64,1024]{1,0:T(8,128)(2,1)S(1)}, u32[]{:S(2)}, u32[]{:S(2)}) collective-permute-start(bf16[64,1024]{1,0:T(8,128)(2,1)S(1)} %get-tuple-element.233), channel_id=1, source_target_pairs={{0,8},{8,16},{16,24},{24,0},{1,9},{9,17},{17,25},{25,1},{2,10},{10... | collective-permute-start | bytes 393224 | tf_op jit(solution)/shard_map/ppermute | solution.py:362
  288.9 101.6 %collective-permute-start.20 = (bf16[64,1024]{1,0:T(8,128)(2,1)}, bf16[64,1024]{1,0:T(8,128)(2,1)S(1)}, u32[]{:S(2)}, u32[]{:S(2)}) collective-permute-start(bf16[64,1024]{1,0:T(8,128)(2,1)} %get-tuple-element.223), channel_id=1, source_target_pairs={{0,24},{8,0},{16,8},{24,16},{1,25},{9,1},{17,9},{25,17},{2,26},{10... | collective-permute-start | bytes 393224 | tf_op jit(solution)/shard_map/ppermute | solution.py:362
  292.3 99.6 %collective-permute-start.19 = (bf16[64,1024]{1,0:T(8,128)(2,1)}, bf16[64,1024]{1,0:T(8,128)(2,1)S(1)}, u32[]{:S(2)}, u32[]{:S(2)}) collective-permute-start(bf16[64,1024]{1,0:T(8,128)(2,1)} %get-tuple-element.224), channel_id=1, source_target_pairs={{0,16},{8,24},{16,0},{24,8},{1,17},{9,25},{17,1},{25,9},{2,18},{10... | collective-permute-start | bytes 393224 | tf_op jit(solution)/shard_map/ppermute | solution.py:362
  293.1 77.2 %collective-permute-start.17 = (bf16[64,1024]{1,0:T(8,128)(2,1)}, bf16[64,1024]{1,0:T(8,128)(2,1)S(1)}, u32[]{:S(2)}, u32[]{:S(2)}) collective-permute-start(bf16[64,1024]{1,0:T(8,128)(2,1)} %get-tuple-element.227), channel_id=1, source_target_pairs={{0,24},{8,0},{16,8},{24,16},{1,25},{9,1},{17,9},{25,17},{2,26},{10... | collective-permute-start | bytes 393224 | tf_op jit(solution)/shard_map/ppermute | solution.py:362
  294.1 77.8 %collective-permute-start.16 = (bf16[64,1024]{1,0:T(8,128)(2,1)}, bf16[64,1024]{1,0:T(8,128)(2,1)S(1)}, u32[]{:S(2)}, u32[]{:S(2)}) collective-permute-start(bf16[64,1024]{1,0:T(8,128)(2,1)} %get-tuple-element.228), channel_id=1, source_target_pairs={{0,16},{8,24},{16,0},{24,8},{1,17},{9,25},{17,1},{25,9},{2,18},{10... | collective-permute-start | bytes 393224 | tf_op jit(solution)/shard_map/ppermute | solution.py:362
  295.3 78.9 %collective-permute-start.15 = (bf16[64,1024]{1,0:T(8,128)(2,1)S(1)}, bf16[64,1024]{1,0:T(8,128)(2,1)S(1)}, u32[]{:S(2)}, u32[]{:S(2)}) collective-permute-start(bf16[64,1024]{1,0:T(8,128)(2,1)S(1)} %get-tuple-element.229), channel_id=1, source_target_pairs={{0,8},{8,16},{16,24},{24,0},{1,9},{9,17},{17,25},{25,1},{2,10},{10... | collective-permute-start | bytes 393224 | tf_op jit(solution)/shard_map/ppermute | solution.py:362
  370.3 24.0 %collective-permute-start.18 = (bf16[64,1024]{1,0:T(8,128)(2,1)S(1)}, bf16[64,1024]{1,0:T(8,128)(2,1)S(1)}, u32[]{:S(2)}, u32[]{:S(2)}) collective-permute-start(bf16[64,1024]{1,0:T(8,128)(2,1)S(1)} %get-tuple-element.225), channel_id=1, source_target_pairs={{0,8},{8,16},{16,24},{24,0},{1,9},{9,17},{17,25},{25,1},{2,10},{10... | collective-permute-start | bytes 393224 | tf_op jit(solution)/shard_map/ppermute | solution.py:362
  371.9 42.3 %collective-permute-start.21 = (bf16[192,1024]{1,0:T(8,128)(2,1)S(1)}, bf16[192,1024]{1,0:T(8,128)(2,1)}, u32[]{:S(2)}, u32[]{:S(2)}) collective-permute-start(bf16[192,1024]{1,0:T(8,128)(2,1)S(1)} %get-tuple-element.116), channel_id=1, source_target_pairs={{0,24},{8,0},{16,8},{24,16},{1,25},{9,1},{17,9},{25,17},{2,26},{10... | collective-permute-start | bytes 1179656 | tf_op jit(solution)/shard_map/ppermute | solution.py:362
  374.2 48.3 %collective-permute-start.24 = (bf16[192,1024]{1,0:T(8,128)(2,1)S(1)}, bf16[192,1024]{1,0:T(8,128)(2,1)}, u32[]{:S(2)}, u32[]{:S(2)}) collective-permute-start(bf16[192,1024]{1,0:T(8,128)(2,1)S(1)} %get-tuple-element.119), channel_id=1, source_target_pairs={{0,16},{8,24},{16,0},{24,8},{1,17},{9,25},{17,1},{25,9},{2,18},{10... | collective-permute-start | bytes 1179656 | tf_op jit(solution)/shard_map/ppermute | solution.py:362
  390.5 117.9 %collective-permute-start.27 = (bf16[192,1024]{1,0:T(8,128)(2,1)S(1)}, bf16[192,1024]{1,0:T(8,128)(2,1)}, u32[]{:S(2)}, u32[]{:S(2)}) collective-permute-start(bf16[192,1024]{1,0:T(8,128)(2,1)S(1)} %get-tuple-element.122), channel_id=1, source_target_pairs={{0,8},{8,16},{16,24},{24,0},{1,9},{9,17},{17,25},{25,1},{2,10},{10... | collective-permute-start | bytes 1179656 | tf_op jit(solution)/shard_map/ppermute | solution.py:362
  391.9 24.5 %collective-permute-start.22 = (bf16[192,1024]{1,0:T(8,128)(2,1)}, bf16[192,1024]{1,0:T(8,128)(2,1)}, u32[]{:S(2)}, u32[]{:S(2)}) collective-permute-start(bf16[192,1024]{1,0:T(8,128)(2,1)} %get-tuple-element.117), channel_id=1, source_target_pairs={{0,24},{8,0},{16,8},{24,16},{1,25},{9,1},{17,9},{25,17},{2,26},{10... | collective-permute-start | bytes 1179656 | tf_op jit(solution)/shard_map/ppermute | solution.py:362
  414.2 32.5 %collective-permute-start.25 = (bf16[192,1024]{1,0:T(8,128)(2,1)S(1)}, bf16[192,1024]{1,0:T(8,128)(2,1)S(1)}, u32[]{:S(2)}, u32[]{:S(2)}) collective-permute-start(bf16[192,1024]{1,0:T(8,128)(2,1)S(1)} %get-tuple-element.120), channel_id=1, source_target_pairs={{0,16},{8,24},{16,0},{24,8},{1,17},{9,25},{17,1},{25,9},{2,18},{10... | collective-permute-start | bytes 1179656 | tf_op jit(solution)/shard_map/ppermute | solution.py:362
  416.5 91.8 %collective-permute-start.26 = (bf16[192,1024]{1,0:T(8,128)(2,1)S(1)}, bf16[192,1024]{1,0:T(8,128)(2,1)S(1)}, u32[]{:S(2)}, u32[]{:S(2)}) collective-permute-start(bf16[192,1024]{1,0:T(8,128)(2,1)S(1)} %copy-done.1), channel_id=1, source_target_pairs={{0,16},{8,24},{16,0},{24,8},{1,17},{9,25},{17,1},{25,9},{2,18},{10... | collective-permute-start | bytes 1179656 | tf_op jit(solution)/shard_map/ppermute | solution.py:362
  419.4 90.0 %collective-permute-start.28 = (bf16[192,1024]{1,0:T(8,128)(2,1)S(1)}, bf16[192,1024]{1,0:T(8,128)(2,1)S(1)}, u32[]{:S(2)}, u32[]{:S(2)}) collective-permute-start(bf16[192,1024]{1,0:T(8,128)(2,1)S(1)} %get-tuple-element.123), channel_id=1, source_target_pairs={{0,8},{8,16},{16,24},{24,0},{1,9},{9,17},{17,25},{25,1},{2,10},{10... | collective-permute-start | bytes 1179656 | tf_op jit(solution)/shard_map/ppermute | solution.py:362
  422.5 87.0 %collective-permute-start.29 = (bf16[192,1024]{1,0:T(8,128)(2,1)S(1)}, bf16[192,1024]{1,0:T(8,128)(2,1)S(1)}, u32[]{:S(2)}, u32[]{:S(2)}) collective-permute-start(bf16[192,1024]{1,0:T(8,128)(2,1)S(1)} %get-tuple-element.124), channel_id=1, source_target_pairs={{0,8},{8,16},{16,24},{24,0},{1,9},{9,17},{17,25},{25,1},{2,10},{10... | collective-permute-start | bytes 1179656 | tf_op jit(solution)/shard_map/ppermute | solution.py:362
  446.7 67.8 %collective-permute-start.30 = (bf16[4,96,576]{2,1,0:T(8,128)(2,1)S(1)}, bf16[4,96,576]{2,1,0:T(8,128)(2,1)S(1)}, u32[]{:S(2)}, u32[]{:S(2)}) collective-permute-start(bf16[4,96,576]{2,1,0:T(8,128)(2,1)S(1)} %fusion.59), channel_id=1, source_target_pairs={{0,1},{1,0},{2,3},{3,2},{4,5},{5,4},{6,7},{7,6},{8,9},{9,8},{10,11... | collective-permute-start | bytes 1327112 | tf_op jit(solution)/shard_map/ppermute | solution.py:387
  (75 other events, 1156.0 us)
Sparse Core Ops, SparseCore 0:
  9.9 26.7 all-gather.7
  39.1 34.6 all-gather.5
  75.7 38.8 all-gather.9
  116.3 38.8 all-gather.11
  228.1 79.1 reduce-scatter.4
  310.7 59.6 reduce-scatter.2
  404.7 140.6 all-reduce.3

commit v4 on v3

--- a/solution.py
+++ b/solution.py
@@ -150,7 +150,7 @@
     query_refs, key_refs, value_refs = refs[:parts], refs[parts : 2 * parts], refs[2 * parts : 3 * parts]
     grad_refs, refs = refs[3 * parts : 4 * parts], refs[4 * parts :]
     exact_ref, log_ref, sends, refs = refs[0], refs[1], refs[2 : 2 + parts], refs[2 + parts :]
-    whole_ref, queries, keys_t, values_t, grads, keys, values, sums, weights, grad_weights, dots = refs
+    whole_ref, queries, keys_t, values_t, grads, keys, values, sums, weights, grad_weights, dots, scores_ref, inner_ref = refs
     blocks = queries.shape[1] // BLK
     length = table[blocks]
     scale = HEAD_DIM ** -0.5
@@ -172,15 +172,18 @@
         grad_weights[:HEAD_DIM, :] = grad_t
         dots[...] = jnp.sum(grad_t.astype(jnp.float32) * exact_ref[:, span], axis=0, keepdims=True)
 
+        halves = [slice(h * HALF, (h + 1) * HALF) for h in range(2)]
+
+        def start_half(number, half):
+            key_span = pl.ds(pl.multiple_of(table[number] * BLK, BLK), BLK)
+            scores_ref[half] = nn(keys[key_span, :], weights[:, halves[half]])
+            inner_ref[half] = nn(values[key_span, :], grad_weights[:, halves[half]])
+
         def step(number, masked):
             key_span = pl.ds(pl.multiple_of(table[number] * BLK, BLK), BLK)
-            key_rows, value_rows = keys[key_span, :], values[key_span, :]
-            halves = [slice(h * HALF, (h + 1) * HALF) for h in range(2)]
-            scores_list = [nn(key_rows, weights[:, h]) for h in halves]
-            inner_list = [nn(value_rows, grad_weights[:, h]) for h in halves]
             signed_list, score_grads_list = [], []
             for half in range(2):
-                scores = scores_list[half]
+                scores = scores_ref[half]
                 log_row = log_ref[:, pl.ds(pl.multiple_of(table[place] * BLK + half * HALF, HALF), HALF)]
                 size = jnp.abs(scores) - log_row
                 if masked:
@@ -190,13 +193,18 @@
                 sign = sign_of(scores)
                 signed_list.append(positive * sign)
                 dot_row = dots[:, halves[half]].astype(jnp.bfloat16)
-                inner = inner_list[half].astype(jnp.bfloat16) - dot_row * sign
+                inner = inner_ref[half].astype(jnp.bfloat16) - dot_row * sign
                 score_grads_list.append(positive * inner)
+                if not masked:
+                    start_half(number + 1, half)
             signed = jnp.concatenate(signed_list, axis=1)
             score_grads = jnp.concatenate(score_grads_list, axis=1)
             sums[0:64, span] += nn(keys_t[:, key_span], score_grads)
             sums[64:128, key_span] += nt(queries[:, span], score_grads)
             sums[128:192, key_span] += nt(grads[:, span], signed)
+
+        for half in range(2):
+            start_half(0, half)
 
         @pl.loop(0, place)
         def _(number):
@@ -211,6 +219,34 @@
             done = (sums[rows, span] * factor).astype(jnp.bfloat16)
             whole_ref[rows, span] = done
             sends[part][rows, :] = done
+
+
+def join_kernel(*refs):
+    pieces, weight_ref, out_ref, joined = refs[:-3], refs[-3], refs[-2], refs[-1]
+    rows = pieces[0].shape[0]
+    for number, piece in enumerate(pieces):
+        joined[number * rows : (number + 1) * rows, :] = piece[...]
+
+    @pl.loop(0, weight_ref.shape[0] // HALF)
+    def _(tile):
+        span = pl.ds(pl.multiple_of(tile * HALF, HALF), HALF)
+        out_ref[:, span] = nn(weight_ref[span, : joined.shape[0]], joined[...]).T
+
+
+def join_product(pieces, weight):
+    rows, span = pieces[0].shape
+    width = weight.shape[0]
+    total = len(pieces) * rows
+    return pl.pallas_call(
+        join_kernel,
+        out_shape=jax.ShapeDtypeStruct((span, width), jnp.float32),
+        scratch_shapes=[pltpu.VMEM((total, span), jnp.bfloat16)],
+        compiler_params=pltpu.CompilerParams(vmem_limit_bytes=48 << 20),
+        cost_estimate=pl.CostEstimate(
+            flops=2 * span * width * total, bytes_accessed=12_000_000, transcendentals=0
+        ),
+        name="join_product",
+    )(*pieces, weight)
 
 
 def make_table(block_order, length, ctx_index, ctx):
@@ -331,6 +367,8 @@
                 pltpu.VMEM((128, BLK), jnp.bfloat16),
                 pltpu.VMEM((128, BLK), jnp.bfloat16),
                 pltpu.VMEM((1, BLK), jnp.float32),
+                pltpu.VMEM((2, BLK, HALF), jnp.float32),
+                pltpu.VMEM((2, BLK, HALF), jnp.float32),
             ],
         ),
         out_shape=[jax.ShapeDtypeStruct((three, span), jnp.bfloat16)] * parts
@@ -493,15 +531,13 @@
     normed_all = jnp.concatenate(normed_list, axis=0)
     grad_qkv_own = product("uj,nu->jn", normed_all, jnp.concatenate(grad_whole, axis=0))
     grad_qkv_own = scatter_pairs(grad_qkv_own, fsdp).astype(jnp.bfloat16)
-    grad_qkv = lax.all_gather(grad_qkv_own, "ctx", axis=0)
+    grad_qkv = [shift(grad_qkv_own, ctx, -part) for part in range(ctx)]
+    grad_qkv = turned(jnp.stack(grad_qkv), 0, (ctx - ctx_index) % ctx)
     rows_here = grad_qkv.shape[1]
     grad_qkv = grad_qkv.reshape(ctx, rows_here, heads_here, 3, HEAD_DIM)
     grad_w_qkv = grad_qkv.transpose(1, 3, 0, 2, 4).reshape(rows_here, 3 * width).astype(jnp.float32)
 
-    grad_packed_t = jnp.concatenate(
-        [grad_parts[head][part] for part in range(ctx) for head in range(heads_here)], axis=0
-    )
-    grad_normed_one = product("nu,jn->uj", grad_packed_t, first[:, : 3 * width])
+    grad_normed_one = join_product([grad_parts[head][part] for part in range(ctx) for head in range(heads_here)], first)
     norm_one_back = jax.vjp(lambda v: layer_norm(v, gain_one), tokens_f)[1]
     grad_tokens = (grad_middle + norm_one_back(grad_normed_one)[0]).astype(jnp.bfloat16)
 

time: 568 us -> 579 us (1.019)
  blocking collectives: 20.6 us -> 0 us
  starting transfers between devices: 108 us -> 122 us
  Pallas kernels: 78.8 us -> 89 us
  local copies, waits for them, and re-layouts: 55.3 us -> 46.6 us
  waiting for transfers between devices: 157 us -> 165 us
    all_gather x1 -> x0, blocking collectives: 20.6 us -> none  [per_device(): grad_qkv = lax.all_gather(grad_qkv_own, 'ctx', axis=0)]
    ppermute x3, starting transfers between devices: 3.55 us -> 23.7 us  [scatter_pairs(): got = lax.ppermute(sent, 'fsdp', [(i, i ^ 2 * other) for i in range(fsdp)])]
    ppermute x30 -> x33, waiting for transfers between devices: 97.1 us -> 82.6 us  [shift(): return lax.ppermute(array, 'ctx', [(i, (i + by) % ctx) for i in range(ctx)])]
    psum x1, waiting for transfers between devices: 0.01 us -> 11.8 us  [per_device(): grad_up_out, grad_w_down = lax.psum((grad_up_out, grad_w_down), 'ctx')]
    ppermute x1, starting transfers between devices: 61.6 us -> 51.4 us  [scatter_pairs(): got = lax.ppermute(sent, 'fsdp', [(i, i ^ 1) for i in range(fsdp)])]
    unnamed x162 -> x179, local copies, waits for them, and re-layouts: 46.5 us -> 37.3 us
    pallas_call x0 -> x1, Pallas kernels: none -> 8.94 us  [join_product(): pl.pallas_call(join_kernel, out_shape=jax.ShapeDtypeStruct((span, width),...]
    reduce_scatter x2, waiting for transfers between devices: 57.2 us -> 64.7 us  [scatter_rows(): lax.psum_scatter(array.astype(jnp.bfloat16), 'fsdp', scatter_dimension=0,...]
  transfers between devices with their start and end apart: 41 -> 44, of which waited for: 10 -> 14; matrix products, arithmetic and copies ran while one was open for 26% -> 24% of each run, Pallas kernels for 14% -> 16%
where the time goes in v4:
time: 579 us; the launch traced here: 569 us
  waiting for transfers between devices  165 us (28%)
  starting transfers between devices  122 us (21%)
  Pallas kernels  89 us (15%)
  matrix products  82.4 us (14%)
  other arithmetic  47.9 us (8%)
  local copies, waits for them, and re-layouts  46.6 us (8%)
  between operations  16.5 us (3%)
    ppermute x33, waiting for transfers between devices, shift(): return lax.ppermute(array, 'ctx', [(i, (i + by) % ctx) for i in range(ctx)])  82.6 us
    dot_general x14, matrix products, product(): return jnp.einsum(equation, left, right, preferred_element_type=jnp.float32)  82.4 us
    reduce_scatter x2, waiting for transfers between devices, scatter_rows(): lax.psum_scatter(array.astype(jnp.bfloat16), 'fsdp', scatter_dimension=0,...  64.7 us
    ppermute x1, starting transfers between devices, scatter_pairs(): got = lax.ppermute(sent, 'fsdp', [(i, i ^ 1) for i in range(fsdp)])  51.4 us
    ppermute x33, starting transfers between devices, shift(): return lax.ppermute(array, 'ctx', [(i, (i + by) % ctx) for i in range(ctx)])  46.3 us
    unnamed x179, local copies, waits for them, and re-layouts  37.3 us
    pallas_call x2, Pallas kernels, attend_early(): pl.pallas_call(functools.partial(early_kernel, parts, heads, state is Non...  30.2 us
    pallas_call x3, Pallas kernels, attend_backward(): pl.pallas_call(functools.partial(backward_kernel, parts), grid_spec=pltpu...  25.4 us
  transfers between devices with their start and end apart: 44, of which 14 were waited for; matrix products, arithmetic and copies ran while one was open for 24% of the time, Pallas kernels for 16%

profile of v4, /device:TPU:0, one launch (start us, length us, event | category | flops | bytes accessed | tf_op | source)
XLA Modules:
  0.0 569.3 jit_solution(9396764627546250736)
XLA Ops:
  14.4 3.1 collective-permute-start
  29.0 24.9 %collective-permute-done = bf16[1024,768]{1,0:T(8,128)(2,1)S(1)} collective-permute-done((bf16[1024,768]{1,0:T(8,128)(2,1)S(1)}, bf16[1024,768]{1,0:T(8,128)(2,1)S(1)}, u32[]{:S(2)}, u32[]{:S(2)}) %collective-permute-start) | collective-permute-done | bytes 1572896 | tf_op jit(solution)/shard_map/ppermute | solution.py:400
  56.8 34.5 %collective-permute-done.1 = bf16[1024,768]{1,0:T(8,128)(2,1)} collective-permute-done((bf16[1024,768]{1,0:T(8,128)(2,1)S(1)}, bf16[1024,768]{1,0:T(8,128)(2,1)}, u32[]{:S(2)}, u32[]{:S(2)}) %collective-permute-start.1) | collective-permute-done | bytes 1572896 | tf_op jit(solution)/shard_map/ppermute | solution.py:400
  99.9 9.9 %attend_early.2 = (f32[3,1,4096]{2,1,0:T(1,128)S(1)}, f32[3,1,4096]{2,1,0:T(1,128)S(1)}, f32[3,64,4096]{2,1,0:T(8,128)S(1)}) custom-call(s32[75]{0:T(128)S(1)} %concatenate.40.table, bf16[576,1024]{1,0:T(8,128)(2,1)S(1)} %convolution_convert_fusion.7.refs_0_.refs_4_.refs_8_, bf16[576,1024]{1,0:T(8,128)(2,1)S(1)} %convolution_convert_fusion.6.refs_1_.refs_5_.refs_9_), custom_call_target="tpu_custom_call" | custom-call | flops 20000000000 | bytes 4000000 | tf_op jit(solution)/shard_map/attend_early/pallas_call | solution.py:292
  118.2 20.3 %attend_early.3 = (f32[3,1,4096]{2,1,0:T(1,128)S(1)}, f32[3,1,4096]{2,1,0:T(1,128)S(1)}, f32[3,64,4096]{2,1,0:T(8,128)}) custom-call(s32[75]{0:T(128)S(1)} %concatenate.41.table, bf16[576,1024]{1,0:T(8,128)(2,1)S(1)} %convolution_convert_fusion.7.refs_0_.refs_4_.refs_8_, bf16[576,1024]{1,0:T(8,128)(2,1)S(1)} %convolution_convert_fusion.6.refs_1_.refs_5_.refs_9_, ...), custom_call_target="tpu_custom_call" | custom-call | flops 20000000000 | bytes 4000000 | tf_op jit(solution)/shard_map/attend_early/pallas_call | solution.py:292
  146.8 8.1 %attend_last.3 = (bf16[64,1024]{1,0:T(8,128)(2,1)S(1)}, bf16[64,1024]{1,0:T(8,128)(2,1)S(1)}, bf16[64,1024]{1,0:T(8,128)(2,1)S(1)}, bf16[64,1024]{1,0:T(8,128)(2...) custom-call(s32[75]{0:T(128)S(1)} %concatenate.42.table, ...), custom_call_target="tpu_custom_call" | custom-call | flops 10000000000 | bytes 4000000 | tf_op jit(solution)/shard_map/attend_last/pallas_call | solution.py:318
  155.8 3.8 collective-permute-start.3
  159.7 8.3 %attend_last.4 = (bf16[64,1024]{1,0:T(8,128)(2,1)S(1)}, bf16[64,1024]{1,0:T(8,128)(2,1)S(1)}, bf16[64,1024]{1,0:T(8,128)(2,1)S(1)}, bf16[64,1024]{1,0:T(8,128)(2...) custom-call(s32[75]{0:T(128)S(1)} %concatenate.42.table, ...), custom_call_target="tpu_custom_call" | custom-call | flops 10000000000 | bytes 4000000 | tf_op jit(solution)/shard_map/attend_last/pallas_call | solution.py:318
  169.7 8.1 %attend_last.5 = (bf16[64,1024]{1,0:T(8,128)(2,1)S(1)}, bf16[64,1024]{1,0:T(8,128)(2,1)S(1)}, bf16[64,1024]{1,0:T(8,128)(2,1)S(1)}, bf16[64,1024]{1,0:T(8,128)(2...) custom-call(s32[75]{0:T(128)S(1)} %concatenate.42.table, ...), custom_call_target="tpu_custom_call" | custom-call | flops 10000000000 | bytes 4000000 | tf_op jit(solution)/shard_map/attend_last/pallas_call | solution.py:318
  177.9 4.0 collective-permute-start.5
  188.5 3.2 collective-permute-start.10
  202.5 8.2 %fusion.80 = f32[1024,3072]{1,0:T(8,128)S(1)} fusion(bf16[768,3072]{1,0:T(8,128)(2,1)} %all-gather.9.cloned.1.call-done, f32[1024,768]{1,0:T(8,128)} %copy-done.49, f32[768]{0:T(1024)S(1)} %get-tuple-element.162, f32[1024]{0:T(1024)S(1)} %fusion.68, f32[1024]{0:T(1024)S(1)} %broadcast_multiply_fusion.1), kind=kOutput, calls=%fused_computation.211 | convolution fusion | flops 4834983936 | bytes 20458496 | tf_op jit(solution)/shard_map/uj,jn->un/dot_general | solution.py:394
  210.6 4.5 copy-done.76
  215.2 8.9 %convolution_convert_fusion = bf16[3072,768]{1,0:T(8,128)(2,1)} fusion(bf16[1024,768]{1,0:T(8,128)(2,1)S(1)} %copy-done.46, f32[1024,3072]{1,0:T(8,128)S(1)} %fusion.80), kind=kOutput, calls=%fused_computation.20 | convolution fusion | flops 4862509056 | bytes 18874368 | tf_op jit(solution)/shard_map/un,uj->nj/dot_general | solution.py:394
  224.6 15.5 %fusion.6 = bf16[1024,3072]{1,0:T(8,128)(2,1)S(1)} fusion(f32[1024,3072]{1,0:T(8,128)} %copy-done.76, bf16[1024,768]{1,0:T(8,128)(2,1)} %bitcast_multiply_fusion, bf16[3072,768]{1,0:T(8,128)(2,1)} %all-gather.11.cloned.1.call-done), kind=kOutput, calls=%fused_computation.9 | convolution fusion | flops 4894752768 | bytes 25165824 | tf_op jit(solution)/shard_map/uj,nj->un/dot_general | solution.py:394
  240.1 10.0 %multiply_reduce_fusion = (f32[1024]{0:T(1024)S(1)}, f32[1024,768]{1,0:T(8,128)S(1)}) fusion(f32[1024,768]{1,0:T(8,128)S(1)} %copy-done.50, f32[768]{0:T(1024)S(1)} %get-tuple-element.162, f32[1024]{0:T(1024)S(1)} %broadcast_multiply_fusion.1, bf16[1024,3072]{1,0:T(8,128)(2,1)S(1)} %fusion.6, bf16[768,3072]{1,0:T(8,128)(2,1)} %all-gather.9.cloned.1.call-done), kind=kOutput, calls=%fused_computation.67 | convolution fusion | flops 4834982912 | bytes 17312768 | tf_op jit(solution)/shard_map/un,jn->uj/dot_general | solution.py:394
  256.8 6.3 %convolution_convert_fusion.1 = bf16[768,3072]{1,0:T(8,128)(2,1)S(1)} fusion(bf16[1024,3072]{1,0:T(8,128)(2,1)S(1)} %bitcast.125, f32[1024,768]{1,0:T(8,128)S(1)} %copy-done.50, f32[768]{0:T(1024)S(1)} %get-tuple-element.162, f32[1024]{0:T(1024)S(1)} %fusion.68, f32[1024]{0:T(1024)S(1)} %broadcast_multiply_fusion.1), kind=kOutput, calls=%fused_computation.21 | convolution fusion | flops 4837343232 | bytes 14167040 | tf_op jit(solution)/shard_map/uj,un->jn/dot_general | solution.py:394
  263.1 3.1 pad_maximum_fusion
  278.4 12.9 %fusion.47 = bf16[1,1024,768]{2,1,0:T(8,128)(2,1)} fusion(f32[1024,768]{1,0:T(8,128)S(1)} %copy-done.51, bf16[3072,768]{1,0:T(8,128)(2,1)} %all-gather.11.cloned.1.call-done, f32[1024,3072]{1,0:T(8,128)} %copy-done.76), kind=kOutput, calls=%fused_computation.84 | convolution fusion | flops 4861722624 | bytes 22020096 | tf_op jit(solution)/shard_map/un,nj->uj/dot_general | solution.py:394
  295.7 8.4 %attend_backward.3 = (bf16[192,1024]{1,0:T(8,128)(2,1)S(1)}, bf16[192,1024]{1,0:T(8,128)(2,1)}, bf16[192,1024]{1,0:T(8,128)(2,1)S(1)}, bf16[192,1024]{1,0:T(8,128)(2,1)S(1)}, bf16[192,4096]{1,0:T(8,128)(2,1)S(1)}) custom-call(s32[9]{0:T(128)S(1)} %pad_add_fusion.table, bf16[576,1024]{1,0:T(8,128)(2,1)S(1)} %copy-done.15, bf16[576,1024]{1,0:T(8,128)(2,1)S(1)} %copy-done.18, ...), custom_call_target="tpu_custom_call" | custom-call | flops 40000000000 | bytes 6000000 | tf_op jit(solution)/shard_map/attend_backward/pallas_call | solution.py:352
  307.8 63.0 %reduce-scatter.3.cloned.1.call-done = bf16[96,3840]{1,0:T(8,128)(2,1)} async-done(((bf16[768,3840]{1,0:T(8,128)(2,1)}), bf16[96,3840]{1,0:T(8,128)(2,1)}) %reduce-scatter.3.cloned.1.call-update) | async-done | bytes 737296 | tf_op jit(solution)/shard_map/reduce_scatter | solution.py:414
  371.5 3.3 collective-permute-start.20
  386.6 8.4 %attend_backward.4 = (bf16[192,1024]{1,0:T(8,128)(2,1)S(1)}, bf16[192,1024]{1,0:T(8,128)(2,1)}, bf16[192,1024]{1,0:T(8,128)(2,1)S(1)}, bf16[192,1024]{1,0:T(8,128)(2,1)S(1)}, bf16[192,4096]{1,0:T(8,128)(2,1)S(1)}) custom-call(s32[9]{0:T(128)S(1)} %pad_add_fusion.table, bf16[576,1024]{1,0:T(8,128)(2,1)S(1)} %copy-done.16, bf16[576,1024]{1,0:T(8,128)(2,1)S(1)} %copy-done.19, ...), custom_call_target="tpu_custom_call" | custom-call | flops 40000000000 | bytes 6000000 | tf_op jit(solution)/shard_map/attend_backward/pallas_call | solution.py:352
  400.9 8.5 %attend_backward.5 = (bf16[192,1024]{1,0:T(8,128)(2,1)S(1)}, bf16[192,1024]{1,0:T(8,128)(2,1)}, bf16[192,1024]{1,0:T(8,128)(2,1)S(1)}, bf16[192,1024]{1,0:T(8,128)(2,1)S(1)}, bf16[192,4096]{1,0:T(8,128)(2,1)S(1)}) custom-call(s32[9]{0:T(128)S(1)} %pad_add_fusion.table, bf16[576,1024]{1,0:T(8,128)(2,1)S(1)} %copy-done.16, bf16[576,1024]{1,0:T(8,128)(2,1)S(1)} %copy-done.19, ...), custom_call_target="tpu_custom_call" | custom-call | flops 40000000000 | bytes 6000000 | tf_op jit(solution)/shard_map/attend_backward/pallas_call | solution.py:352
  418.5 9.3 %fusion.7 = f32[768,576]{1,0:T(8,128)S(1)} fusion(bf16[1024,768]{1,0:T(8,128)(2,1)} %copy-done.58, bf16[1024,768]{1,0:T(8,128)(2,1)} %copy-done.57, bf16[1024,768]{1,0:T(8,128)(2,1)} %copy-done.56, bf16[1024,768]{1,0:T(8,128)(2,1)} %copy-done.55, bf16[192,4096]{1,0:T(8,128)(2,1)} %copy-done.35, bf16[192,4096]{1,0:T(8,128)(2,1)} %copy-done.34, ...), kind=kOutput, calls=%fused_computation.11 | convolution fusion | flops 3663200256 | bytes 12779520 | tf_op jit(solution)/shard_map/uj,nu->jn/dot_general | solution.py:394
  428.0 51.4 %collective-permute-start.30 = (bf16[4,96,576]{2,1,0:T(8,128)(2,1)S(1)}, bf16[4,96,576]{2,1,0:T(8,128)(2,1)S(1)}, u32[]{:S(2)}, u32[]{:S(2)}) collective-permute-start(bf16[4,96,576]{2,1,0:T(8,128)(2,1)S(1)} %fusion.57), channel_id=1, source_target_pairs={{0,1},{1,0},{2,3},{3,2},{4,5},{5,4},{6,7},{7,6},{8,9},{9,8},{10,11... | collective-permute-start | bytes 1327112 | tf_op jit(solution)/shard_map/ppermute | solution.py:425
  479.4 8.9 %join_product.1 = f32[1024,768]{1,0:T(8,128)} custom-call(bf16[192,1024]{1,0:T(8,128)(2,1)S(1)} %copy-done.9, bf16[192,1024]{1,0:T(8,128)(2,1)S(1)} %copy-done.11, bf16[192,1024]{1,0:T(8,128)(2,1)S(1)} %copy-done.13, bf16[192,1024]{1,0:T(8,128)(2,1)S(1)} %collective-permute-done.21.refs_3_, bf16[192,1024]{1,0:T(8,128)(2,1)S(1)} %collective-permute-done.22.refs_4_, ...), custom_call_target="tpu_custom_call" | custom-call | flops 3623878656 | bytes 12000000 | tf_op jit(solution)/shard_map/join_product/pallas_call | solution.py:240
  488.4 3.1 fusion.43
  493.1 23.1 %collective-permute-start.33 = (bf16[96,576]{1,0:T(8,128)(2,1)S(1)}, bf16[96,576]{1,0:T(8,128)(2,1)S(1)}, u32[]{:S(2)}, u32[]{:S(2)}) collective-permute-start(bf16[96,576]{1,0:T(8,128)(2,1)S(1)} %get-tuple-element.198), channel_id=1, source_target_pairs={{0,6},{1,7},{2,4},{3,5},{4,2},{5,3},{6,0},{7,1},{8,14},{9,15},{10,... | collective-permute-start | bytes 331784 | tf_op jit(solution)/shard_map/ppermute | solution.py:431
  527.9 3.2 collective-permute-done.34
  531.1 10.6 %collective-permute-done.35 = bf16[96,576]{1,0:T(8,128)(2,1)S(1)} collective-permute-done((bf16[96,576]{1,0:T(8,128)(2,1)S(1)}, bf16[96,576]{1,0:T(8,128)(2,1)S(1)}, u32[]{:S(2)}, u32[]{:S(2)}) %collective-permute-start.35) | collective-permute-done | bytes 110624 | tf_op jit(solution)/shard_map/ppermute | solution.py:400
  544.6 11.8 %all-reduce.4.cloned.1.call-done = (bf16[96,3840]{1,0:T(8,128)(2,1)}, bf16[384,768]{1,0:T(8,128)(2,1)}) async-done(((bf16[96,3840]{1,0:T(8,128)(2,1)}, bf16[384,768]{1,0:T(8,128)(2,1)}), (bf16[96,3840]{1,0:T(8,128)(2,1)}, bf16[384,768]{1,0:T(8,128)(2,1)})) %all-reduce.4.cloned.1.call-update) | async-done | bytes 1327120 | tf_op jit(solution)/shard_map/psum | solution.py:527
  (358 shorter events, 142.1 us)
Async XLA Ops:
  7.2 46.8 %all-gather.7.cloned.1.call-start = ((), (), s32[]{:S(2)}) async-start(), calls=%async_computation.3 | async-start | bytes 1327104 | tf_op jit(solution)/shard_map/all_gather | solution.py:410
  7.9 83.5 %all-gather.5.cloned.1.call-start = ((), (), s32[]{:S(2)}) async-start(), calls=%async_computation.2 | async-start | bytes 4202496 | tf_op jit(solution)/shard_map/all_gather | solution.py:410
  13.6 188.9 %all-gather.9.cloned.1.call-start = ((), (), s32[]{:S(2)}) async-start(), calls=%async_computation.4 | async-start | bytes 5308416 | tf_op jit(solution)/shard_map/all_gather | solution.py:410
  14.3 210.3 %all-gather.11.cloned.1.call-start = ((), (), s32[]{:S(2)}) async-start(), calls=%async_computation.5 | async-start | bytes 5308416 | tf_op jit(solution)/shard_map/all_gather | solution.py:410
  14.4 39.5 %collective-permute-start = (bf16[1024,768]{1,0:T(8,128)(2,1)S(1)}, bf16[1024,768]{1,0:T(8,128)(2,1)S(1)}, u32[]{:S(2)}, u32[]{:S(2)}) collective-permute-start(bf16[1024,768]{1,0:T(8,128)(2,1)S(1)} %bitcast.104), channel_id=1, source_target_pairs={{0,8},{8,16},{16,24},{24,0},{1,9},{9,17},{17,25},{25,1},{2,10},{10... | collective-permute-start | bytes 4718600 | tf_op jit(solution)/shard_map/ppermute | solution.py:400
  53.9 37.5 %collective-permute-start.1 = (bf16[1024,768]{1,0:T(8,128)(2,1)S(1)}, bf16[1024,768]{1,0:T(8,128)(2,1)}, u32[]{:S(2)}, u32[]{:S(2)}) collective-permute-start(bf16[1024,768]{1,0:T(8,128)(2,1)S(1)} %collective-permute-done), channel_id=1, source_target_pairs={{0,8},{8,16},{16,24},{24,0},{1,9},{9,17},{17,25},{25,1},{2,10},{10... | collective-permute-start | bytes 4718600 | tf_op jit(solution)/shard_map/ppermute | solution.py:400
  53.9 253.9 %reduce-scatter.5.cloned.1.call-start = ((), (), s32[]{:S(2)}) async-start(), calls=%async_computation.7 | async-start | bytes 5308416 | tf_op jit(solution)/shard_map/reduce_scatter | solution.py:414
  91.3 47.1 %collective-permute-start.2 = (bf16[1024,768]{1,0:T(8,128)(2,1)}, bf16[1024,768]{1,0:T(8,128)(2,1)}, u32[]{:S(2)}, u32[]{:S(2)}) collective-permute-start(bf16[1024,768]{1,0:T(8,128)(2,1)} %collective-permute-done.1), channel_id=1, source_target_pairs={{0,8},{8,16},{16,24},{24,0},{1,9},{9,17},{17,25},{25,1},{2,10},{10... | collective-permute-start | bytes 4718600 | tf_op jit(solution)/shard_map/ppermute | solution.py:400
  155.8 27.5 %collective-permute-start.3 = (bf16[64,1024]{1,0:T(8,128)(2,1)S(1)}, bf16[64,1024]{1,0:T(8,128)(2,1)S(1)}, u32[]{:S(2)}, u32[]{:S(2)}) collective-permute-start(bf16[64,1024]{1,0:T(8,128)(2,1)S(1)} %get-tuple-element.93), channel_id=1, source_target_pairs={{0,24},{8,0},{16,8},{24,16},{1,25},{9,1},{17,9},{25,17},{2,26},{10... | collective-permute-start | bytes 393224 | tf_op jit(solution)/shard_map/ppermute | solution.py:400
  224.1 146.7 %reduce-scatter.3.cloned.1.call-start = ((), (), s32[]{:S(2)}) async-start(), calls=%async_computation.6 | async-start | bytes 6635520 | tf_op jit(solution)/shard_map/reduce_scatter | solution.py:414
  266.2 290.2 %all-reduce.4.cloned.1.call-start = ((), (), s32[]{:S(2)}) async-start(), calls=%async_computation.8 | async-start | bytes 2654208 | tf_op jit(solution)/shard_map/psum | solution.py:527
  272.5 18.9 %collective-permute-start.12 = (bf16[64,1024]{1,0:T(8,128)(2,1)S(1)}, bf16[64,1024]{1,0:T(8,128)(2,1)S(1)}, u32[]{:S(2)}, u32[]{:S(2)}) collective-permute-start(bf16[64,1024]{1,0:T(8,128)(2,1)S(1)} %get-tuple-element.195), channel_id=1, source_target_pairs={{0,8},{8,16},{16,24},{24,0},{1,9},{9,17},{17,25},{25,1},{2,10},{10... | collective-permute-start | bytes 393224 | tf_op jit(solution)/shard_map/ppermute | solution.py:400
  272.5 21.7 %collective-permute-start.13 = (bf16[64,1024]{1,0:T(8,128)(2,1)S(1)}, bf16[64,1024]{1,0:T(8,128)(2,1)S(1)}, u32[]{:S(2)}, u32[]{:S(2)}) collective-permute-start(bf16[64,1024]{1,0:T(8,128)(2,1)S(1)} %get-tuple-element.194), channel_id=1, source_target_pairs={{0,16},{8,24},{16,0},{24,8},{1,17},{9,25},{17,1},{25,9},{2,18},{10... | collective-permute-start | bytes 393224 | tf_op jit(solution)/shard_map/ppermute | solution.py:400
  274.4 19.9 %collective-permute-start.14 = (bf16[64,1024]{1,0:T(8,128)(2,1)S(1)}, bf16[64,1024]{1,0:T(8,128)(2,1)S(1)}, u32[]{:S(2)}, u32[]{:S(2)}) collective-permute-start(bf16[64,1024]{1,0:T(8,128)(2,1)S(1)} %get-tuple-element.193), channel_id=1, source_target_pairs={{0,24},{8,0},{16,8},{24,16},{1,25},{9,1},{17,9},{25,17},{2,26},{10... | collective-permute-start | bytes 393224 | tf_op jit(solution)/shard_map/ppermute | solution.py:400
  277.0 93.8 %collective-permute-start.15 = (bf16[64,1024]{1,0:T(8,128)(2,1)S(1)}, bf16[64,1024]{1,0:T(8,128)(2,1)S(1)}, u32[]{:S(2)}, u32[]{:S(2)}) collective-permute-start(bf16[64,1024]{1,0:T(8,128)(2,1)S(1)} %get-tuple-element.191), channel_id=1, source_target_pairs={{0,8},{8,16},{16,24},{24,0},{1,9},{9,17},{17,25},{25,1},{2,10},{10... | collective-permute-start | bytes 393224 | tf_op jit(solution)/shard_map/ppermute | solution.py:400
  277.1 97.7 %collective-permute-start.16 = (bf16[64,1024]{1,0:T(8,128)(2,1)S(1)}, bf16[64,1024]{1,0:T(8,128)(2,1)S(1)}, u32[]{:S(2)}, u32[]{:S(2)}) collective-permute-start(bf16[64,1024]{1,0:T(8,128)(2,1)S(1)} %get-tuple-element.190), channel_id=1, source_target_pairs={{0,16},{8,24},{16,0},{24,8},{1,17},{9,25},{17,1},{25,9},{2,18},{10... | collective-permute-start | bytes 393224 | tf_op jit(solution)/shard_map/ppermute | solution.py:400
  291.3 84.8 %collective-permute-start.17 = (bf16[64,1024]{1,0:T(8,128)(2,1)}, bf16[64,1024]{1,0:T(8,128)(2,1)S(1)}, u32[]{:S(2)}, u32[]{:S(2)}) collective-permute-start(bf16[64,1024]{1,0:T(8,128)(2,1)} %get-tuple-element.189), channel_id=1, source_target_pairs={{0,24},{8,0},{16,8},{24,16},{1,25},{9,1},{17,9},{25,17},{2,26},{10... | collective-permute-start | bytes 393224 | tf_op jit(solution)/shard_map/ppermute | solution.py:400
  294.1 102.8 %collective-permute-start.18 = (bf16[64,1024]{1,0:T(8,128)(2,1)}, bf16[64,1024]{1,0:T(8,128)(2,1)S(1)}, u32[]{:S(2)}, u32[]{:S(2)}) collective-permute-start(bf16[64,1024]{1,0:T(8,128)(2,1)} %get-tuple-element.187), channel_id=1, source_target_pairs={{0,8},{8,16},{16,24},{24,0},{1,9},{9,17},{17,25},{25,1},{2,10},{10... | collective-permute-start | bytes 393224 | tf_op jit(solution)/shard_map/ppermute | solution.py:400
  294.2 104.2 %collective-permute-start.19 = (bf16[64,1024]{1,0:T(8,128)(2,1)}, bf16[64,1024]{1,0:T(8,128)(2,1)S(1)}, u32[]{:S(2)}, u32[]{:S(2)}) collective-permute-start(bf16[64,1024]{1,0:T(8,128)(2,1)} %get-tuple-element.186), channel_id=1, source_target_pairs={{0,16},{8,24},{16,0},{24,8},{1,17},{9,25},{17,1},{25,9},{2,18},{10... | collective-permute-start | bytes 393224 | tf_op jit(solution)/shard_map/ppermute | solution.py:400
  371.5 29.4 %collective-permute-start.20 = (bf16[64,1024]{1,0:T(8,128)(2,1)}, bf16[64,1024]{1,0:T(8,128)(2,1)S(1)}, u32[]{:S(2)}, u32[]{:S(2)}) collective-permute-start(bf16[64,1024]{1,0:T(8,128)(2,1)} %get-tuple-element.185), channel_id=1, source_target_pairs={{0,24},{8,0},{16,8},{24,16},{1,25},{9,1},{17,9},{25,17},{2,26},{10... | collective-permute-start | bytes 393224 | tf_op jit(solution)/shard_map/ppermute | solution.py:400
  375.4 39.4 %collective-permute-start.21 = (bf16[192,1024]{1,0:T(8,128)(2,1)}, bf16[192,1024]{1,0:T(8,128)(2,1)S(1)}, u32[]{:S(2)}, u32[]{:S(2)}) collective-permute-start(bf16[192,1024]{1,0:T(8,128)(2,1)} %get-tuple-element.116), channel_id=1, source_target_pairs={{0,24},{8,0},{16,8},{24,16},{1,25},{9,1},{17,9},{25,17},{2,26},{10... | collective-permute-start | bytes 1179656 | tf_op jit(solution)/shard_map/ppermute | solution.py:400
  376.8 38.1 %collective-permute-start.24 = (bf16[192,1024]{1,0:T(8,128)(2,1)S(1)}, bf16[192,1024]{1,0:T(8,128)(2,1)S(1)}, u32[]{:S(2)}, u32[]{:S(2)}) collective-permute-start(bf16[192,1024]{1,0:T(8,128)(2,1)S(1)} %get-tuple-element.119), channel_id=1, source_target_pairs={{0,16},{8,24},{16,0},{24,8},{1,17},{9,25},{17,1},{25,9},{2,18},{10... | collective-permute-start | bytes 1179656 | tf_op jit(solution)/shard_map/ppermute | solution.py:400
  397.0 20.9 %collective-permute-start.27 = (bf16[192,1024]{1,0:T(8,128)(2,1)S(1)}, bf16[192,1024]{1,0:T(8,128)(2,1)S(1)}, u32[]{:S(2)}, u32[]{:S(2)}) collective-permute-start(bf16[192,1024]{1,0:T(8,128)(2,1)S(1)} %get-tuple-element.122), channel_id=1, source_target_pairs={{0,8},{8,16},{16,24},{24,0},{1,9},{9,17},{17,25},{25,1},{2,10},{10... | collective-permute-start | bytes 1179656 | tf_op jit(solution)/shard_map/ppermute | solution.py:400
  398.4 19.5 %collective-permute-start.22 = (bf16[192,1024]{1,0:T(8,128)(2,1)}, bf16[192,1024]{1,0:T(8,128)(2,1)S(1)}, u32[]{:S(2)}, u32[]{:S(2)}) collective-permute-start(bf16[192,1024]{1,0:T(8,128)(2,1)} %get-tuple-element.117), channel_id=1, source_target_pairs={{0,24},{8,0},{16,8},{24,16},{1,25},{9,1},{17,9},{25,17},{2,26},{10... | collective-permute-start | bytes 1179656 | tf_op jit(solution)/shard_map/ppermute | solution.py:400
  414.9 64.4 %collective-permute-start.25 = (bf16[192,1024]{1,0:T(8,128)(2,1)S(1)}, bf16[192,1024]{1,0:T(8,128)(2,1)S(1)}, u32[]{:S(2)}, u32[]{:S(2)}) collective-permute-start(bf16[192,1024]{1,0:T(8,128)(2,1)S(1)} %get-tuple-element.120), channel_id=1, source_target_pairs={{0,16},{8,24},{16,0},{24,8},{1,17},{9,25},{17,1},{25,9},{2,18},{10... | collective-permute-start | bytes 1179656 | tf_op jit(solution)/shard_map/ppermute | solution.py:400
  415.0 64.3 %collective-permute-start.26 = (bf16[192,1024]{1,0:T(8,128)(2,1)}, bf16[192,1024]{1,0:T(8,128)(2,1)S(1)}, u32[]{:S(2)}, u32[]{:S(2)}) collective-permute-start(bf16[192,1024]{1,0:T(8,128)(2,1)} %copy-done.1), channel_id=1, source_target_pairs={{0,16},{8,24},{16,0},{24,8},{1,17},{9,25},{17,1},{25,9},{2,18},{10... | collective-permute-start | bytes 1179656 | tf_op jit(solution)/shard_map/ppermute | solution.py:400
  417.9 61.4 %collective-permute-start.28 = (bf16[192,1024]{1,0:T(8,128)(2,1)S(1)}, bf16[192,1024]{1,0:T(8,128)(2,1)S(1)}, u32[]{:S(2)}, u32[]{:S(2)}) collective-permute-start(bf16[192,1024]{1,0:T(8,128)(2,1)S(1)} %get-tuple-element.123), channel_id=1, source_target_pairs={{0,8},{8,16},{16,24},{24,0},{1,9},{9,17},{17,25},{25,1},{2,10},{10... | collective-permute-start | bytes 1179656 | tf_op jit(solution)/shard_map/ppermute | solution.py:400
  417.9 61.4 %collective-permute-start.29 = (bf16[192,1024]{1,0:T(8,128)(2,1)}, bf16[192,1024]{1,0:T(8,128)(2,1)S(1)}, u32[]{:S(2)}, u32[]{:S(2)}) collective-permute-start(bf16[192,1024]{1,0:T(8,128)(2,1)} %copy-done), channel_id=1, source_target_pairs={{0,8},{8,16},{16,24},{24,0},{1,9},{9,17},{17,25},{25,1},{2,10},{10... | collective-permute-start | bytes 1179656 | tf_op jit(solution)/shard_map/ppermute | solution.py:400
  428.0 64.9 %collective-permute-start.30 = (bf16[4,96,576]{2,1,0:T(8,128)(2,1)S(1)}, bf16[4,96,576]{2,1,0:T(8,128)(2,1)S(1)}, u32[]{:S(2)}, u32[]{:S(2)}) collective-permute-start(bf16[4,96,576]{2,1,0:T(8,128)(2,1)S(1)} %fusion.57), channel_id=1, source_target_pairs={{0,1},{1,0},{2,3},{3,2},{4,5},{5,4},{6,7},{7,6},{8,9},{9,8},{10,11... | collective-permute-start | bytes 1327112 | tf_op jit(solution)/shard_map/ppermute | solution.py:425
  493.1 25.9 %collective-permute-start.33 = (bf16[96,576]{1,0:T(8,128)(2,1)S(1)}, bf16[96,576]{1,0:T(8,128)(2,1)S(1)}, u32[]{:S(2)}, u32[]{:S(2)}) collective-permute-start(bf16[96,576]{1,0:T(8,128)(2,1)S(1)} %get-tuple-element.198), channel_id=1, source_target_pairs={{0,6},{1,7},{2,4},{3,5},{4,2},{5,3},{6,0},{7,1},{8,14},{9,15},{10,... | collective-permute-start | bytes 331784 | tf_op jit(solution)/shard_map/ppermute | solution.py:431
  524.1 17.6 %collective-permute-start.35 = (bf16[96,576]{1,0:T(8,128)(2,1)S(1)}, bf16[96,576]{1,0:T(8,128)(2,1)S(1)}, u32[]{:S(2)}, u32[]{:S(2)}) collective-permute-start(bf16[96,576]{1,0:T(8,128)(2,1)S(1)} %get-tuple-element.180), channel_id=1, source_target_pairs={{0,16},{8,24},{16,0},{24,8},{1,17},{9,25},{17,1},{25,9},{2,18},{10... | collective-permute-start | bytes 331784 | tf_op jit(solution)/shard_map/ppermute | solution.py:400
  525.9 15.8 %collective-permute-start.36 = (bf16[96,576]{1,0:T(8,128)(2,1)S(1)}, bf16[96,576]{1,0:T(8,128)(2,1)S(1)}, u32[]{:S(2)}, u32[]{:S(2)}) collective-permute-start(bf16[96,576]{1,0:T(8,128)(2,1)S(1)} %get-tuple-element.180), channel_id=1, source_target_pairs={{0,8},{8,16},{16,24},{24,0},{1,9},{9,17},{17,25},{25,1},{2,10},{10... | collective-permute-start | bytes 331784 | tf_op jit(solution)/shard_map/ppermute | solution.py:400
  (91 other events, 1053.7 us)
Sparse Core Ops, SparseCore 0:
  9.9 26.6 all-gather.6
  39.0 34.6 all-gather.4
  75.6 38.7 all-gather.8
  116.2 38.8 all-gather.10
  224.2 83.4 reduce-scatter.4
  311.1 59.6 reduce-scatter.2
  415.0 141.3 all-reduce.3

commit v5 on v4

--- a/solution.py
+++ b/solution.py
@@ -241,7 +241,7 @@
         join_kernel,
         out_shape=jax.ShapeDtypeStruct((span, width), jnp.float32),
         scratch_shapes=[pltpu.VMEM((total, span), jnp.bfloat16)],
-        compiler_params=pltpu.CompilerParams(vmem_limit_bytes=48 << 20),
+        compiler_params=pltpu.CompilerParams(vmem_limit_bytes=62 << 20),
         cost_estimate=pl.CostEstimate(
             flops=2 * span * width * total, bytes_accessed=12_000_000, transcendentals=0
         ),
@@ -304,7 +304,7 @@
             ],
         ),
         out_shape=[jax.ShapeDtypeStruct(shape, jnp.float32) for shape in shapes],
-        compiler_params=pltpu.CompilerParams(vmem_limit_bytes=48 << 20),
+        compiler_params=pltpu.CompilerParams(vmem_limit_bytes=62 << 20),
         cost_estimate=pl.CostEstimate(flops=20_000_000_000, bytes_accessed=4_000_000, transcendentals=0),
         name="attend_early",
     )(table, *packed_list, *([] if state is None else state))
@@ -338,7 +338,7 @@
             jax.ShapeDtypeStruct((HEAD_DIM, slots), jnp.float32),
             jax.ShapeDtypeStruct((1, slots), jnp.float32),
         ],
-        compiler_params=pltpu.CompilerParams(vmem_limit_bytes=40 << 20),
+        compiler_params=pltpu.CompilerParams(vmem_limit_bytes=62 << 20),
         cost_estimate=pl.CostEstimate(flops=10_000_000_000, bytes_accessed=4_000_000, transcendentals=0),
         name="attend_last",
     )(table, *packed_list, *packed_list, *packed_list, *state)
@@ -357,7 +357,7 @@
             in_specs=head_specs(parts, span, 3 * head)
             + head_specs(parts, span, 3 * head + 1)
             + head_specs(parts, span, 3 * head + 2)
-            + [whole((HEAD_DIM, span))] * parts
+            + head_specs(parts, span, max(head - 1, 0))
             + [whole((HEAD_DIM, slots)), whole((1, slots))],
             out_specs=[whole((three, span))] * parts + [whole((three, slots))],
             scratch_shapes=[pltpu.VMEM((HEAD_DIM, slots), jnp.bfloat16)] * 4
@@ -373,7 +373,7 @@
         ),
         out_shape=[jax.ShapeDtypeStruct((three, span), jnp.bfloat16)] * parts
         + [jax.ShapeDtypeStruct((three, slots), jnp.bfloat16)],
-        compiler_params=pltpu.CompilerParams(vmem_limit_bytes=40 << 20),
+        compiler_params=pltpu.CompilerParams(vmem_limit_bytes=62 << 20),
         cost_estimate=pl.CostEstimate(flops=40_000_000_000, bytes_accessed=6_000_000, transcendentals=0),
         name="attend_backward",
     )(table, *packed_list, *packed_list, *packed_list, *grad_list, exact, logs)
@@ -498,14 +498,15 @@
     grad_middle = grad_z.astype(jnp.float32) + norm_two_back(grad_normed_two)[0]
     grad_branch = grad_middle.astype(jnp.bfloat16)
     grad_mixed_t = product("nj,uj->nu", w_out_turned, grad_branch).astype(jnp.bfloat16)
-    grads_by_head = []
-    for head in range(heads_here):
-        pieces = []
-        for part in range(ctx):
-            row = (head * ctx + part) * HEAD_DIM
-            piece = grad_mixed_t[row : row + HEAD_DIM]
-            pieces.append(shift(piece, ctx, part))
-        grads_by_head.append(pieces)
+    count = ctx * HEAD_DIM
+    grads_by_head = [[] for _ in range(heads_here)]
+    for part in range(ctx):
+        rows = [head * count + part * HEAD_DIM for head in range(heads_here)]
+        pieces = [grad_mixed_t[row : row + HEAD_DIM] for row in rows]
+        grads_by_head[0].append(shift(pieces[0], ctx, part))
+        others = shift(jnp.concatenate(pieces[1:], axis=0), ctx, part)
+        for head in range(1, heads_here):
+            grads_by_head[head].append(others)
 
     grad_w_down = product("un,uj->nj", activation, grad_z).astype(jnp.bfloat16)
     grad_w_up = product("uj,un->jn", normed_two, grad_pre).astype(jnp.bfloat16)

time: 579 us -> 581 us (level)
  Pallas kernels: 89 us -> 114 us
  local copies, waits for them, and re-layouts: 46.6 us -> 31 us
  waiting for transfers between devices: 165 us -> 158 us
    unnamed x179 -> x129, local copies, waits for them, and re-layouts: 37.3 us -> 20.4 us
    pallas_call x3, Pallas kernels: 24.5 us -> 34.1 us  [attend_last(): pl.pallas_call(functools.partial(last_kernel, parts), grid_spec=pltpu.Pre...]
    pallas_call x3, Pallas kernels: 25.4 us -> 34.5 us  [attend_backward(): pl.pallas_call(functools.partial(backward_kernel, parts), grid_spec=pltpu...]
    ppermute x33 -> x30, starting transfers between devices: 46.3 us -> 41 us  [shift(): return lax.ppermute(array, 'ctx', [(i, (i + by) % ctx) for i in range(ctx)])]
    ppermute x33 -> x30, waiting for transfers between devices: 82.6 us -> 81.2 us  [shift(): return lax.ppermute(array, 'ctx', [(i, (i + by) % ctx) for i in range(ctx)])]
  transfers between devices with their start and end apart: 44 -> 41, of which waited for: 14 -> 14; matrix products, arithmetic and copies ran while one was open for 24% -> 25% of each run, Pallas kernels for 16% -> 20%
where the time goes in v5:
time: 581 us; the launch traced here: 571 us
  waiting for transfers between devices  158 us (27%)
  starting transfers between devices  117 us (20%)
  Pallas kernels  114 us (20%)
  matrix products  86.9 us (15%)
  other arithmetic  48.5 us (8%)
  local copies, waits for them, and re-layouts  31 us (5%)
  between operations  16.1 us (3%)
    dot_general x14, matrix products, product(): return jnp.einsum(equation, left, right, preferred_element_type=jnp.float32)  86.9 us
    ppermute x30, waiting for transfers between devices, shift(): return lax.ppermute(array, 'ctx', [(i, (i + by) % ctx) for i in range(ctx)])  81.2 us
    reduce_scatter x2, waiting for transfers between devices, scatter_rows(): lax.psum_scatter(array.astype(jnp.bfloat16), 'fsdp', scatter_dimension=0,...  65 us
    ppermute x1, starting transfers between devices, scatter_pairs(): got = lax.ppermute(sent, 'fsdp', [(i, i ^ 1) for i in range(fsdp)])  52 us
    ppermute x30, starting transfers between devices, shift(): return lax.ppermute(array, 'ctx', [(i, (i + by) % ctx) for i in range(ctx)])  41 us
    pallas_call x2, Pallas kernels, attend_early(): pl.pallas_call(functools.partial(early_kernel, parts, heads, state is Non...  35.1 us
    pallas_call x3, Pallas kernels, attend_backward(): pl.pallas_call(functools.partial(backward_kernel, parts), grid_spec=pltpu...  34.5 us
    pallas_call x3, Pallas kernels, attend_last(): pl.pallas_call(functools.partial(last_kernel, parts), grid_spec=pltpu.Pre...  34.1 us
  transfers between devices with their start and end apart: 41, of which 14 were waited for; matrix products, arithmetic and copies ran while one was open for 25% of the time, Pallas kernels for 20%

profile of v5, /device:TPU:0, one launch (start us, length us, event | category | flops | bytes accessed | tf_op | source)
XLA Modules:
  0.0 571.3 jit_solution(2659183117287616722)
XLA Ops:
  28.7 23.3 %collective-permute-done = bf16[1024,768]{1,0:T(8,128)(2,1)S(1)} collective-permute-done((bf16[1024,768]{1,0:T(8,128)(2,1)S(1)}, bf16[1024,768]{1,0:T(8,128)(2,1)S(1)}, u32[]{:S(2)}, u32[]{:S(2)}) %collective-permute-start) | collective-permute-done | bytes 1572896 | tf_op jit(solution)/shard_map/ppermute | solution.py:400
  54.9 34.5 %collective-permute-done.1 = bf16[1024,768]{1,0:T(8,128)(2,1)} collective-permute-done((bf16[1024,768]{1,0:T(8,128)(2,1)S(1)}, bf16[1024,768]{1,0:T(8,128)(2,1)}, u32[]{:S(2)}, u32[]{:S(2)}) %collective-permute-start.1) | collective-permute-done | bytes 1572896 | tf_op jit(solution)/shard_map/ppermute | solution.py:400
  100.0 13.4 %attend_early.2 = (f32[3,1,4096]{2,1,0:T(1,128)}, f32[3,1,4096]{2,1,0:T(1,128)}, f32[3,64,4096]{2,1,0:T(8,128)}) custom-call(s32[75]{0:T(128)} %concatenate.52.table, bf16[576,1024]{1,0:T(8,128)(2,1)} %convolution_convert_fusion.7.refs_0_.refs_4_.refs_8_, bf16[576,1024]{1,0:T(8,128)(2,1)} %convolution_convert_fusion.6.refs_1_.refs_5_.refs_9_), custom_call_target="tpu_custom_call" | custom-call | flops 20000000000 | bytes 4000000 | tf_op jit(solution)/shard_map/attend_early/pallas_call | solution.py:292
  120.2 3.6 convolution_convert_fusion.5.refs_2_.refs_6_.refs_10_
  123.8 21.7 %attend_early.3 = (f32[3,1,4096]{2,1,0:T(1,128)}, f32[3,1,4096]{2,1,0:T(1,128)}, f32[3,64,4096]{2,1,0:T(8,128)}) custom-call(s32[75]{0:T(128)} %concatenate.53.table, bf16[576,1024]{1,0:T(8,128)(2,1)} %convolution_convert_fusion.7.refs_0_.refs_4_.refs_8_, bf16[576,1024]{1,0:T(8,128)(2,1)} %convolution_convert_fusion.6.refs_1_.refs_5_.refs_9_, ...), custom_call_target="tpu_custom_call" | custom-call | flops 20000000000 | bytes 4000000 | tf_op jit(solution)/shard_map/attend_early/pallas_call | solution.py:292
  152.4 3.6 convolution_convert_fusion.4.refs_3_.refs_7_.refs_11_
  156.0 11.1 %attend_last.3 = (bf16[64,1024]{1,0:T(8,128)(2,1)}, bf16[64,1024]{1,0:T(8,128)(2,1)}, bf16[64,1024]{1,0:T(8,128)(2,1)}, bf16[64,1024]{1,0:T(8,128)(2,1)}, f32[64,4096]{1,0:T(8,128)}, /*index=5*/f32[1,4096]{1,0:T(1,128)}) custom-call(s32[75]{0:T(128)} %concatenate.54.table, bf16[576,1024]{1,0:T(8,128)(2,1)} %convolution_convert_fusion.7.refs_0_.refs_4_.refs_8_, ...), custom_call_target="tpu_custom_call" | custom-call | flops 10000000000 | bytes 4000000 | tf_op jit(solution)/shard_map/attend_last/pallas_call | solution.py:318
  167.1 3.9 collective-permute-start.3
  171.0 11.7 %attend_last.4 = (bf16[64,1024]{1,0:T(8,128)(2,1)}, bf16[64,1024]{1,0:T(8,128)(2,1)}, bf16[64,1024]{1,0:T(8,128)(2,1)}, bf16[64,1024]{1,0:T(8,128)(2,1)}, f32[64,4096]{1,0:T(8,128)}, /*index=5*/f32[1,4096]{1,0:T(1,128)}) custom-call(s32[75]{0:T(128)} %concatenate.54.table, bf16[576,1024]{1,0:T(8,128)(2,1)} %convolution_convert_fusion.7.refs_0_.refs_4_.refs_8_, ...), custom_call_target="tpu_custom_call" | custom-call | flops 10000000000 | bytes 4000000 | tf_op jit(solution)/shard_map/attend_last/pallas_call | solution.py:318
  182.7 11.3 %attend_last.5 = (bf16[64,1024]{1,0:T(8,128)(2,1)}, bf16[64,1024]{1,0:T(8,128)(2,1)}, bf16[64,1024]{1,0:T(8,128)(2,1)}, bf16[64,1024]{1,0:T(8,128)(2,1)}, f32[64,4096]{1,0:T(8,128)}, /*index=5*/f32[1,4096]{1,0:T(1,128)}) custom-call(s32[75]{0:T(128)} %concatenate.54.table, bf16[576,1024]{1,0:T(8,128)(2,1)} %convolution_convert_fusion.7.refs_0_.refs_4_.refs_8_, ...), custom_call_target="tpu_custom_call" | custom-call | flops 10000000000 | bytes 4000000 | tf_op jit(solution)/shard_map/attend_last/pallas_call | solution.py:318
  194.1 4.0 collective-permute-start.5
  204.4 3.4 collective-permute-start.11
  210.0 4.2 collective-permute-done.10
  218.2 8.2 %fusion.80 = f32[1024,3072]{1,0:T(8,128)S(1)} fusion(bf16[768,3072]{1,0:T(8,128)(2,1)} %all-gather.9.cloned.1.call-done, f32[1024,768]{1,0:T(8,128)} %copy-done.7, f32[768]{0:T(1024)S(1)} %get-tuple-element.162, f32[1024]{0:T(1024)S(1)} %fusion.68, f32[1024]{0:T(1024)S(1)} %broadcast_multiply_fusion.1), kind=kOutput, calls=%fused_computation.215 | convolution fusion | flops 4834983936 | bytes 20458496 | tf_op jit(solution)/shard_map/uj,jn->un/dot_general | solution.py:394
  226.4 4.5 copy-done.51
  230.9 8.9 %convolution_convert_fusion = bf16[3072,768]{1,0:T(8,128)(2,1)} fusion(bf16[1024,768]{1,0:T(8,128)(2,1)S(1)} %copy-done.5, f32[1024,3072]{1,0:T(8,128)S(1)} %fusion.80), kind=kOutput, calls=%fused_computation.20 | convolution fusion | flops 4862509056 | bytes 18874368 | tf_op jit(solution)/shard_map/un,uj->nj/dot_general | solution.py:394
  240.1 14.1 %fusion.6 = bf16[1024,3072]{1,0:T(8,128)(2,1)S(1)} fusion(f32[1024,3072]{1,0:T(8,128)} %copy-done.51, bf16[1024,768]{1,0:T(8,128)(2,1)S(1)} %copy-done.5, bf16[3072,768]{1,0:T(8,128)(2,1)} %all-gather.11.cloned.1.call-done), kind=kOutput, calls=%fused_computation.9 | convolution fusion | flops 4894752768 | bytes 25165824 | tf_op jit(solution)/shard_map/uj,nj->un/dot_general | solution.py:394
  254.2 10.0 %multiply_reduce_fusion = (f32[1024]{0:T(1024)S(1)}, f32[1024,768]{1,0:T(8,128)S(1)}) fusion(f32[1024,768]{1,0:T(8,128)S(1)} %copy-done.8, f32[768]{0:T(1024)S(1)} %get-tuple-element.162, f32[1024]{0:T(1024)S(1)} %broadcast_multiply_fusion.1, bf16[1024,3072]{1,0:T(8,128)(2,1)S(1)} %fusion.6, bf16[768,3072]{1,0:T(8,128)(2,1)} %all-gather.9.cloned.1.call-done), kind=kOutput, calls=%fused_computation.67 | convolution fusion | flops 4834982912 | bytes 17312768 | tf_op jit(solution)/shard_map/un,jn->uj/dot_general | solution.py:394
  270.8 6.3 %convolution_convert_fusion.1 = bf16[768,3072]{1,0:T(8,128)(2,1)S(1)} fusion(bf16[1024,3072]{1,0:T(8,128)(2,1)S(1)} %bitcast.125, f32[1024,768]{1,0:T(8,128)S(1)} %copy-done.8, f32[768]{0:T(1024)S(1)} %get-tuple-element.162, f32[1024]{0:T(1024)S(1)} %fusion.68, f32[1024]{0:T(1024)S(1)} %broadcast_multiply_fusion.1), kind=kOutput, calls=%fused_computation.21 | convolution fusion | flops 4837343232 | bytes 14167040 | tf_op jit(solution)/shard_map/uj,un->jn/dot_general | solution.py:394
  293.0 12.9 %fusion.47 = bf16[1,1024,768]{2,1,0:T(8,128)(2,1)} fusion(f32[1024,768]{1,0:T(8,128)S(1)} %copy-done.9, bf16[3072,768]{1,0:T(8,128)(2,1)} %all-gather.11.cloned.1.call-done, f32[1024,3072]{1,0:T(8,128)} %copy-done.51), kind=kOutput, calls=%fused_computation.84 | convolution fusion | flops 4861722624 | bytes 22020096 | tf_op jit(solution)/shard_map/un,nj->uj/dot_general | solution.py:394
  306.7 3.4 collective-permute-start.17
  310.8 11.4 %attend_backward.3 = (bf16[192,1024]{1,0:T(8,128)(2,1)}, bf16[192,1024]{1,0:T(8,128)(2,1)}, bf16[192,1024]{1,0:T(8,128)(2,1)}, bf16[192,1024]{1,0:T(8,128)(2,1)}, bf16[192,4096]{1,0:T(8,128)(2,1)}) custom-call(s32[9]{0:T(128)} %pad_add_fusion.table, bf16[576,1024]{1,0:T(8,128)(2,1)} %convolution_convert_fusion.7.refs_0_.refs_4_.refs_8_, ...), custom_call_target="tpu_custom_call" | custom-call | flops 40000000000 | bytes 6000000 | tf_op jit(solution)/shard_map/attend_backward/pallas_call | solution.py:352
  324.5 63.0 %reduce-scatter.3.cloned.1.call-done = bf16[96,3840]{1,0:T(8,128)(2,1)} async-done(((bf16[768,3840]{1,0:T(8,128)(2,1)}), bf16[96,3840]{1,0:T(8,128)(2,1)}) %reduce-scatter.3.cloned.1.call-update) | async-done | bytes 737296 | tf_op jit(solution)/shard_map/reduce_scatter | solution.py:414
  389.8 11.5 %attend_backward.4 = (bf16[192,1024]{1,0:T(8,128)(2,1)}, bf16[192,1024]{1,0:T(8,128)(2,1)}, bf16[192,1024]{1,0:T(8,128)(2,1)}, bf16[192,1024]{1,0:T(8,128)(2,1)}, bf16[192,4096]{1,0:T(8,128)(2,1)}) custom-call(s32[9]{0:T(128)} %pad_add_fusion.table, bf16[576,1024]{1,0:T(8,128)(2,1)} %convolution_convert_fusion.7.refs_0_.refs_4_.refs_8_, ...), custom_call_target="tpu_custom_call" | custom-call | flops 40000000000 | bytes 6000000 | tf_op jit(solution)/shard_map/attend_backward/pallas_call | solution.py:352
  404.1 11.6 %attend_backward.5 = (bf16[192,1024]{1,0:T(8,128)(2,1)}, bf16[192,1024]{1,0:T(8,128)(2,1)}, bf16[192,1024]{1,0:T(8,128)(2,1)}, bf16[192,1024]{1,0:T(8,128)(2,1)}, bf16[192,4096]{1,0:T(8,128)(2,1)}) custom-call(s32[9]{0:T(128)} %pad_add_fusion.table, bf16[576,1024]{1,0:T(8,128)(2,1)} %convolution_convert_fusion.7.refs_0_.refs_4_.refs_8_, ...), custom_call_target="tpu_custom_call" | custom-call | flops 40000000000 | bytes 6000000 | tf_op jit(solution)/shard_map/attend_backward/pallas_call | solution.py:352
  420.9 8.8 %fusion.7 = f32[768,576]{1,0:T(8,128)S(1)} fusion(bf16[1024,768]{1,0:T(8,128)(2,1)} %copy-done.16, bf16[1024,768]{1,0:T(8,128)(2,1)} %copy-done.15, bf16[1024,768]{1,0:T(8,128)(2,1)} %copy-done.14, bf16[1024,768]{1,0:T(8,128)(2,1)S(1)} %copy-done.13, bf16[192,4096]{1,0:T(8,128)(2,1)} %get-tuple-element.127, bf16[192,4096]{1,0:T(8,128)(2,1)} %get-tuple-element.126, ...), kind=kOutput, calls=%fused_computation.11 | convolution fusion | flops 3663200256 | bytes 12779520 | tf_op jit(solution)/shard_map/uj,nu->jn/dot_general | solution.py:394
  430.6 52.0 %collective-permute-start.27 = (bf16[4,96,576]{2,1,0:T(8,128)(2,1)}, bf16[4,96,576]{2,1,0:T(8,128)(2,1)}, u32[]{:S(2)}, u32[]{:S(2)}) collective-permute-start(bf16[4,96,576]{2,1,0:T(8,128)(2,1)} %fusion.57), channel_id=1, source_target_pairs={{0,1},{1,0},{2,3},{3,2},{4,5},{5,4},{6,7},{7,6},{8,9},{9,8},{10,11... | collective-permute-start | bytes 1327112 | tf_op jit(solution)/shard_map/ppermute | solution.py:425
  483.8 10.2 %join_product.1 = f32[1024,768]{1,0:T(8,128)} custom-call(bf16[192,1024]{1,0:T(8,128)(2,1)} %get-tuple-element.108.refs_0_, bf16[192,1024]{1,0:T(8,128)(2,1)} %get-tuple-element.112.refs_1_, bf16[192,1024]{1,0:T(8,128)(2,1)} %get-tuple-element.115.refs_2_, bf16[192,1024]{1,0:T(8,128)(2,1)} %copy-done.35, bf16[192,1024]{1,0:T(8,128)(2,1)} %collective-permute-done.19.refs_4_, ...), custom_call_target="tpu_custom_call" | custom-call | flops 3623878656 | bytes 12000000 | tf_op jit(solution)/shard_map/join_product/pallas_call | solution.py:240
  500.1 22.6 %collective-permute-start.30 = (bf16[96,576]{1,0:T(8,128)(2,1)S(1)}, bf16[96,576]{1,0:T(8,128)(2,1)S(1)}, u32[]{:S(2)}, u32[]{:S(2)}) collective-permute-start(bf16[96,576]{1,0:T(8,128)(2,1)S(1)} %get-tuple-element.198), channel_id=1, source_target_pairs={{0,6},{1,7},{2,4},{3,5},{4,2},{5,3},{6,0},{7,1},{8,14},{9,15},{10,... | collective-permute-start | bytes 331784 | tf_op jit(solution)/shard_map/ppermute | solution.py:431
  534.7 3.4 collective-permute-done.31
  538.1 11.4 %collective-permute-done.32 = bf16[96,576]{1,0:T(8,128)(2,1)S(1)} collective-permute-done((bf16[96,576]{1,0:T(8,128)(2,1)S(1)}, bf16[96,576]{1,0:T(8,128)(2,1)S(1)}, u32[]{:S(2)}, u32[]{:S(2)}) %collective-permute-start.32) | collective-permute-done | bytes 110624 | tf_op jit(solution)/shard_map/ppermute | solution.py:400
  552.4 6.1 %all-reduce.4.cloned.1.call-done = (bf16[96,3840]{1,0:T(8,128)(2,1)}, bf16[384,768]{1,0:T(8,128)(2,1)}) async-done(((bf16[96,3840]{1,0:T(8,128)(2,1)}, bf16[384,768]{1,0:T(8,128)(2,1)}), (bf16[96,3840]{1,0:T(8,128)(2,1)}, bf16[384,768]{1,0:T(8,128)(2,1)})) %all-reduce.4.cloned.1.call-update) | async-done | bytes 1327120 | tf_op jit(solution)/shard_map/psum | solution.py:528
  (306 shorter events, 125.2 us)
Async XLA Ops:
  7.2 44.9 %all-gather.7.cloned.1.call-start = ((), (), s32[]{:S(2)}) async-start(), calls=%async_computation.3 | async-start | bytes 1327104 | tf_op jit(solution)/shard_map/all_gather | solution.py:410
  7.9 81.6 %all-gather.5.cloned.1.call-start = ((), (), s32[]{:S(2)}) async-start(), calls=%async_computation.2 | async-start | bytes 4202496 | tf_op jit(solution)/shard_map/all_gather | solution.py:410
  11.7 206.5 %all-gather.9.cloned.1.call-start = ((), (), s32[]{:S(2)}) async-start(), calls=%async_computation.4 | async-start | bytes 5308416 | tf_op jit(solution)/shard_map/all_gather | solution.py:410
  12.4 227.7 %all-gather.11.cloned.1.call-start = ((), (), s32[]{:S(2)}) async-start(), calls=%async_computation.5 | async-start | bytes 5308416 | tf_op jit(solution)/shard_map/all_gather | solution.py:410
  12.5 39.5 %collective-permute-start = (bf16[1024,768]{1,0:T(8,128)(2,1)S(1)}, bf16[1024,768]{1,0:T(8,128)(2,1)S(1)}, u32[]{:S(2)}, u32[]{:S(2)}) collective-permute-start(bf16[1024,768]{1,0:T(8,128)(2,1)S(1)} %bitcast.104), channel_id=1, source_target_pairs={{0,8},{8,16},{16,24},{24,0},{1,9},{9,17},{17,25},{25,1},{2,10},{10... | collective-permute-start | bytes 4718600 | tf_op jit(solution)/shard_map/ppermute | solution.py:400
  52.0 37.5 %collective-permute-start.1 = (bf16[1024,768]{1,0:T(8,128)(2,1)S(1)}, bf16[1024,768]{1,0:T(8,128)(2,1)}, u32[]{:S(2)}, u32[]{:S(2)}) collective-permute-start(bf16[1024,768]{1,0:T(8,128)(2,1)S(1)} %collective-permute-done), channel_id=1, source_target_pairs={{0,8},{8,16},{16,24},{24,0},{1,9},{9,17},{17,25},{25,1},{2,10},{10... | collective-permute-start | bytes 4718600 | tf_op jit(solution)/shard_map/ppermute | solution.py:400
  52.0 272.5 %reduce-scatter.5.cloned.1.call-start = ((), (), s32[]{:S(2)}) async-start(), calls=%async_computation.7 | async-start | bytes 5308416 | tf_op jit(solution)/shard_map/reduce_scatter | solution.py:414
  89.5 56.1 %collective-permute-start.2 = (bf16[1024,768]{1,0:T(8,128)(2,1)}, bf16[1024,768]{1,0:T(8,128)(2,1)}, u32[]{:S(2)}, u32[]{:S(2)}) collective-permute-start(bf16[1024,768]{1,0:T(8,128)(2,1)} %collective-permute-done.1), channel_id=1, source_target_pairs={{0,8},{8,16},{16,24},{24,0},{1,9},{9,17},{17,25},{25,1},{2,10},{10... | collective-permute-start | bytes 4718600 | tf_op jit(solution)/shard_map/ppermute | solution.py:400
  167.1 32.5 %collective-permute-start.3 = (bf16[64,1024]{1,0:T(8,128)(2,1)}, bf16[64,1024]{1,0:T(8,128)(2,1)S(1)}, u32[]{:S(2)}, u32[]{:S(2)}) collective-permute-start(bf16[64,1024]{1,0:T(8,128)(2,1)} %get-tuple-element.93), channel_id=1, source_target_pairs={{0,24},{8,0},{16,8},{24,16},{1,25},{9,1},{17,9},{25,17},{2,26},{10... | collective-permute-start | bytes 393224 | tf_op jit(solution)/shard_map/ppermute | solution.py:400
  198.1 10.5 %collective-permute-start.7 = (bf16[64,1024]{1,0:T(8,128)(2,1)}, bf16[64,1024]{1,0:T(8,128)(2,1)S(1)}, u32[]{:S(2)}, u32[]{:S(2)}) collective-permute-start(bf16[64,1024]{1,0:T(8,128)(2,1)} %get-tuple-element.98), channel_id=1, source_target_pairs={{0,16},{8,24},{16,0},{24,8},{1,17},{9,25},{17,1},{25,9},{2,18},{10... | collective-permute-start | bytes 393224 | tf_op jit(solution)/shard_map/ppermute | solution.py:400
  203.7 10.5 %collective-permute-start.10 = (bf16[64,1024]{1,0:T(8,128)(2,1)}, bf16[64,1024]{1,0:T(8,128)(2,1)S(1)}, u32[]{:S(2)}, u32[]{:S(2)}) collective-permute-start(bf16[64,1024]{1,0:T(8,128)(2,1)} %get-tuple-element.102), channel_id=1, source_target_pairs={{0,16},{8,24},{16,0},{24,8},{1,17},{9,25},{17,1},{25,9},{2,18},{10... | collective-permute-start | bytes 393224 | tf_op jit(solution)/shard_map/ppermute | solution.py:400
  239.8 147.7 %reduce-scatter.3.cloned.1.call-start = ((), (), s32[]{:S(2)}) async-start(), calls=%async_computation.6 | async-start | bytes 6635520 | tf_op jit(solution)/shard_map/reduce_scatter | solution.py:414
  280.4 278.1 %all-reduce.4.cloned.1.call-start = ((), (), s32[]{:S(2)}) async-start(), calls=%async_computation.8 | async-start | bytes 2654208 | tf_op jit(solution)/shard_map/psum | solution.py:528
  287.0 19.7 %collective-permute-start.12 = (bf16[64,1024]{1,0:T(8,128)(2,1)S(1)}, bf16[64,1024]{1,0:T(8,128)(2,1)S(1)}, u32[]{:S(2)}, u32[]{:S(2)}) collective-permute-start(bf16[64,1024]{1,0:T(8,128)(2,1)S(1)} %get-tuple-element.195), channel_id=1, source_target_pairs={{0,8},{8,16},{16,24},{24,0},{1,9},{9,17},{17,25},{25,1},{2,10},{10... | collective-permute-start | bytes 393224 | tf_op jit(solution)/shard_map/ppermute | solution.py:400
  287.0 23.1 %collective-permute-start.13 = (bf16[64,1024]{1,0:T(8,128)(2,1)S(1)}, bf16[64,1024]{1,0:T(8,128)(2,1)S(1)}, u32[]{:S(2)}, u32[]{:S(2)}) collective-permute-start(bf16[64,1024]{1,0:T(8,128)(2,1)S(1)} %get-tuple-element.194), channel_id=1, source_target_pairs={{0,16},{8,24},{16,0},{24,8},{1,17},{9,25},{17,1},{25,9},{2,18},{10... | collective-permute-start | bytes 393224 | tf_op jit(solution)/shard_map/ppermute | solution.py:400
  288.0 22.1 %collective-permute-start.14 = (bf16[64,1024]{1,0:T(8,128)(2,1)S(1)}, bf16[64,1024]{1,0:T(8,128)(2,1)S(1)}, u32[]{:S(2)}, u32[]{:S(2)}) collective-permute-start(bf16[64,1024]{1,0:T(8,128)(2,1)S(1)} %get-tuple-element.193), channel_id=1, source_target_pairs={{0,24},{8,0},{16,8},{24,16},{1,25},{9,1},{17,9},{25,17},{2,26},{10... | collective-permute-start | bytes 393224 | tf_op jit(solution)/shard_map/ppermute | solution.py:400
  290.8 96.7 %collective-permute-start.15 = (bf16[128,1024]{1,0:T(8,128)(2,1)S(1)}, bf16[128,1024]{1,0:T(8,128)(2,1)S(1)}, u32[]{:S(2)}, u32[]{:S(2)}) collective-permute-start(bf16[128,1024]{1,0:T(8,128)(2,1)S(1)} %pad_maximum_fusion.2), channel_id=1, source_target_pairs={{0,8},{8,16},{16,24},{24,0},{1,9},{9,17},{17,25},{25,1},{2,10},{10... | collective-permute-start | bytes 786440 | tf_op jit(solution)/shard_map/ppermute | solution.py:400
  291.5 97.5 %collective-permute-start.16 = (bf16[128,1024]{1,0:T(8,128)(2,1)S(1)}, bf16[128,1024]{1,0:T(8,128)(2,1)S(1)}, u32[]{:S(2)}, u32[]{:S(2)}) collective-permute-start(bf16[128,1024]{1,0:T(8,128)(2,1)S(1)} %pad_maximum_fusion.3), channel_id=1, source_target_pairs={{0,16},{8,24},{16,0},{24,8},{1,17},{9,25},{17,1},{25,9},{2,18},{10... | collective-permute-start | bytes 786440 | tf_op jit(solution)/shard_map/ppermute | solution.py:400
  306.7 82.3 %collective-permute-start.17 = (bf16[128,1024]{1,0:T(8,128)(2,1)S(1)}, bf16[128,1024]{1,0:T(8,128)(2,1)S(1)}, u32[]{:S(2)}, u32[]{:S(2)}) collective-permute-start(bf16[128,1024]{1,0:T(8,128)(2,1)S(1)} %pad_maximum_fusion.4), channel_id=1, source_target_pairs={{0,24},{8,0},{16,8},{24,16},{1,25},{9,1},{17,9},{25,17},{2,26},{10... | collective-permute-start | bytes 786440 | tf_op jit(solution)/shard_map/ppermute | solution.py:400
  322.2 95.0 %collective-permute-start.18 = (bf16[192,1024]{1,0:T(8,128)(2,1)}, bf16[192,1024]{1,0:T(8,128)(2,1)S(1)}, u32[]{:S(2)}, u32[]{:S(2)}) collective-permute-start(bf16[192,1024]{1,0:T(8,128)(2,1)} %get-tuple-element.116), channel_id=1, source_target_pairs={{0,24},{8,0},{16,8},{24,16},{1,25},{9,1},{17,9},{25,17},{2,26},{10... | collective-permute-start | bytes 1179656 | tf_op jit(solution)/shard_map/ppermute | solution.py:400
  322.3 94.9 %collective-permute-start.21 = (bf16[192,1024]{1,0:T(8,128)(2,1)}, bf16[192,1024]{1,0:T(8,128)(2,1)}, u32[]{:S(2)}, u32[]{:S(2)}) collective-permute-start(bf16[192,1024]{1,0:T(8,128)(2,1)} %get-tuple-element.119), channel_id=1, source_target_pairs={{0,16},{8,24},{16,0},{24,8},{1,17},{9,25},{17,1},{25,9},{2,18},{10... | collective-permute-start | bytes 1179656 | tf_op jit(solution)/shard_map/ppermute | solution.py:400
  387.5 32.7 %collective-permute-start.24 = (bf16[192,1024]{1,0:T(8,128)(2,1)}, bf16[192,1024]{1,0:T(8,128)(2,1)}, u32[]{:S(2)}, u32[]{:S(2)}) collective-permute-start(bf16[192,1024]{1,0:T(8,128)(2,1)} %get-tuple-element.122), channel_id=1, source_target_pairs={{0,8},{8,16},{16,24},{24,0},{1,9},{9,17},{17,25},{25,1},{2,10},{10... | collective-permute-start | bytes 1179656 | tf_op jit(solution)/shard_map/ppermute | solution.py:400
  401.3 19.4 %collective-permute-start.19 = (bf16[192,1024]{1,0:T(8,128)(2,1)}, bf16[192,1024]{1,0:T(8,128)(2,1)}, u32[]{:S(2)}, u32[]{:S(2)}) collective-permute-start(bf16[192,1024]{1,0:T(8,128)(2,1)} %get-tuple-element.117), channel_id=1, source_target_pairs={{0,24},{8,0},{16,8},{24,16},{1,25},{9,1},{17,9},{25,17},{2,26},{10... | collective-permute-start | bytes 1179656 | tf_op jit(solution)/shard_map/ppermute | solution.py:400
  415.6 15.0 %collective-permute-start.20 = (bf16[192,1024]{1,0:T(8,128)(2,1)}, bf16[192,1024]{1,0:T(8,128)(2,1)S(1)}, u32[]{:S(2)}, u32[]{:S(2)}) collective-permute-start(bf16[192,1024]{1,0:T(8,128)(2,1)} %get-tuple-element.118), channel_id=1, source_target_pairs={{0,24},{8,0},{16,8},{24,16},{1,25},{9,1},{17,9},{25,17},{2,26},{10... | collective-permute-start | bytes 1179656 | tf_op jit(solution)/shard_map/ppermute | solution.py:400
  417.2 65.4 %collective-permute-start.22 = (bf16[192,1024]{1,0:T(8,128)(2,1)}, bf16[192,1024]{1,0:T(8,128)(2,1)S(1)}, u32[]{:S(2)}, u32[]{:S(2)}) collective-permute-start(bf16[192,1024]{1,0:T(8,128)(2,1)} %get-tuple-element.120), channel_id=1, source_target_pairs={{0,16},{8,24},{16,0},{24,8},{1,17},{9,25},{17,1},{25,9},{2,18},{10... | collective-permute-start | bytes 1179656 | tf_op jit(solution)/shard_map/ppermute | solution.py:400
  417.3 65.3 %collective-permute-start.23 = (bf16[192,1024]{1,0:T(8,128)(2,1)}, bf16[192,1024]{1,0:T(8,128)(2,1)S(1)}, u32[]{:S(2)}, u32[]{:S(2)}) collective-permute-start(bf16[192,1024]{1,0:T(8,128)(2,1)} %get-tuple-element.121), channel_id=1, source_target_pairs={{0,16},{8,24},{16,0},{24,8},{1,17},{9,25},{17,1},{25,9},{2,18},{10... | collective-permute-start | bytes 1179656 | tf_op jit(solution)/shard_map/ppermute | solution.py:400
  420.2 62.4 %collective-permute-start.25 = (bf16[192,1024]{1,0:T(8,128)(2,1)}, bf16[192,1024]{1,0:T(8,128)(2,1)S(1)}, u32[]{:S(2)}, u32[]{:S(2)}) collective-permute-start(bf16[192,1024]{1,0:T(8,128)(2,1)} %get-tuple-element.123), channel_id=1, source_target_pairs={{0,8},{8,16},{16,24},{24,0},{1,9},{9,17},{17,25},{25,1},{2,10},{10... | collective-permute-start | bytes 1179656 | tf_op jit(solution)/shard_map/ppermute | solution.py:400
  420.7 61.9 %collective-permute-start.26 = (bf16[192,1024]{1,0:T(8,128)(2,1)}, bf16[192,1024]{1,0:T(8,128)(2,1)S(1)}, u32[]{:S(2)}, u32[]{:S(2)}) collective-permute-start(bf16[192,1024]{1,0:T(8,128)(2,1)} %get-tuple-element.124), channel_id=1, source_target_pairs={{0,8},{8,16},{16,24},{24,0},{1,9},{9,17},{17,25},{25,1},{2,10},{10... | collective-permute-start | bytes 1179656 | tf_op jit(solution)/shard_map/ppermute | solution.py:400
  430.6 68.0 %collective-permute-start.27 = (bf16[4,96,576]{2,1,0:T(8,128)(2,1)}, bf16[4,96,576]{2,1,0:T(8,128)(2,1)}, u32[]{:S(2)}, u32[]{:S(2)}) collective-permute-start(bf16[4,96,576]{2,1,0:T(8,128)(2,1)} %fusion.57), channel_id=1, source_target_pairs={{0,1},{1,0},{2,3},{3,2},{4,5},{5,4},{6,7},{7,6},{8,9},{9,8},{10,11... | collective-permute-start | bytes 1327112 | tf_op jit(solution)/shard_map/ppermute | solution.py:425
  500.1 25.5 %collective-permute-start.30 = (bf16[96,576]{1,0:T(8,128)(2,1)S(1)}, bf16[96,576]{1,0:T(8,128)(2,1)S(1)}, u32[]{:S(2)}, u32[]{:S(2)}) collective-permute-start(bf16[96,576]{1,0:T(8,128)(2,1)S(1)} %get-tuple-element.198), channel_id=1, source_target_pairs={{0,6},{1,7},{2,4},{3,5},{4,2},{5,3},{6,0},{7,1},{8,14},{9,15},{10,... | collective-permute-start | bytes 331784 | tf_op jit(solution)/shard_map/ppermute | solution.py:431
  530.4 19.1 %collective-permute-start.32 = (bf16[96,576]{1,0:T(8,128)(2,1)S(1)}, bf16[96,576]{1,0:T(8,128)(2,1)S(1)}, u32[]{:S(2)}, u32[]{:S(2)}) collective-permute-start(bf16[96,576]{1,0:T(8,128)(2,1)S(1)} %get-tuple-element.180), channel_id=1, source_target_pairs={{0,16},{8,24},{16,0},{24,8},{1,17},{9,25},{17,1},{25,9},{2,18},{10... | collective-permute-start | bytes 331784 | tf_op jit(solution)/shard_map/ppermute | solution.py:400
  532.7 16.8 %collective-permute-start.33 = (bf16[96,576]{1,0:T(8,128)(2,1)S(1)}, bf16[96,576]{1,0:T(8,128)(2,1)S(1)}, u32[]{:S(2)}, u32[]{:S(2)}) collective-permute-start(bf16[96,576]{1,0:T(8,128)(2,1)S(1)} %get-tuple-element.180), channel_id=1, source_target_pairs={{0,8},{8,16},{16,24},{24,0},{1,9},{9,17},{17,25},{25,1},{2,10},{10... | collective-permute-start | bytes 331784 | tf_op jit(solution)/shard_map/ppermute | solution.py:400
  (63 other events, 605.4 us)
Sparse Core Ops, SparseCore 0:
  9.9 26.6 all-gather.6
  39.0 34.6 all-gather.4
  75.6 38.7 all-gather.8
  116.1 38.8 all-gather.10
  239.9 84.5 reduce-scatter.4
  327.9 59.6 reduce-scatter.2
  417.3 141.1 all-reduce.3

commit v6 on v5

--- a/solution.py
+++ b/solution.py
@@ -241,7 +241,7 @@
         join_kernel,
         out_shape=jax.ShapeDtypeStruct((span, width), jnp.float32),
         scratch_shapes=[pltpu.VMEM((total, span), jnp.bfloat16)],
-        compiler_params=pltpu.CompilerParams(vmem_limit_bytes=62 << 20),
+        compiler_params=pltpu.CompilerParams(vmem_limit_bytes=48 << 20),
         cost_estimate=pl.CostEstimate(
             flops=2 * span * width * total, bytes_accessed=12_000_000, transcendentals=0
         ),
@@ -304,7 +304,7 @@
             ],
         ),
         out_shape=[jax.ShapeDtypeStruct(shape, jnp.float32) for shape in shapes],
-        compiler_params=pltpu.CompilerParams(vmem_limit_bytes=62 << 20),
+        compiler_params=pltpu.CompilerParams(vmem_limit_bytes=48 << 20),
         cost_estimate=pl.CostEstimate(flops=20_000_000_000, bytes_accessed=4_000_000, transcendentals=0),
         name="attend_early",
     )(table, *packed_list, *([] if state is None else state))
@@ -338,7 +338,7 @@
             jax.ShapeDtypeStruct((HEAD_DIM, slots), jnp.float32),
             jax.ShapeDtypeStruct((1, slots), jnp.float32),
         ],
-        compiler_params=pltpu.CompilerParams(vmem_limit_bytes=62 << 20),
+        compiler_params=pltpu.CompilerParams(vmem_limit_bytes=40 << 20),
         cost_estimate=pl.CostEstimate(flops=10_000_000_000, bytes_accessed=4_000_000, transcendentals=0),
         name="attend_last",
     )(table, *packed_list, *packed_list, *packed_list, *state)
@@ -373,7 +373,7 @@
         ),
         out_shape=[jax.ShapeDtypeStruct((three, span), jnp.bfloat16)] * parts
         + [jax.ShapeDtypeStruct((three, slots), jnp.bfloat16)],
-        compiler_params=pltpu.CompilerParams(vmem_limit_bytes=62 << 20),
+        compiler_params=pltpu.CompilerParams(vmem_limit_bytes=40 << 20),
         cost_estimate=pl.CostEstimate(flops=40_000_000_000, bytes_accessed=6_000_000, transcendentals=0),
         name="attend_backward",
     )(table, *packed_list, *packed_list, *packed_list, *grad_list, exact, logs)

time: 581 us -> 578 us (level)
  Pallas kernels: 114 us -> 90.9 us
  local copies, waits for them, and re-layouts: 31 us -> 41.5 us
  waiting for transfers between devices: 158 us -> 165 us
  other arithmetic: 48.5 us -> 55.3 us
    unnamed x129 -> x175, local copies, waits for them, and re-layouts: 20.4 us -> 33 us
    pallas_call x3, Pallas kernels: 34.1 us -> 24.4 us  [attend_last(): pl.pallas_call(functools.partial(last_kernel, parts), grid_spec=pltpu.Pre...]
    pallas_call x3, Pallas kernels: 34.5 us -> 27.2 us  [attend_backward(): pl.pallas_call(functools.partial(backward_kernel, parts), grid_spec=pltpu...]
    psum x1, waiting for transfers between devices: 6.06 us -> 12 us  [per_device(): grad_up_out, grad_w_down = lax.psum((grad_up_out, grad_w_down), 'ctx')]
  transfers between devices with their start and end apart: 41 -> 41, of which waited for: 14 -> 14; matrix products, arithmetic and copies ran while one was open for 25% -> 25% of each run, Pallas kernels for 20% -> 16%
where the time goes in v6:
time: 578 us; the launch traced here: 569 us
  waiting for transfers between devices  165 us (29%)
  starting transfers between devices  118 us (20%)
  Pallas kernels  90.9 us (16%)
  matrix products  81.6 us (14%)
  other arithmetic  55.3 us (10%)
  local copies, waits for them, and re-layouts  41.5 us (7%)
  between operations  16.5 us (3%)
    ppermute x30, waiting for transfers between devices, shift(): return lax.ppermute(array, 'ctx', [(i, (i + by) % ctx) for i in range(ctx)])  82.3 us
    dot_general x14, matrix products, product(): return jnp.einsum(equation, left, right, preferred_element_type=jnp.float32)  81.6 us
    reduce_scatter x2, waiting for transfers between devices, scatter_rows(): lax.psum_scatter(array.astype(jnp.bfloat16), 'fsdp', scatter_dimension=0,...  64.6 us
    ppermute x1, starting transfers between devices, scatter_pairs(): got = lax.ppermute(sent, 'fsdp', [(i, i ^ 1) for i in range(fsdp)])  52.2 us
    ppermute x30, starting transfers between devices, shift(): return lax.ppermute(array, 'ctx', [(i, (i + by) % ctx) for i in range(ctx)])  42 us
    unnamed x175, local copies, waits for them, and re-layouts  33 us
    pallas_call x2, Pallas kernels, attend_early(): pl.pallas_call(functools.partial(early_kernel, parts, heads, state is Non...  30.5 us
    pallas_call x3, Pallas kernels, attend_backward(): pl.pallas_call(functools.partial(backward_kernel, parts), grid_spec=pltpu...  27.2 us
  transfers between devices with their start and end apart: 41, of which 14 were waited for; matrix products, arithmetic and copies ran while one was open for 25% of the time, Pallas kernels for 16%

profile of v6, /device:TPU:0, one launch (start us, length us, event | category | flops | bytes accessed | tf_op | source)
XLA Modules:
  0.0 569.0 jit_solution(14009653444526757438)
XLA Ops:
  14.3 3.1 collective-permute-start
  29.0 25.0 %collective-permute-done = bf16[1024,768]{1,0:T(8,128)(2,1)} collective-permute-done((bf16[1024,768]{1,0:T(8,128)(2,1)S(1)}, bf16[1024,768]{1,0:T(8,128)(2,1)}, u32[]{:S(2)}, u32[]{:S(2)}) %collective-permute-start) | collective-permute-done | bytes 1572896 | tf_op jit(solution)/shard_map/ppermute | solution.py:400
  56.9 34.8 %collective-permute-done.1 = bf16[1024,768]{1,0:T(8,128)(2,1)} collective-permute-done((bf16[1024,768]{1,0:T(8,128)(2,1)}, bf16[1024,768]{1,0:T(8,128)(2,1)}, u32[]{:S(2)}, u32[]{:S(2)}) %collective-permute-start.1) | collective-permute-done | bytes 1572896 | tf_op jit(solution)/shard_map/ppermute | solution.py:400
  104.1 9.9 %attend_early.2 = (f32[3,1,4096]{2,1,0:T(1,128)S(1)}, f32[3,1,4096]{2,1,0:T(1,128)S(1)}, f32[3,64,4096]{2,1,0:T(8,128)S(1)}) custom-call(s32[75]{0:T(128)S(1)} %concatenate.52.table, bf16[576,1024]{1,0:T(8,128)(2,1)S(1)} %convolution_convert_fusion.7.refs_0_.refs_4_.refs_8_, bf16[576,1024]{1,0:T(8,128)(2,1)S(1)} %convolution_convert_fusion.6.refs_1_.refs_5_.refs_9_), custom_call_target="tpu_custom_call" | custom-call | flops 20000000000 | bytes 4000000 | tf_op jit(solution)/shard_map/attend_early/pallas_call | solution.py:292
  122.2 20.5 %attend_early.3 = (f32[3,1,4096]{2,1,0:T(1,128)S(1)}, f32[3,1,4096]{2,1,0:T(1,128)S(1)}, f32[3,64,4096]{2,1,0:T(8,128)}) custom-call(s32[75]{0:T(128)S(1)} %concatenate.53.table, bf16[576,1024]{1,0:T(8,128)(2,1)S(1)} %convolution_convert_fusion.7.refs_0_.refs_4_.refs_8_, bf16[576,1024]{1,0:T(8,128)(2,1)S(1)} %convolution_convert_fusion.6.refs_1_.refs_5_.refs_9_, ...), custom_call_target="tpu_custom_call" | custom-call | flops 20000000000 | bytes 4000000 | tf_op jit(solution)/shard_map/attend_early/pallas_call | solution.py:292
  151.0 8.1 %attend_last.3 = (bf16[64,1024]{1,0:T(8,128)(2,1)S(1)}, bf16[64,1024]{1,0:T(8,128)(2,1)S(1)}, bf16[64,1024]{1,0:T(8,128)(2,1)S(1)}, bf16[64,1024]{1,0:T(8,128)(2...) custom-call(s32[75]{0:T(128)S(1)} %concatenate.54.table, ...), custom_call_target="tpu_custom_call" | custom-call | flops 10000000000 | bytes 4000000 | tf_op jit(solution)/shard_map/attend_last/pallas_call | solution.py:318
  160.1 3.7 collective-permute-start.3
  163.8 8.3 %attend_last.4 = (bf16[64,1024]{1,0:T(8,128)(2,1)S(1)}, bf16[64,1024]{1,0:T(8,128)(2,1)S(1)}, bf16[64,1024]{1,0:T(8,128)(2,1)S(1)}, bf16[64,1024]{1,0:T(8,128)(2...) custom-call(s32[75]{0:T(128)S(1)} %concatenate.54.table, ...), custom_call_target="tpu_custom_call" | custom-call | flops 10000000000 | bytes 4000000 | tf_op jit(solution)/shard_map/attend_last/pallas_call | solution.py:318
  173.1 8.1 %attend_last.5 = (bf16[64,1024]{1,0:T(8,128)(2,1)S(1)}, bf16[64,1024]{1,0:T(8,128)(2,1)S(1)}, bf16[64,1024]{1,0:T(8,128)(2,1)S(1)}, bf16[64,1024]{1,0:T(8,128)(2...) custom-call(s32[75]{0:T(128)S(1)} %concatenate.54.table, ...), custom_call_target="tpu_custom_call" | custom-call | flops 10000000000 | bytes 4000000 | tf_op jit(solution)/shard_map/attend_last/pallas_call | solution.py:318
  181.3 3.4 collective-permute-start.5
  191.1 3.7 collective-permute-start.10
  196.6 3.2 collective-permute-done.10
  205.5 8.2 %fusion.80 = f32[1024,3072]{1,0:T(8,128)S(1)} fusion(bf16[768,3072]{1,0:T(8,128)(2,1)} %all-gather.9.cloned.1.call-done, f32[1024,768]{1,0:T(8,128)} %copy-done.45, f32[768]{0:T(1024)S(1)} %get-tuple-element.162, f32[1024]{0:T(1024)S(1)} %fusion.68, f32[1024]{0:T(1024)S(1)} %broadcast_multiply_fusion.1), kind=kOutput, calls=%fused_computation.215 | convolution fusion | flops 4834983936 | bytes 20458496 | tf_op jit(solution)/shard_map/uj,jn->un/dot_general | solution.py:394
  213.7 4.5 copy-done.72
  218.2 8.9 %convolution_convert_fusion = bf16[3072,768]{1,0:T(8,128)(2,1)} fusion(bf16[1024,768]{1,0:T(8,128)(2,1)S(1)} %copy-done.42, f32[1024,3072]{1,0:T(8,128)S(1)} %fusion.80), kind=kOutput, calls=%fused_computation.20 | convolution fusion | flops 4862509056 | bytes 18874368 | tf_op jit(solution)/shard_map/un,uj->nj/dot_general | solution.py:394
  227.7 15.5 %fusion.6 = bf16[1024,3072]{1,0:T(8,128)(2,1)S(1)} fusion(f32[1024,3072]{1,0:T(8,128)} %copy-done.72, bf16[1024,768]{1,0:T(8,128)(2,1)} %bitcast_multiply_fusion, bf16[3072,768]{1,0:T(8,128)(2,1)} %all-gather.11.cloned.1.call-done), kind=kOutput, calls=%fused_computation.9 | convolution fusion | flops 4894752768 | bytes 25165824 | tf_op jit(solution)/shard_map/uj,nj->un/dot_general | solution.py:394
  243.2 10.0 %multiply_reduce_fusion = (f32[1024]{0:T(1024)S(1)}, f32[1024,768]{1,0:T(8,128)S(1)}) fusion(f32[1024,768]{1,0:T(8,128)S(1)} %copy-done.46, f32[768]{0:T(1024)S(1)} %get-tuple-element.162, f32[1024]{0:T(1024)S(1)} %broadcast_multiply_fusion.1, bf16[1024,3072]{1,0:T(8,128)(2,1)S(1)} %fusion.6, bf16[768,3072]{1,0:T(8,128)(2,1)} %all-gather.9.cloned.1.call-done), kind=kOutput, calls=%fused_computation.67 | convolution fusion | flops 4834982912 | bytes 17312768 | tf_op jit(solution)/shard_map/un,jn->uj/dot_general | solution.py:394
  259.9 6.3 %convolution_convert_fusion.1 = bf16[768,3072]{1,0:T(8,128)(2,1)S(1)} fusion(bf16[1024,3072]{1,0:T(8,128)(2,1)S(1)} %bitcast.127, f32[1024,768]{1,0:T(8,128)S(1)} %copy-done.46, f32[768]{0:T(1024)S(1)} %get-tuple-element.162, f32[1024]{0:T(1024)S(1)} %fusion.68, f32[1024]{0:T(1024)S(1)} %broadcast_multiply_fusion.1), kind=kOutput, calls=%fused_computation.21 | convolution fusion | flops 4837343232 | bytes 14167040 | tf_op jit(solution)/shard_map/uj,un->jn/dot_general | solution.py:394
  271.8 3.4 convolution_convert_fusion.2
  282.8 11.5 %fusion.47 = bf16[1,1024,768]{2,1,0:T(8,128)(2,1)} fusion(f32[1024,768]{1,0:T(8,128)S(1)} %copy-done.47, bf16[3072,768]{1,0:T(8,128)(2,1)S(1)} %bitcast.123, f32[1024,3072]{1,0:T(8,128)} %copy-done.72), kind=kOutput, calls=%fused_computation.84 | convolution fusion | flops 4861722624 | bytes 22020096 | tf_op jit(solution)/shard_map/un,nj->uj/dot_general | solution.py:394
  297.9 8.5 %attend_backward.3 = (bf16[192,1024]{1,0:T(8,128)(2,1)S(1)}, bf16[192,1024]{1,0:T(8,128)(2,1)}, bf16[192,1024]{1,0:T(8,128)(2,1)S(1)}, bf16[192,1024]{1,0:T(8,128)(2,1)S(1)}, bf16[192,4096]{1,0:T(8,128)(2,1)S(1)}) custom-call(s32[9]{0:T(128)S(1)} %pad_add_fusion.table, bf16[576,1024]{1,0:T(8,128)(2,1)S(1)} %copy-done.15, bf16[576,1024]{1,0:T(8,128)(2,1)S(1)} %copy-done.18, ...), custom_call_target="tpu_custom_call" | custom-call | flops 40000000000 | bytes 6000000 | tf_op jit(solution)/shard_map/attend_backward/pallas_call | solution.py:352
  311.3 63.0 %reduce-scatter.3.cloned.1.call-done = bf16[96,3840]{1,0:T(8,128)(2,1)} async-done(((bf16[768,3840]{1,0:T(8,128)(2,1)}), bf16[96,3840]{1,0:T(8,128)(2,1)}) %reduce-scatter.3.cloned.1.call-update) | async-done | bytes 737296 | tf_op jit(solution)/shard_map/reduce_scatter | solution.py:414
  385.7 9.4 %attend_backward.4 = (bf16[192,1024]{1,0:T(8,128)(2,1)S(1)}, bf16[192,1024]{1,0:T(8,128)(2,1)}, bf16[192,1024]{1,0:T(8,128)(2,1)S(1)}, bf16[192,1024]{1,0:T(8,128)(2,1)S(1)}, bf16[192,4096]{1,0:T(8,128)(2,1)S(1)}) custom-call(s32[9]{0:T(128)S(1)} %pad_add_fusion.table, bf16[576,1024]{1,0:T(8,128)(2,1)S(1)} %copy-done.16, bf16[576,1024]{1,0:T(8,128)(2,1)S(1)} %copy-done.19, ...), custom_call_target="tpu_custom_call" | custom-call | flops 40000000000 | bytes 6000000 | tf_op jit(solution)/shard_map/attend_backward/pallas_call | solution.py:352
  399.3 9.4 %attend_backward.5 = (bf16[192,1024]{1,0:T(8,128)(2,1)S(1)}, bf16[192,1024]{1,0:T(8,128)(2,1)}, bf16[192,1024]{1,0:T(8,128)(2,1)S(1)}, bf16[192,1024]{1,0:T(8,128)(2,1)S(1)}, bf16[192,4096]{1,0:T(8,128)(2,1)S(1)}) custom-call(s32[9]{0:T(128)S(1)} %pad_add_fusion.table, bf16[576,1024]{1,0:T(8,128)(2,1)S(1)} %copy-done.16, bf16[576,1024]{1,0:T(8,128)(2,1)S(1)} %copy-done.19, ...), custom_call_target="tpu_custom_call" | custom-call | flops 40000000000 | bytes 6000000 | tf_op jit(solution)/shard_map/attend_backward/pallas_call | solution.py:352
  417.4 9.3 %fusion.7 = f32[768,576]{1,0:T(8,128)S(1)} fusion(bf16[1024,768]{1,0:T(8,128)(2,1)} %copy-done.54, bf16[1024,768]{1,0:T(8,128)(2,1)} %copy-done.53, bf16[1024,768]{1,0:T(8,128)(2,1)} %copy-done.52, bf16[1024,768]{1,0:T(8,128)(2,1)} %copy-done.51, bf16[192,4096]{1,0:T(8,128)(2,1)} %copy-done.35, bf16[192,4096]{1,0:T(8,128)(2,1)} %copy-done.34, ...), kind=kOutput, calls=%fused_computation.11 | convolution fusion | flops 3663200256 | bytes 12779520 | tf_op jit(solution)/shard_map/uj,nu->jn/dot_general | solution.py:394
  426.8 52.2 %collective-permute-start.27 = (bf16[4,96,576]{2,1,0:T(8,128)(2,1)S(1)}, bf16[4,96,576]{2,1,0:T(8,128)(2,1)S(1)}, u32[]{:S(2)}, u32[]{:S(2)}) collective-permute-start(bf16[4,96,576]{2,1,0:T(8,128)(2,1)S(1)} %fusion.57), channel_id=1, source_target_pairs={{0,1},{1,0},{2,3},{3,2},{4,5},{5,4},{6,7},{7,6},{8,9},{9,8},{10,11... | collective-permute-start | bytes 1327112 | tf_op jit(solution)/shard_map/ppermute | solution.py:425
  479.1 8.8 %join_product.1 = f32[1024,768]{1,0:T(8,128)} custom-call(bf16[192,1024]{1,0:T(8,128)(2,1)S(1)} %copy-done.9, bf16[192,1024]{1,0:T(8,128)(2,1)S(1)} %copy-done.11, bf16[192,1024]{1,0:T(8,128)(2,1)S(1)} %copy-done.13, bf16[192,1024]{1,0:T(8,128)(2,1)S(1)} %collective-permute-done.18.refs_3_, bf16[192,1024]{1,0:T(8,128)(2,1)S(1)} %collective-permute-done.19.refs_4_, ...), custom_call_target="tpu_custom_call" | custom-call | flops 3623878656 | bytes 12000000 | tf_op jit(solution)/shard_map/join_product/pallas_call | solution.py:240
  487.9 3.1 fusion.43
  492.6 23.0 %collective-permute-start.30 = (bf16[96,576]{1,0:T(8,128)(2,1)S(1)}, bf16[96,576]{1,0:T(8,128)(2,1)S(1)}, u32[]{:S(2)}, u32[]{:S(2)}) collective-permute-start(bf16[96,576]{1,0:T(8,128)(2,1)S(1)} %get-tuple-element.198), channel_id=1, source_target_pairs={{0,6},{1,7},{2,4},{3,5},{4,2},{5,3},{6,0},{7,1},{8,14},{9,15},{10,... | collective-permute-start | bytes 331784 | tf_op jit(solution)/shard_map/ppermute | solution.py:431
  527.4 3.3 collective-permute-done.31
  530.7 10.4 %collective-permute-done.32 = bf16[96,576]{1,0:T(8,128)(2,1)S(1)} collective-permute-done((bf16[96,576]{1,0:T(8,128)(2,1)S(1)}, bf16[96,576]{1,0:T(8,128)(2,1)S(1)}, u32[]{:S(2)}, u32[]{:S(2)}) %collective-permute-start.32) | collective-permute-done | bytes 110624 | tf_op jit(solution)/shard_map/ppermute | solution.py:400
  544.1 12.0 %all-reduce.4.cloned.1.call-done = (bf16[96,3840]{1,0:T(8,128)(2,1)}, bf16[384,768]{1,0:T(8,128)(2,1)}) async-done(((bf16[96,3840]{1,0:T(8,128)(2,1)}, bf16[384,768]{1,0:T(8,128)(2,1)}), (bf16[96,3840]{1,0:T(8,128)(2,1)}, bf16[384,768]{1,0:T(8,128)(2,1)})) %all-reduce.4.cloned.1.call-update) | async-done | bytes 1327120 | tf_op jit(solution)/shard_map/psum | solution.py:528
  (353 shorter events, 140.2 us)
Async XLA Ops:
  7.2 46.9 %all-gather.7.cloned.1.call-start = ((), (), s32[]{:S(2)}) async-start(), calls=%async_computation.3 | async-start | bytes 1327104 | tf_op jit(solution)/shard_map/all_gather | solution.py:410
  7.9 83.7 %all-gather.5.cloned.1.call-start = ((), (), s32[]{:S(2)}) async-start(), calls=%async_computation.2 | async-start | bytes 4202496 | tf_op jit(solution)/shard_map/all_gather | solution.py:410
  13.5 192.0 %all-gather.9.cloned.1.call-start = ((), (), s32[]{:S(2)}) async-start(), calls=%async_computation.4 | async-start | bytes 5308416 | tf_op jit(solution)/shard_map/all_gather | solution.py:410
  14.3 213.4 %all-gather.11.cloned.1.call-start = ((), (), s32[]{:S(2)}) async-start(), calls=%async_computation.5 | async-start | bytes 5308416 | tf_op jit(solution)/shard_map/all_gather | solution.py:410
  14.3 39.6 %collective-permute-start = (bf16[1024,768]{1,0:T(8,128)(2,1)S(1)}, bf16[1024,768]{1,0:T(8,128)(2,1)}, u32[]{:S(2)}, u32[]{:S(2)}) collective-permute-start(bf16[1024,768]{1,0:T(8,128)(2,1)S(1)} %bitcast.104), channel_id=1, source_target_pairs={{0,8},{8,16},{16,24},{24,0},{1,9},{9,17},{17,25},{25,1},{2,10},{10... | collective-permute-start | bytes 4718600 | tf_op jit(solution)/shard_map/ppermute | solution.py:400
  53.9 37.7 %collective-permute-start.1 = (bf16[1024,768]{1,0:T(8,128)(2,1)}, bf16[1024,768]{1,0:T(8,128)(2,1)}, u32[]{:S(2)}, u32[]{:S(2)}) collective-permute-start(bf16[1024,768]{1,0:T(8,128)(2,1)} %collective-permute-done), channel_id=1, source_target_pairs={{0,8},{8,16},{16,24},{24,0},{1,9},{9,17},{17,25},{25,1},{2,10},{10... | collective-permute-start | bytes 4718600 | tf_op jit(solution)/shard_map/ppermute | solution.py:400
  54.0 257.4 %reduce-scatter.5.cloned.1.call-start = ((), (), s32[]{:S(2)}) async-start(), calls=%async_computation.7 | async-start | bytes 5308416 | tf_op jit(solution)/shard_map/reduce_scatter | solution.py:414
  91.6 51.1 %collective-permute-start.2 = (bf16[1024,768]{1,0:T(8,128)(2,1)}, bf16[1024,768]{1,0:T(8,128)(2,1)}, u32[]{:S(2)}, u32[]{:S(2)}) collective-permute-start(bf16[1024,768]{1,0:T(8,128)(2,1)} %collective-permute-done.1), channel_id=1, source_target_pairs={{0,8},{8,16},{16,24},{24,0},{1,9},{9,17},{17,25},{25,1},{2,10},{10... | collective-permute-start | bytes 4718600 | tf_op jit(solution)/shard_map/ppermute | solution.py:400
  160.1 26.3 %collective-permute-start.3 = (bf16[64,1024]{1,0:T(8,128)(2,1)S(1)}, bf16[64,1024]{1,0:T(8,128)(2,1)S(1)}, u32[]{:S(2)}, u32[]{:S(2)}) collective-permute-start(bf16[64,1024]{1,0:T(8,128)(2,1)S(1)} %get-tuple-element.93), channel_id=1, source_target_pairs={{0,24},{8,0},{16,8},{24,16},{1,25},{9,1},{17,9},{25,17},{2,26},{10... | collective-permute-start | bytes 393224 | tf_op jit(solution)/shard_map/ppermute | solution.py:400
  185.2 10.4 %collective-permute-start.7 = (bf16[64,1024]{1,0:T(8,128)(2,1)S(1)}, bf16[64,1024]{1,0:T(8,128)(2,1)S(1)}, u32[]{:S(2)}, u32[]{:S(2)}) collective-permute-start(bf16[64,1024]{1,0:T(8,128)(2,1)S(1)} %get-tuple-element.98), channel_id=1, source_target_pairs={{0,16},{8,24},{16,0},{24,8},{1,17},{9,25},{17,1},{25,9},{2,18},{10... | collective-permute-start | bytes 393224 | tf_op jit(solution)/shard_map/ppermute | solution.py:400
  227.2 147.2 %reduce-scatter.3.cloned.1.call-start = ((), (), s32[]{:S(2)}) async-start(), calls=%async_computation.6 | async-start | bytes 6635520 | tf_op jit(solution)/shard_map/reduce_scatter | solution.py:414
  269.2 286.9 %all-reduce.4.cloned.1.call-start = ((), (), s32[]{:S(2)}) async-start(), calls=%async_computation.8 | async-start | bytes 2654208 | tf_op jit(solution)/shard_map/psum | solution.py:528
  275.3 19.7 %collective-permute-start.12 = (bf16[64,1024]{1,0:T(8,128)(2,1)S(1)}, bf16[64,1024]{1,0:T(8,128)(2,1)S(1)}, u32[]{:S(2)}, u32[]{:S(2)}) collective-permute-start(bf16[64,1024]{1,0:T(8,128)(2,1)S(1)} %get-tuple-element.195), channel_id=1, source_target_pairs={{0,8},{8,16},{16,24},{24,0},{1,9},{9,17},{17,25},{25,1},{2,10},{10... | collective-permute-start | bytes 393224 | tf_op jit(solution)/shard_map/ppermute | solution.py:400
  275.4 22.4 %collective-permute-start.13 = (bf16[64,1024]{1,0:T(8,128)(2,1)S(1)}, bf16[64,1024]{1,0:T(8,128)(2,1)S(1)}, u32[]{:S(2)}, u32[]{:S(2)}) collective-permute-start(bf16[64,1024]{1,0:T(8,128)(2,1)S(1)} %get-tuple-element.194), channel_id=1, source_target_pairs={{0,16},{8,24},{16,0},{24,8},{1,17},{9,25},{17,1},{25,9},{2,18},{10... | collective-permute-start | bytes 393224 | tf_op jit(solution)/shard_map/ppermute | solution.py:400
  277.4 20.5 %collective-permute-start.14 = (bf16[64,1024]{1,0:T(8,128)(2,1)S(1)}, bf16[64,1024]{1,0:T(8,128)(2,1)S(1)}, u32[]{:S(2)}, u32[]{:S(2)}) collective-permute-start(bf16[64,1024]{1,0:T(8,128)(2,1)S(1)} %get-tuple-element.193), channel_id=1, source_target_pairs={{0,24},{8,0},{16,8},{24,16},{1,25},{9,1},{17,9},{25,17},{2,26},{10... | collective-permute-start | bytes 393224 | tf_op jit(solution)/shard_map/ppermute | solution.py:400
  280.7 93.6 %collective-permute-start.15 = (bf16[128,1024]{1,0:T(8,128)(2,1)}, bf16[128,1024]{1,0:T(8,128)(2,1)S(1)}, u32[]{:S(2)}, u32[]{:S(2)}) collective-permute-start(bf16[128,1024]{1,0:T(8,128)(2,1)} %pad_maximum_fusion.2), channel_id=1, source_target_pairs={{0,8},{8,16},{16,24},{24,0},{1,9},{9,17},{17,25},{25,1},{2,10},{10... | collective-permute-start | bytes 786440 | tf_op jit(solution)/shard_map/ppermute | solution.py:400
  281.4 95.3 %collective-permute-start.16 = (bf16[128,1024]{1,0:T(8,128)(2,1)}, bf16[128,1024]{1,0:T(8,128)(2,1)S(1)}, u32[]{:S(2)}, u32[]{:S(2)}) collective-permute-start(bf16[128,1024]{1,0:T(8,128)(2,1)} %pad_maximum_fusion.3), channel_id=1, source_target_pairs={{0,16},{8,24},{16,0},{24,8},{1,17},{9,25},{17,1},{25,9},{2,18},{10... | collective-permute-start | bytes 786440 | tf_op jit(solution)/shard_map/ppermute | solution.py:400
  295.0 82.4 %collective-permute-start.17 = (bf16[128,1024]{1,0:T(8,128)(2,1)}, bf16[128,1024]{1,0:T(8,128)(2,1)}, u32[]{:S(2)}, u32[]{:S(2)}) collective-permute-start(bf16[128,1024]{1,0:T(8,128)(2,1)} %pad_maximum_fusion.4), channel_id=1, source_target_pairs={{0,24},{8,0},{16,8},{24,16},{1,25},{9,1},{17,9},{25,17},{2,26},{10... | collective-permute-start | bytes 786440 | tf_op jit(solution)/shard_map/ppermute | solution.py:400
  308.2 105.5 %collective-permute-start.18 = (bf16[192,1024]{1,0:T(8,128)(2,1)}, bf16[192,1024]{1,0:T(8,128)(2,1)S(1)}, u32[]{:S(2)}, u32[]{:S(2)}) collective-permute-start(bf16[192,1024]{1,0:T(8,128)(2,1)} %get-tuple-element.116), channel_id=1, source_target_pairs={{0,24},{8,0},{16,8},{24,16},{1,25},{9,1},{17,9},{25,17},{2,26},{10... | collective-permute-start | bytes 1179656 | tf_op jit(solution)/shard_map/ppermute | solution.py:400
  308.5 105.3 %collective-permute-start.21 = (bf16[192,1024]{1,0:T(8,128)(2,1)S(1)}, bf16[192,1024]{1,0:T(8,128)(2,1)S(1)}, u32[]{:S(2)}, u32[]{:S(2)}) collective-permute-start(bf16[192,1024]{1,0:T(8,128)(2,1)S(1)} %get-tuple-element.119), channel_id=1, source_target_pairs={{0,16},{8,24},{16,0},{24,8},{1,17},{9,25},{17,1},{25,9},{2,18},{10... | collective-permute-start | bytes 1179656 | tf_op jit(solution)/shard_map/ppermute | solution.py:400
  375.0 41.7 %collective-permute-start.24 = (bf16[192,1024]{1,0:T(8,128)(2,1)S(1)}, bf16[192,1024]{1,0:T(8,128)(2,1)S(1)}, u32[]{:S(2)}, u32[]{:S(2)}) collective-permute-start(bf16[192,1024]{1,0:T(8,128)(2,1)S(1)} %get-tuple-element.122), channel_id=1, source_target_pairs={{0,8},{8,16},{16,24},{24,0},{1,9},{9,17},{17,25},{25,1},{2,10},{10... | collective-permute-start | bytes 1179656 | tf_op jit(solution)/shard_map/ppermute | solution.py:400
  396.9 20.3 %collective-permute-start.19 = (bf16[192,1024]{1,0:T(8,128)(2,1)}, bf16[192,1024]{1,0:T(8,128)(2,1)S(1)}, u32[]{:S(2)}, u32[]{:S(2)}) collective-permute-start(bf16[192,1024]{1,0:T(8,128)(2,1)} %get-tuple-element.117), channel_id=1, source_target_pairs={{0,24},{8,0},{16,8},{24,16},{1,25},{9,1},{17,9},{25,17},{2,26},{10... | collective-permute-start | bytes 1179656 | tf_op jit(solution)/shard_map/ppermute | solution.py:400
  412.2 14.6 %collective-permute-start.20 = (bf16[192,1024]{1,0:T(8,128)(2,1)}, bf16[192,1024]{1,0:T(8,128)(2,1)S(1)}, u32[]{:S(2)}, u32[]{:S(2)}) collective-permute-start(bf16[192,1024]{1,0:T(8,128)(2,1)} %get-tuple-element.118), channel_id=1, source_target_pairs={{0,24},{8,0},{16,8},{24,16},{1,25},{9,1},{17,9},{25,17},{2,26},{10... | collective-permute-start | bytes 1179656 | tf_op jit(solution)/shard_map/ppermute | solution.py:400
  413.7 65.2 %collective-permute-start.22 = (bf16[192,1024]{1,0:T(8,128)(2,1)S(1)}, bf16[192,1024]{1,0:T(8,128)(2,1)S(1)}, u32[]{:S(2)}, u32[]{:S(2)}) collective-permute-start(bf16[192,1024]{1,0:T(8,128)(2,1)S(1)} %get-tuple-element.120), channel_id=1, source_target_pairs={{0,16},{8,24},{16,0},{24,8},{1,17},{9,25},{17,1},{25,9},{2,18},{10... | collective-permute-start | bytes 1179656 | tf_op jit(solution)/shard_map/ppermute | solution.py:400
  413.8 65.2 %collective-permute-start.23 = (bf16[192,1024]{1,0:T(8,128)(2,1)}, bf16[192,1024]{1,0:T(8,128)(2,1)S(1)}, u32[]{:S(2)}, u32[]{:S(2)}) collective-permute-start(bf16[192,1024]{1,0:T(8,128)(2,1)} %copy-done.1), channel_id=1, source_target_pairs={{0,16},{8,24},{16,0},{24,8},{1,17},{9,25},{17,1},{25,9},{2,18},{10... | collective-permute-start | bytes 1179656 | tf_op jit(solution)/shard_map/ppermute | solution.py:400
  416.7 62.3 %collective-permute-start.25 = (bf16[192,1024]{1,0:T(8,128)(2,1)S(1)}, bf16[192,1024]{1,0:T(8,128)(2,1)S(1)}, u32[]{:S(2)}, u32[]{:S(2)}) collective-permute-start(bf16[192,1024]{1,0:T(8,128)(2,1)S(1)} %get-tuple-element.123), channel_id=1, source_target_pairs={{0,8},{8,16},{16,24},{24,0},{1,9},{9,17},{17,25},{25,1},{2,10},{10... | collective-permute-start | bytes 1179656 | tf_op jit(solution)/shard_map/ppermute | solution.py:400
  417.2 61.8 %collective-permute-start.26 = (bf16[192,1024]{1,0:T(8,128)(2,1)}, bf16[192,1024]{1,0:T(8,128)(2,1)S(1)}, u32[]{:S(2)}, u32[]{:S(2)}) collective-permute-start(bf16[192,1024]{1,0:T(8,128)(2,1)} %copy-done), channel_id=1, source_target_pairs={{0,8},{8,16},{16,24},{24,0},{1,9},{9,17},{17,25},{25,1},{2,10},{10... | collective-permute-start | bytes 1179656 | tf_op jit(solution)/shard_map/ppermute | solution.py:400
  426.8 65.6 %collective-permute-start.27 = (bf16[4,96,576]{2,1,0:T(8,128)(2,1)S(1)}, bf16[4,96,576]{2,1,0:T(8,128)(2,1)S(1)}, u32[]{:S(2)}, u32[]{:S(2)}) collective-permute-start(bf16[4,96,576]{2,1,0:T(8,128)(2,1)S(1)} %fusion.57), channel_id=1, source_target_pairs={{0,1},{1,0},{2,3},{3,2},{4,5},{5,4},{6,7},{7,6},{8,9},{9,8},{10,11... | collective-permute-start | bytes 1327112 | tf_op jit(solution)/shard_map/ppermute | solution.py:425
  492.6 25.8 %collective-permute-start.30 = (bf16[96,576]{1,0:T(8,128)(2,1)S(1)}, bf16[96,576]{1,0:T(8,128)(2,1)S(1)}, u32[]{:S(2)}, u32[]{:S(2)}) collective-permute-start(bf16[96,576]{1,0:T(8,128)(2,1)S(1)} %get-tuple-element.198), channel_id=1, source_target_pairs={{0,6},{1,7},{2,4},{3,5},{4,2},{5,3},{6,0},{7,1},{8,14},{9,15},{10,... | collective-permute-start | bytes 331784 | tf_op jit(solution)/shard_map/ppermute | solution.py:431
  520.5 10.2 %collective-permute-start.31 = (bf16[96,576]{1,0:T(8,128)(2,1)S(1)}, bf16[96,576]{1,0:T(8,128)(2,1)S(1)}, u32[]{:S(2)}, u32[]{:S(2)}) collective-permute-start(bf16[96,576]{1,0:T(8,128)(2,1)S(1)} %get-tuple-element.180), channel_id=1, source_target_pairs={{0,24},{8,0},{16,8},{24,16},{1,25},{9,1},{17,9},{25,17},{2,26},{10... | collective-permute-start | bytes 331784 | tf_op jit(solution)/shard_map/ppermute | solution.py:400
  523.1 18.1 %collective-permute-start.32 = (bf16[96,576]{1,0:T(8,128)(2,1)S(1)}, bf16[96,576]{1,0:T(8,128)(2,1)S(1)}, u32[]{:S(2)}, u32[]{:S(2)}) collective-permute-start(bf16[96,576]{1,0:T(8,128)(2,1)S(1)} %get-tuple-element.180), channel_id=1, source_target_pairs={{0,16},{8,24},{16,0},{24,8},{1,17},{9,25},{17,1},{25,9},{2,18},{10... | collective-permute-start | bytes 331784 | tf_op jit(solution)/shard_map/ppermute | solution.py:400
  525.4 15.8 %collective-permute-start.33 = (bf16[96,576]{1,0:T(8,128)(2,1)S(1)}, bf16[96,576]{1,0:T(8,128)(2,1)S(1)}, u32[]{:S(2)}, u32[]{:S(2)}) collective-permute-start(bf16[96,576]{1,0:T(8,128)(2,1)S(1)} %get-tuple-element.180), channel_id=1, source_target_pairs={{0,8},{8,16},{16,24},{24,0},{1,9},{9,17},{17,25},{25,1},{2,10},{10... | collective-permute-start | bytes 331784 | tf_op jit(solution)/shard_map/ppermute | solution.py:400
  (86 other events, 1033.1 us)
Sparse Core Ops, SparseCore 0:
  9.9 26.6 all-gather.6
  39.1 34.6 all-gather.4
  75.6 38.7 all-gather.8
  116.2 38.8 all-gather.10
  227.3 84.0 reduce-scatter.4
  314.7 59.6 reduce-scatter.2
  413.8 142.2 all-reduce.3
